TPU v7x, 128 devices: a whole 4x4x4 slice. The times are simulated.
128 devices in a mesh: replica: 16 (over z, y), model: 8 (over x, core).
Axes of the slice: x: 4, y: 4, z: 4, core: 2. Of those that a mesh axis runs over, the one named last changes fastest.
Arguments:
- slope_up: float32 [16, 1024, 4096], P('replica', None, 'model'), may hold values from -4 to 4
- slope_down: float32 [16, 4096, 1024], P('replica', 'model'), may hold values from -4 to 4
- slope_query: float32 [16, 1024, 1024], P('replica', None, 'model'), may hold values from -4 to 4
- slope_key: float32 [16, 1024, 1024], P('replica', None, 'model'), may hold values from -4 to 4
- slope_value: float32 [16, 1024, 1024], P('replica', None, 'model'), may hold values from -4 to 4
- slope_mixed: float32 [16, 1024, 1024], P('replica', 'model'), may hold values from -4 to 4
- slope_norm: float32 [16, 1024], P('replica'), may hold values from -8 to 8
- slope_bias: float32 [16, 1024], P('replica'), may hold values from -8 to 8
- param_up: float32 [1024, 4096], P('replica', 'model'), may hold values from -0.25 to 0.25
- param_down: float32 [4096, 1024], P('model', 'replica'), may hold values from -0.125 to 0.125
- param_query: float32 [1024, 1024], P('replica', 'model'), may hold values from -0.25 to 0.25
- param_key: float32 [1024, 1024], P('replica', 'model'), may hold values from -0.25 to 0.25
- param_value: float32 [1024, 1024], P('replica', 'model'), may hold values from -0.25 to 0.25
- param_mixed: float32 [1024, 1024], P('model', 'replica'), may hold values from -0.25 to 0.25
- param_norm: float32 [1024], P('replica'), may hold values from 0.25 to 1.75
- param_bias: float32 [1024], P('replica'), may hold values from -3 to 3
- state_up: float32 [1024, 4096], P('replica', 'model'), may hold values from 0.0001953125 to 0.001953125
- state_down: float32 [4096, 1024], P('model', 'replica'), may hold values from 4.8828126e-05 to 0.00048828125
- state_query: float32 [1024, 1024], P('replica', 'model'), may hold values from 0.0001953125 to 0.001953125
- state_key: float32 [1024, 1024], P('replica', 'model'), may hold values from 0.0001953125 to 0.001953125
- state_value: float32 [1024, 1024], P('replica', 'model'), may hold values from 0.0001953125 to 0.001953125
- state_mixed: float32 [1024, 1024], P('model', 'replica'), may hold values from 0.0001953125 to 0.001953125
- state_norm: float32 [1024], P('replica'), may hold values from 0.05 to 0.8
- state_bias: float32 [1024], P('replica'), may hold values from 0.05 to 0.8
Outputs:
- half_up: bfloat16 [1024, 4096], P(None, 'model')
- half_down: bfloat16 [4096, 1024], P('model')
- half_query: bfloat16 [1024, 1024], P(None, 'model')
- half_key: bfloat16 [1024, 1024], P(None, 'model')
- half_value: bfloat16 [1024, 1024], P(None, 'model')
- half_mixed: bfloat16 [1024, 1024], P('model')
- half_norm: bfloat16 [1024], replicated
- half_bias: bfloat16 [1024], replicated
- next_up: float32 [1024, 4096], P('replica', 'model')
- next_down: float32 [4096, 1024], P('model', 'replica')
- next_query: float32 [1024, 1024], P('replica', 'model')
- next_key: float32 [1024, 1024], P('replica', 'model')
- next_value: float32 [1024, 1024], P('replica', 'model')
- next_mixed: float32 [1024, 1024], P('model', 'replica')
- next_norm: float32 [1024], P('replica')
- next_bias: float32 [1024], P('replica')
- state_new_up: float32 [1024, 4096], P('replica', 'model')
- state_new_down: float32 [4096, 1024], P('model', 'replica')
- state_new_query: float32 [1024, 1024], P('replica', 'model')
- state_new_key: float32 [1024, 1024], P('replica', 'model')
- state_new_value: float32 [1024, 1024], P('replica', 'model')
- state_new_mixed: float32 [1024, 1024], P('model', 'replica')
- state_new_norm: float32 [1024], P('replica')
- state_new_bias: float32 [1024], P('replica')
All inputs are finite; a program needn't handle non-finite values.
Results may differ from a plain program's by a relative error of at most 0.001.
Values may be sent and summed in bfloat16 or wider, within the bound.
A program may use at most 64 MiB of HBM per device.

v0:
```python
import jax
import jax.numpy as jnp
from jax import lax
from jax.sharding import PartitionSpec as P

learn_rate = 0.025
hold_rate = 0.7


def split_up(x, dim, length):
    before, after = (x.shape[:dim], x.shape[dim + 1 :])
    return jnp.moveaxis(x.reshape(*before, length, -1, *after), dim, 0)


def one_scatter(arrays, axis, dims):
    length = lax.axis_size(axis)
    parts = [split_up(a, dim, length) for a, dim in zip(arrays, dims)]
    lines = jnp.concatenate([b.reshape(length, -1) for b in parts], axis=1)
    rows = max(16, -(-lines.shape[1] // 1024) * 8)
    lines = jnp.pad(lines, ((0, 0), (0, rows * 128 - lines.shape[1]))).reshape(-1, 128)
    line, at, finished = (lax.psum_scatter(lines, axis, tiled=True).reshape(-1), 0, [])
    for b in parts:
        part = b[0]
        finished.append(line[at : at + part.size].reshape(part.shape))
        at += part.size
    return tuple(finished)


def from_everyone(x, axis):
    copies = jnp.broadcast_to(x, (lax.axis_size(axis), *x.shape))
    return lax.all_to_all(copies, axis, split_axis=0, concat_axis=0, tiled=True)


def taken_together(x, axis):
    return from_everyone(x, axis).sum(axis=0)


def together(arrays, axis):
    ends = [0]
    for a in arrays:
        ends.append(ends[-1] + a.size)
    subtotal = taken_together(jnp.concatenate([a.ravel() for a in arrays]), axis)
    return tuple((subtotal[b:e].reshape(a.shape) for a, b, e in zip(arrays, ends, ends[1:])))


def rows_first(arrays, axis, dims):
    turned = [jnp.moveaxis(a, dim, 0) for a, dim in zip(arrays, dims)]
    both = jnp.concatenate([t.reshape(len(t), -1) for t in turned], axis=1)
    whole, at, finished = (lax.all_gather(both, axis, axis=0, tiled=True), 0, [])
    for t, dim in zip(turned, dims):
        section = whole[:, at : at + t[0].size].reshape(-1, *t.shape[1:])
        finished.append(jnp.moveaxis(section, 0, dim))
        at += t[0].size
    return tuple(finished)


def local(
    slope_up,
    slope_down,
    slope_query,
    slope_key,
    slope_value,
    slope_mixed,
    slope_norm,
    slope_bias,
    param_up,
    param_down,
    param_query,
    param_key,
    param_value,
    param_mixed,
    param_norm,
    param_bias,
    state_up,
    state_down,
    state_query,
    state_key,
    state_value,
    state_mixed,
    state_norm,
    state_bias,
):
    mean_up, mean_down, mean_query, mean_key, mean_value, mean_mixed, mean_norm, mean_bias = (
        one_scatter(
            (
                slope_up[0],
                slope_down[0],
                slope_query[0],
                slope_key[0],
                slope_value[0],
                slope_mixed[0],
                slope_norm[0],
                slope_bias[0],
            ),
            "replica",
            (0, 1, 0, 0, 0, 1, 0, 0),
        )
    )
    mean_rate = lax.axis_size("replica") ** (-0.5)
    mean_up = mean_up * mean_rate
    mean_down = mean_down * mean_rate
    mean_query = mean_query * mean_rate
    mean_key = mean_key * mean_rate
    mean_value = mean_value * mean_rate
    mean_mixed = mean_mixed * mean_rate
    mean_norm = mean_norm * mean_rate
    mean_bias = mean_bias * mean_rate
    (
        own_up,
        own_down,
        own_query,
        own_key,
        own_value,
        own_mixed,
        slope_up_norm,
        slope_down_norm,
        slope_query_norm,
        slope_key_norm,
        slope_value_norm,
        slope_mixed_norm,
    ) = together(
        (
            jnp.sum(param_up * param_up, axis=1, keepdims=True),
            jnp.sum(param_down * param_down, axis=0, keepdims=True),
            jnp.sum(param_query * param_query, axis=1, keepdims=True),
            jnp.sum(param_key * param_key, axis=1, keepdims=True),
            jnp.sum(param_value * param_value, axis=1, keepdims=True),
            jnp.sum(param_mixed * param_mixed, axis=0, keepdims=True),
            jnp.sum(mean_up * mean_up, axis=1, keepdims=True),
            jnp.sum(mean_down * mean_down, axis=0, keepdims=True),
            jnp.sum(mean_query * mean_query, axis=1, keepdims=True),
            jnp.sum(mean_key * mean_key, axis=1, keepdims=True),
            jnp.sum(mean_value * mean_value, axis=1, keepdims=True),
            jnp.sum(mean_mixed * mean_mixed, axis=0, keepdims=True),
        ),
        "model",
    )
    mean_up = mean_up * (jnp.sqrt(own_up) * lax.rsqrt(slope_up_norm + 1e-06))
    mean_down = mean_down * (jnp.sqrt(own_down) * lax.rsqrt(slope_down_norm + 1e-06))
    mean_query = mean_query * (jnp.sqrt(own_query) * lax.rsqrt(slope_query_norm + 1e-06))
    mean_key = mean_key * (jnp.sqrt(own_key) * lax.rsqrt(slope_key_norm + 1e-06))
    mean_value = mean_value * (jnp.sqrt(own_value) * lax.rsqrt(slope_value_norm + 1e-06))
    mean_mixed = mean_mixed * (jnp.sqrt(own_mixed) * lax.rsqrt(slope_mixed_norm + 1e-06))
    state_new_up = hold_rate * state_up + (1.0 - hold_rate) * mean_up * mean_up
    next_up = param_up - learn_rate * mean_up * lax.rsqrt(state_new_up + 1e-06)
    state_new_down = hold_rate * state_down + (1.0 - hold_rate) * mean_down * mean_down
    next_down = param_down - learn_rate * mean_down * lax.rsqrt(state_new_down + 1e-06)
    state_new_query = hold_rate * state_query + (1.0 - hold_rate) * mean_query * mean_query
    next_query = param_query - learn_rate * mean_query * lax.rsqrt(state_new_query + 1e-06)
    state_new_key = hold_rate * state_key + (1.0 - hold_rate) * mean_key * mean_key
    next_key = param_key - learn_rate * mean_key * lax.rsqrt(state_new_key + 1e-06)
    state_new_value = hold_rate * state_value + (1.0 - hold_rate) * mean_value * mean_value
    next_value = param_value - learn_rate * mean_value * lax.rsqrt(state_new_value + 1e-06)
    state_new_mixed = hold_rate * state_mixed + (1.0 - hold_rate) * mean_mixed * mean_mixed
    next_mixed = param_mixed - learn_rate * mean_mixed * lax.rsqrt(state_new_mixed + 1e-06)
    state_new_norm = hold_rate * state_norm + (1.0 - hold_rate) * mean_norm * mean_norm
    next_norm = param_norm - learn_rate * mean_norm * lax.rsqrt(state_new_norm + 1e-06)
    state_new_bias = hold_rate * state_bias + (1.0 - hold_rate) * mean_bias * mean_bias
    next_bias = param_bias - learn_rate * mean_bias * lax.rsqrt(state_new_bias + 1e-06)
    half_up, half_down, half_query, half_key, half_value, half_mixed, half_norm, half_bias = (
        rows_first(
            (
                next_up.astype(jnp.bfloat16),
                next_down.astype(jnp.bfloat16),
                next_query.astype(jnp.bfloat16),
                next_key.astype(jnp.bfloat16),
                next_value.astype(jnp.bfloat16),
                next_mixed.astype(jnp.bfloat16),
                next_norm.astype(jnp.bfloat16),
                next_bias.astype(jnp.bfloat16),
            ),
            "replica",
            (0, 1, 0, 0, 0, 1, 0, 0),
        )
    )
    return (
        half_up,
        half_down,
        half_query,
        half_key,
        half_value,
        half_mixed,
        half_norm,
        half_bias,
        next_up,
        next_down,
        next_query,
        next_key,
        next_value,
        next_mixed,
        next_norm,
        next_bias,
        state_new_up,
        state_new_down,
        state_new_query,
        state_new_key,
        state_new_value,
        state_new_mixed,
        state_new_norm,
        state_new_bias,
    )


def solution(mesh):
    placed = (
        P("replica", None, "model"),
        P("replica", "model", None),
        P("replica", None, "model"),
        P("replica", None, "model"),
        P("replica", None, "model"),
        P("replica", "model", None),
        P("replica", None),
        P("replica", None),
        P("replica", "model"),
        P("model", "replica"),
        P("replica", "model"),
        P("replica", "model"),
        P("replica", "model"),
        P("model", "replica"),
        P("replica"),
        P("replica"),
        P("replica", "model"),
        P("model", "replica"),
        P("replica", "model"),
        P("replica", "model"),
        P("replica", "model"),
        P("model", "replica"),
        P("replica"),
        P("replica"),
    )
    return jax.shard_map(
        local,
        mesh=mesh,
        in_specs=placed,
        out_specs=(
            P(None, "model"),
            P("model", None),
            P(None, "model"),
            P(None, "model"),
            P(None, "model"),
            P("model", None),
            P(),
            P(),
            P("replica", "model"),
            P("model", "replica"),
            P("replica", "model"),
            P("replica", "model"),
            P("replica", "model"),
            P("model", "replica"),
            P("replica"),
            P("replica"),
            P("replica", "model"),
            P("model", "replica"),
            P("replica", "model"),
            P("replica", "model"),
            P("replica", "model"),
            P("model", "replica"),
            P("replica"),
            P("replica"),
        ),
        check_vma=False,
    )
```

profile of v0, /device:TPU:0, one launch (start us, length us, event | category | flops | bytes accessed | tf_op | source)
XLA Modules:
  0.0 255.0 jit_solution(3883371217189918573)
XLA Ops:
  7.2 1.8 reshape_reshape_squeeze.12
  9.0 1.4 constant_dynamic-update-slice_fusion.5
  10.4 1.9 copy.120
  12.4 2.7 %copy.121 = f32[16,512,64]{2,1,0:T(8,128)} copy(f32[16,512,64]{1,2,0:T(8,128)S(1)} %bitcast.21) | data formatting | bytes 4194304 | tf_op jit(solution)/shard_map/transpose | solution.py:12
  15.1 2.9 %reshape.143 = f32[16,32768]{1,0:T(8,128)S(1)} reshape(f32[16,512,64]{2,1,0:T(8,128)} %copy.121) | data formatting | bytes 4194304 | tf_op jit(solution)/shard_map/reshape | solution.py:18
  18.1 0.9 reshape_reshape_squeeze.13
  18.9 0.9 reshape_reshape_squeeze.14
  19.8 1.9 reshape_reshape_squeeze.15
  21.8 2.1 copy.122
  23.8 1.4 copy.123
  25.2 1.2 reshape.144
  28.4 1.4 constant_dynamic-update-slice_fusion.4
  29.8 1.9 constant_dynamic-update-slice_fusion.3
  31.7 1.9 constant_dynamic-update-slice_fusion.2
  34.4 0.8 constant_dynamic-update-slice_fusion
  35.2 1.3 dynamic-update-slice.6
  36.5 1.4 dynamic-update-slice.7
  37.9 5.9 %pad.4 = f32[16,99328]{1,0:T(8,128)} pad(f32[16,98432]{1,0:T(8,128)} %dynamic-update-slice.7, f32[]{:T(128)} %constant.8.clone.1), padding=0_0x0_896 | pad | bytes 12656644 | tf_op jit(solution)/shard_map/jit(_pad)/pad | solution.py:20
  43.7 5.0 %reshape.145 = f32[12416,128]{1,0:T(8,128)} reshape(f32[16,99328]{1,0:T(8,128)} %pad.4) | data formatting | bytes 12713984 | tf_op jit(solution)/shard_map/reshape | solution.py:20
  51.3 123.2 %all-reduce.4.cloned.1.call-done = f32[12416,128]{1,0:T(8,128)} async-done(((f32[12416,128]{1,0:T(8,128)}), f32[12416,128]{1,0:T(8,128)}) %all-reduce.4.cloned.1.call-update) | async-done | bytes 6357008
  174.5 1.1 multiply_reduce_fusion.1
  176.0 1.0 multiply_reduce_fusion.5
  177.8 4.3 %all-to-all-start = ((f32[8,1,768]{2,1,0:T(1,128)}), f32[8,1,768]{2,1,0:T(1,128)S(1)}, u32[]{:S(2)}, u32[]{:S(2)}) async-start(f32[8,1,768]{2,1,0:T(1,128)} %broadcast_in_dim.3), calls=%async_computation | async-start | bytes 49152 | tf_op jit(solution)/shard_map/all_to_all | solution.py:31
  182.1 1.0 dynamic-slice_bitcast_fusion
  184.3 3.2 %all-to-all-done = f32[8,1,768]{2,1,0:T(1,128)S(1)} async-done(((f32[8,1,768]{2,1,0:T(1,128)}), f32[8,1,768]{2,1,0:T(1,128)S(1)}, u32[]{:S(2)}, u32[]{:S(2)}) %all-to-all-start) | async-done | bytes 24608 | tf_op jit(solution)/shard_map/all_to_all | solution.py:31
  190.0 1.6 fusion.7
  192.4 46.9 %all-gather.2.cloned.1.call-done = bf16[1024,1538]{1,0:T(8,128)(2,1)} async-done(((bf16[64,1538]{1,0:T(8,128)(2,1)}), bf16[1024,1538]{1,0:T(8,128)(2,1)}) %all-gather.2.cloned.1.call-update) | async-done | bytes 3149840 | tf_op jit(solution)/shard_map/all_gather | solution.py:49
  239.3 2.7 %slice_bitcast_fusion = (bf16[512,1024]{0,1:T(8,128)(2,1)S(1)}, bf16[1024,512]{1,0:T(8,128)(2,1)}) fusion(bf16[1024,1538]{1,0:T(8,128)(2,1)} %all-gather.2.cloned.1.call-done), kind=kLoop, calls=%fused_computation | loop fusion | bytes 4194304 | tf_op jit(solution)/shard_map/transpose | solution.py:52
  241.9 1.3 copy.129
  243.2 2.1 slice_bitcast_fusion.1
  245.3 0.8 copy.130
  246.2 1.9 slice_reduce_fusion
  (82 shorter events, 10.1 us)
Async XLA Ops:
  7.2 167.3 %all-reduce.4.cloned.1.call-start = ((), (), s32[]{:S(2)}) async-start(), calls=%async_computation.2 | async-start | bytes 12713984
  12.4 5.7 %copy-start.4 = (f32[1,1024,128]{2,1,0:T(8,128)S(1)}, f32[1,1024,128]{2,1,0:T(8,128)}, u32[]{:S(2)}) copy-start(f32[1,1024,128]{2,1,0:T(8,128)} %param.26) | copy-start | bytes 1572868
  12.4 6.6 %copy-start.5 = (f32[1,1024,128]{2,1,0:T(8,128)S(1)}, f32[1,1024,128]{2,1,0:T(8,128)}, u32[]{:S(2)}) copy-start(f32[1,1024,128]{2,1,0:T(8,128)} %param.27) | copy-start | bytes 1572868
  15.1 11.8 %copy-start.16 = (f32[1,1024]{1,0:T(1,128)S(1)}, f32[1,1024]{1,0:T(1,128)}, u32[]{:S(2)}) copy-start(f32[1,1024]{1,0:T(1,128)} %param.30) | copy-start | bytes 12292
  15.1 12.5 %copy-start.17 = (f32[1,1024]{1,0:T(1,128)S(1)}, f32[1,1024]{1,0:T(1,128)}, u32[]{:S(2)}) copy-start(f32[1,1024]{1,0:T(1,128)} %param.31) | copy-start | bytes 12292
  26.4 7.2 %copy-start.1 = (f32[16,8192]{1,0:T(8,128)S(1)}, f32[16,8192]{1,0:T(8,128)}, u32[]{:S(2)}) copy-start(f32[16,8192]{1,0:T(8,128)} %reshape_reshape_squeeze.15) | copy-start | bytes 1572868
  26.4 8.0 %copy-start = (f32[16,8192]{1,0:T(8,128)S(1)}, f32[16,8192]{1,0:T(8,128)}, u32[]{:S(2)}) copy-start(f32[16,8192]{1,0:T(8,128)} %reshape.144) | copy-start | bytes 1572868
  48.8 0.7 copy-start.22
  48.8 1.9 copy-start.8
  48.8 2.0 copy-start.11
  48.8 2.1 copy-start.9
  48.8 2.1 copy-start.10
  48.8 2.2 copy-start.2
  48.8 2.3 copy-start.3
  48.8 134.4 %copy-start.18 = (f32[64]{0:T(128)S(1)}, f32[64]{0:T(128)}, u32[]{:S(2)}) copy-start(f32[64]{0:T(128)} %param.39) | copy-start | bytes 772
  48.8 134.4 %copy-start.19 = (f32[64]{0:T(128)S(1)}, f32[64]{0:T(128)}, u32[]{:S(2)}) copy-start(f32[64]{0:T(128)} %param.47) | copy-start | bytes 772
  48.8 134.4 %copy-start.20 = (f32[64]{0:T(128)S(1)}, f32[64]{0:T(128)}, u32[]{:S(2)}) copy-start(f32[64]{0:T(128)} %param.38) | copy-start | bytes 772
  48.9 134.3 %copy-start.21 = (f32[64]{0:T(128)S(1)}, f32[64]{0:T(128)}, u32[]{:S(2)}) copy-start(f32[64]{0:T(128)} %param.46) | copy-start | bytes 772
  48.9 138.8 %copy-start.6 = (f32[64,512]{1,0:T(8,128)S(1)}, f32[64,512]{1,0:T(8,128)}, u32[]{:S(2)}) copy-start(f32[64,512]{1,0:T(8,128)} %param.40) | copy-start | bytes 393220
  48.9 139.6 %copy-start.7 = (f32[512,64]{0,1:T(8,128)S(1)}, f32[512,64]{0,1:T(8,128)}, u32[]{:S(2)}) copy-start(f32[512,64]{0,1:T(8,128)} %param.41) | copy-start | bytes 393220
  48.9 140.4 %copy-start.15 = (f32[128,64]{0,1:T(8,128)S(1)}, f32[128,64]{0,1:T(8,128)}, u32[]{:S(2)}) copy-start(f32[128,64]{0,1:T(8,128)} %param.45) | copy-start | bytes 98308
  48.9 141.1 %copy-start.12 = (f32[64,128]{1,0:T(8,128)S(1)}, f32[64,128]{1,0:T(8,128)}, u32[]{:S(2)}) copy-start(f32[64,128]{1,0:T(8,128)} %param.44) | copy-start | bytes 98308
  48.9 141.0 %copy-start.13 = (f32[64,128]{1,0:T(8,128)S(1)}, f32[64,128]{1,0:T(8,128)}, u32[]{:S(2)}) copy-start(f32[64,128]{1,0:T(8,128)} %param.43) | copy-start | bytes 98308
  48.9 141.0 %copy-start.14 = (f32[64,128]{1,0:T(8,128)S(1)}, f32[64,128]{1,0:T(8,128)}, u32[]{:S(2)}) copy-start(f32[64,128]{1,0:T(8,128)} %param.42) | copy-start | bytes 98308
  177.8 9.7 %all-to-all-start = ((f32[8,1,768]{2,1,0:T(1,128)}), f32[8,1,768]{2,1,0:T(1,128)S(1)}, u32[]{:S(2)}, u32[]{:S(2)}) async-start(f32[8,1,768]{2,1,0:T(1,128)} %broadcast_in_dim.3), calls=%async_computation | async-start | bytes 49152 | tf_op jit(solution)/shard_map/all_to_all | solution.py:31
  182.1 57.2 %all-gather.2.cloned.1.call-start = ((), (), s32[]{:S(2)}) async-start(), calls=%async_computation.1 | async-start | bytes 3620864 | tf_op jit(solution)/shard_map/all_gather | solution.py:49
Sparse Core Ops, SparseCore 0:
  49.1 125.3 all-reduce.3
  192.5 46.6 all-gather.1
where the time goes:
time: 256 us; the launch traced here: 255 us
  waiting for transfers between devices  173 us (68%)
  local copies, waits for them, and re-layouts  53.3 us (21%)
  between operations  15.1 us (6%)
  other arithmetic  8.86 us (3%)
  starting transfers between devices  4.33 us (2%)
    unnamed x3, waiting for transfers between devices  123 us
    all_gather x1, waiting for transfers between devices, rows_first(): lax.all_gather(both, axis, axis=0, tiled=True)  46.9 us
    unnamed x59, local copies, waits for them, and re-layouts  17.4 us
    pad x1, local copies, waits for them, and re-layouts, one_scatter(): jnp.pad(lines, ((0, 0), (0, rows * 128 - lines.shape[1]))).reshape(-1, 128)  5.86 us
    another operation x4, local copies, waits for them, and re-layouts, one_scatter(): lines = jnp.concatenate([b.reshape(length, -1) for b in parts], axis=1)  5.46 us
  transfers between devices with their start and end apart: 3, of which 3 were waited for; matrix products, arithmetic and copies ran while one was open for 1% of the time, Pallas kernels for 0%

commit v1 on v0

v1 whole, which is shorter than its diff:
```python
import functools

import jax
import jax.numpy as jnp
from jax import lax
from jax.experimental import pallas as pl
from jax.experimental.pallas import tpu as pltpu
from jax.sharding import PartitionSpec as P

learn_rate = 0.025
hold_rate = 0.7
MESH = pl.DeviceIdType.MESH
SIDE = 4
PEERS = 8

UP, QUERY, KEY, DOWN, MIXED, VALUE, SMALL, ROWS = 0, 256, 320, 384, 640, 704, 768, 784

CHUNKS = (
    ("y", 0, 64, 64),
    ("z", 384, 64, 64),
    ("y", 128, 64, 64),
    ("z", 512, 64, 64),
    ("y", 256, 64, 64),
    ("z", 640, 80, 64),
)
PER = 12
GATHERS = (
    ("y", 0, 128, 128),
    ("z", 384, 128, 128),
    ("y", 256, 64, 64),
    ("z", 640, 80, 64),
)
PER_GATHER = 8

GRAIN = 2.0**15
GRAIN2 = 2.0**13


def to_wire(x, grain):
    v = x * grain
    v2 = v * v
    v4 = v2 * v2
    return (v4 * v2 * v).astype(jnp.bfloat16)


def from_wire(c, grain):
    c = c.astype(jnp.float32)
    root = jnp.exp(jnp.log(jnp.abs(c)) * (1.0 / 7.0)) * (1.0 / grain)
    return jnp.where(c < 0.0, -root, root)


def low_lanes(shape):
    return lax.broadcasted_iota(jnp.int32, shape, len(shape) - 1) < 64


def turn(x):
    return pltpu.roll(x, 64, 1)


def beside(x):
    half = x.shape[0] // 2
    return jnp.concatenate([x[:half], x[half:]], axis=1)


def exchange_kernel(
    up,
    down,
    query,
    key,
    value,
    mixed,
    norm,
    bias,
    param_up,
    param_down,
    param_query,
    param_key,
    param_value,
    param_mixed,
    param_small,
    state_up,
    state_down,
    state_query,
    state_key,
    state_value,
    state_mixed,
    state_small,
    gathered,
    scaled,
    mine,
    raw_down,
    raw_mixed,
    raw_norm,
    raw_bias,
    send_op,
    send_dir,
    send_fwd,
    recv_op,
    recv_dir,
    recv_fwd,
    first_sum,
    send_op2,
    send_dir2,
    send_fwd2,
    recv_op2,
    recv_dir2,
    recv_fwd2,
    mean,
    squares,
    load_sem,
    send_sem,
    recv_sem,
    gsend_sem,
    grecv_sem,
    nsend_sem,
    nrecv_sem,
):
    replica = lax.axis_index("replica")
    model = lax.axis_index("model")
    z, y = replica // SIDE, replica % SIDE

    def place(axis, step):
        if axis == "y":
            return (z * SIDE + (y + step) % SIDE, model)
        return (((z + step) % SIDE) * SIDE + y, model)

    position = {"y": y, "z": z}
    other = {"y": "z", "z": "y"}

    loads = {}

    def load(name, pairs):
        loads[name] = []
        for src, dst in pairs:
            copy = pltpu.make_async_copy(src, dst, load_sem.at[load.count])
            load.count += 1
            copy.start()
            loads[name].append(copy)

    load.count = 0

    def loaded(name):
        for copy in loads[name]:
            copy.wait()

    load(
        "up",
        [
            (up.at[:, :, :, pl.ds(128 * c, 128)], mine.at[:, :, pl.ds(UP + 64 * c, 64), :])
            for c in range(4)
        ],
    )
    load("down", [(down, raw_down)])
    load(
        "rest",
        [
            (query, mine.at[:, :, pl.ds(QUERY, 64), :]),
            (key, mine.at[:, :, pl.ds(KEY, 64), :]),
            (value, mine.at[:, :, pl.ds(VALUE, 64), :]),
            (mixed, raw_mixed),
            (norm, raw_norm),
            (bias, raw_bias),
        ],
    )

    barrier = pltpu.get_barrier_semaphore()
    for axis in ("y", "z"):
        for step in (1, SIDE - 1):
            pl.semaphore_signal(barrier, 1, device_id=place(axis, step), device_id_type=MESH)
    for step in range(1, PEERS):
        pl.semaphore_signal(
            barrier, 1, device_id=(replica, (model + step) % PEERS), device_id_type=MESH
        )

    def pack_columns(raw, row, half):
        low = low_lanes((64, 128))
        for pair in range(8):
            lanes = pl.ds(128 * pair, 128)
            zz, yy = (2 * pair) // SIDE, (2 * pair) % SIDE

            def body(i, _):
                at = pl.multiple_of(i * 64, 64)
                a = raw[pl.ds(at, 64), lanes]
                b = raw[pl.ds(half + at, 64), lanes]
                mine[zz, yy, pl.ds(row + at, 64), :] = jnp.where(low, a, turn(b))
                mine[zz, yy + 1, pl.ds(row + at, 64), :] = jnp.where(low, turn(a), b)
                return 0

            lax.fori_loop(0, half // 64, body, 0)

    def pack_small():
        low = low_lanes((1, 128))
        for pair in range(8):
            lanes = pl.ds(128 * pair, 128)
            zz, yy = (2 * pair) // SIDE, (2 * pair) % SIDE
            a = raw_norm[:, lanes] * 0.5
            b = raw_bias[:, lanes] * 0.5
            mine[zz, yy, pl.ds(SMALL, 16), :] = jnp.broadcast_to(
                jnp.where(low, a, turn(b)), (16, 128)
            )
            mine[zz, yy + 1, pl.ds(SMALL, 16), :] = jnp.broadcast_to(
                jnp.where(low, turn(a), b), (16, 128)
            )

    def halves(chunk):
        _, row, first, second = CHUNKS[chunk]
        return pl.ds(row, first), pl.ds(row + first, second)

    def share(axis, at, b):
        if axis == "y":
            return mine.at[b, at]
        return mine.at[at, b]

    def remote(chunk, number, src, dst, axis, step):
        k = chunk * PER + number
        return pltpu.make_async_remote_copy(
            src_ref=src,
            dst_ref=dst,
            send_sem=send_sem.at[k],
            recv_sem=recv_sem.at[k],
            device_id=place(axis, step),
            device_id_type=MESH,
        )

    def copies(chunk, number):
        axis = CHUNKS[chunk][0]
        a, b = halves(chunk)
        if number >= 6:
            axis = other[axis]
            bufs = ((send_op2, recv_op2), (send_dir2, recv_dir2), (send_fwd2, recv_fwd2))
            a, b = (a, slice(None)), (b, slice(None))
        else:
            bufs = ((send_op, recv_op), (send_dir, recv_dir), (send_fwd, recv_fwd))
            a, b = (slice(None), a, slice(None)), (slice(None), b, slice(None))
        kind, half = divmod(number % 6, 2)
        src, dst = bufs[kind]
        rows = b if half else a
        step = (SIDE - 1, 1)[half] if kind != 1 else (1, SIDE - 1)[half]
        return remote(chunk, number, src.at[rows], dst.at[rows], axis, step)

    def reduce_send(chunk, first=False):
        axis = CHUNKS[chunk][0]
        p = position[axis]
        a, b = halves(chunk)
        far, right, left = (p + 2) % SIDE, (p + 1) % SIDE, (p + SIDE - 1) % SIDE

        def op(i, _):
            send_op[i, a, :] = to_wire(share(axis, far, i)[a, :], GRAIN)
            send_op[i, b, :] = to_wire(share(axis, far, i)[b, :], GRAIN)
            return 0

        lax.fori_loop(0, SIDE, op, 0)
        if first:
            pl.semaphore_wait(barrier, 4 + PEERS - 1)
        copies(chunk, 0).start()
        copies(chunk, 1).start()

        def direct(i, _):
            send_dir[i, a, :] = to_wire(share(axis, right, i)[a, :], GRAIN)
            send_dir[i, b, :] = to_wire(share(axis, left, i)[b, :], GRAIN)
            return 0

        lax.fori_loop(0, SIDE, direct, 0)
        copies(chunk, 2).start()
        copies(chunk, 3).start()

    def reduce_forward(chunk):
        axis = CHUNKS[chunk][0]
        p = position[axis]
        a, b = halves(chunk)
        right, left = (p + 1) % SIDE, (p + SIDE - 1) % SIDE
        for number, rows, at in ((0, a, left), (1, b, right)):
            copies(chunk, number).wait_recv()

            def body(i, _):
                part = from_wire(recv_op[i, rows, :], GRAIN) + share(axis, at, i)[rows, :]
                send_fwd[i, rows, :] = to_wire(part, GRAIN)
                return 0

            lax.fori_loop(0, SIDE, body, 0)
            copies(chunk, 4 + number).start()

    def reduce_finish(chunk):
        axis = CHUNKS[chunk][0]
        p = position[axis]
        for number in (2, 3, 4, 5):
            copies(chunk, number).wait_recv()

        def body(i, _):
            for rows in halves(chunk):
                first_sum[i, rows, :] = (
                    share(axis, p, i)[rows, :]
                    + from_wire(recv_dir[i, rows, :], GRAIN)
                    + from_wire(recv_fwd[i, rows, :], GRAIN)
                )
            return 0

        lax.fori_loop(0, SIDE, body, 0)

    def second_send(chunk):
        p = position[other[CHUNKS[chunk][0]]]
        a, b = halves(chunk)
        far, right, left = (p + 2) % SIDE, (p + 1) % SIDE, (p + SIDE - 1) % SIDE
        send_op2[a, :] = to_wire(first_sum[far, a, :], GRAIN2)
        copies(chunk, 6).start()
        send_op2[b, :] = to_wire(first_sum[far, b, :], GRAIN2)
        copies(chunk, 7).start()
        send_dir2[a, :] = to_wire(first_sum[right, a, :], GRAIN2)
        copies(chunk, 8).start()
        send_dir2[b, :] = to_wire(first_sum[left, b, :], GRAIN2)
        copies(chunk, 9).start()

    def second_forward(chunk):
        p = position[other[CHUNKS[chunk][0]]]
        a, b = halves(chunk)
        right, left = (p + 1) % SIDE, (p + SIDE - 1) % SIDE
        for number, rows, at in ((6, a, left), (7, b, right)):
            copies(chunk, number).wait_recv()
            part = from_wire(recv_op2[rows, :], GRAIN2) + first_sum[at, rows, :]
            send_fwd2[rows, :] = to_wire(part, GRAIN2)
            copies(chunk, 4 + number).start()

    def second_finish(chunk):
        p = position[other[CHUNKS[chunk][0]]]
        for number in (8, 9, 10, 11):
            copies(chunk, number).wait_recv()
        for rows in halves(chunk):
            mean[rows, :] = (
                first_sum[p, rows, :]
                + from_wire(recv_dir2[rows, :], GRAIN2)
                + from_wire(recv_fwd2[rows, :], GRAIN2)
            ) * (SIDE * SIDE) ** (-0.5)

    def row_squares(row, width, param):
        got = jnp.zeros((64, 128), jnp.float32)
        own = jnp.zeros((64, 128), jnp.float32)
        for c in range(width):
            m = mean[pl.ds(row + 64 * c, 64), :]
            w = param[:, pl.ds(128 * c, 128)]
            got, own = got + m * m, own + w * w
        both = jnp.concatenate([got, own], axis=0)
        return jnp.sum(both, axis=1, keepdims=True)

    def column_squares(row, length, param):
        m = mean[pl.ds(row, length), :]
        w = beside(param[...])
        got = jnp.sum(m * m, axis=0, keepdims=True)
        own = jnp.sum(w * w, axis=0, keepdims=True)
        got, own = got + turn(got), own + turn(own)
        return jnp.where(low_lanes((1, 128)), got, own)

    def norm_copy(turn_number, step):
        k = turn_number * (PEERS - 1) + step - 1
        return pltpu.make_async_remote_copy(
            src_ref=squares.at[turn_number, 0],
            dst_ref=squares.at[turn_number, step],
            send_sem=nsend_sem.at[k],
            recv_sem=nrecv_sem.at[k],
            device_id=(replica, (model + step) % PEERS),
            device_id_type=MESH,
        )

    def norm_send(turn_number, by_rows, by_columns):
        lane = lax.broadcasted_iota(jnp.int32, (128, 128), 1)
        block = jnp.zeros((128, 128), jnp.float32)
        for k, column in enumerate(by_rows):
            block = jnp.where(lane == k, column, block)
        tile = block.T[0:8]
        sub = lax.broadcasted_iota(jnp.int32, (8, 128), 0)
        for k, line in enumerate(by_columns):
            tile = jnp.where(sub == len(by_rows) + k, line, tile)
        squares[turn_number, 0] = tile
        for step in range(1, PEERS):
            norm_copy(turn_number, step).start()

    def norm_ratios(turn_number):
        for step in range(1, PEERS):
            norm_copy(turn_number, step).wait_recv()
        total = squares[turn_number, 0]
        for step in range(1, PEERS):
            total = total + squares[turn_number, step]
        low = low_lanes((8, 128))
        back = turn(total)
        got, own = jnp.where(low, total, back), jnp.where(low, back, total)
        ratio = jnp.sqrt(own) * lax.rsqrt(got + 1e-06)
        return ratio, jnp.concatenate([ratio] * 16, axis=0).T

    def updated(rows, m, param, state):
        scaled[rows, :] = m
        state_new = hold_rate * state + (1.0 - hold_rate) * m * m
        new = param - learn_rate * m * lax.rsqrt(state_new + 1e-06)
        gathered[z, y, rows, :] = new.astype(jnp.bfloat16)

    def row_update(row, width, ratio, param, state):
        for c in range(width):
            rows, lanes = pl.ds(row + 64 * c, 64), pl.ds(128 * c, 128)
            updated(rows, mean[rows, :] * ratio, param[:, lanes], state[:, lanes])

    def column_update(row, length, ratio, param, state):
        rows = pl.ds(row, length)
        updated(rows, mean[rows, :] * ratio, beside(param[...]), beside(state[...]))

    def gather_copies(chunk, number):
        name, row, first, second = GATHERS[chunk]
        k = chunk * PER_GATHER + number
        a, b = pl.ds(row, first), pl.ds(row + first, second)
        whole = pl.ds(row, first + second)
        stage, number = divmod(number, 4)
        axis = other[name] if stage == 0 else name
        rows = (whole, whole, b, a)[number]
        step = (1, SIDE - 1, 1, SIDE - 1)[number]
        shift = (0, 0, SIDE - 1, 1)[number]
        p = (position[axis] + shift) % SIDE
        if stage == 0:
            ref = gathered.at[p, y, rows] if axis == "z" else gathered.at[z, p, rows]
        else:
            ref = gathered.at[p, :, rows] if axis == "z" else gathered.at[:, p, rows]
        return pltpu.make_async_remote_copy(
            src_ref=ref,
            dst_ref=ref,
            send_sem=gsend_sem.at[k],
            recv_sem=grecv_sem.at[k],
            device_id=place(axis, step),
            device_id_type=MESH,
        )

    def gather_send(chunk, stage):
        if stage == 1:
            gather_copies(chunk, 2).wait_recv()
            gather_copies(chunk, 3).wait_recv()
        gather_copies(chunk, 4 * stage).start()
        gather_copies(chunk, 4 * stage + 1).start()

    def gather_forward(chunk, stage):
        gather_copies(chunk, 4 * stage).wait_recv()
        gather_copies(chunk, 4 * stage + 2).start()
        gather_copies(chunk, 4 * stage + 1).wait_recv()
        gather_copies(chunk, 4 * stage + 3).start()

    def gather_finish(chunk):
        gather_copies(chunk, 6).wait_recv()
        gather_copies(chunk, 7).wait_recv()

    loaded("up")
    reduce_send(0, first=True)
    loaded("down")
    pack_columns(raw_down, DOWN, 256)
    reduce_send(1)
    reduce_send(2)
    reduce_send(3)
    loaded("rest")
    pack_columns(raw_mixed, MIXED, 64)
    pack_small()
    reduce_forward(0)
    reduce_forward(1)
    reduce_send(4)
    reduce_send(5)
    for chunk in (0, 1):
        reduce_finish(chunk)
        second_send(chunk)
    reduce_forward(2)
    reduce_forward(3)
    second_forward(0)
    second_forward(1)
    for chunk in (2, 3):
        reduce_finish(chunk)
        second_send(chunk)
    reduce_forward(4)
    reduce_forward(5)
    second_finish(0)
    second_finish(1)
    second_forward(2)
    second_forward(3)
    for chunk in (4, 5):
        reduce_finish(chunk)
        second_send(chunk)
    second_finish(2)
    second_finish(3)
    norm_send(
        0, (row_squares(UP, 4, param_up),), (column_squares(DOWN, 256, param_down),)
    )
    second_forward(4)
    second_forward(5)
    across, down_rows = norm_ratios(0)
    row_update(UP, 4, down_rows[0:64, 0:1], param_up, state_up)
    gather_send(0, 0)
    column_update(DOWN, 256, across[1:2], param_down, state_down)
    gather_send(1, 0)
    second_finish(4)
    second_finish(5)
    norm_send(
        1,
        (
            row_squares(QUERY, 1, param_query),
            row_squares(KEY, 1, param_key),
            row_squares(VALUE, 1, param_value),
        ),
        (column_squares(MIXED, 64, param_mixed),),
    )
    gather_forward(0, 0)
    gather_forward(1, 0)
    across, down_rows = norm_ratios(1)
    row_update(QUERY, 1, down_rows[0:64, 0:1], param_query, state_query)
    row_update(KEY, 1, down_rows[0:64, 1:2], param_key, state_key)
    gather_send(2, 0)
    row_update(VALUE, 1, down_rows[0:64, 2:3], param_value, state_value)
    column_update(MIXED, 64, across[3:4], param_mixed, state_mixed)
    small = pl.ds(SMALL, 16)
    updated(
        small,
        mean[small, :] * 2.0,
        jnp.broadcast_to(param_small[...], (16, 128)),
        jnp.broadcast_to(state_small[...], (16, 128)),
    )
    gather_send(3, 0)
    gather_send(0, 1)
    gather_send(1, 1)
    gather_forward(2, 0)
    gather_forward(3, 0)
    gather_send(2, 1)
    gather_send(3, 1)
    gather_forward(0, 1)
    gather_forward(1, 1)
    gather_forward(2, 1)
    gather_forward(3, 1)
    for chunk in range(len(GATHERS)):
        gather_finish(chunk)

    for chunk in range(len(CHUNKS)):
        for number in range(PER):
            copies(chunk, number).wait_send()
    for chunk in range(len(GATHERS)):
        for number in range(PER_GATHER):
            gather_copies(chunk, number).wait_send()
    for turn_number in range(2):
        for step in range(1, PEERS):
            norm_copy(turn_number, step).wait_send()


def output_kernel(
    gathered,
    scaled,
    param_up,
    param_down,
    param_query,
    param_key,
    param_value,
    param_mixed,
    param_small,
    state_up,
    state_down,
    state_query,
    state_key,
    state_value,
    state_mixed,
    state_small,
    half_up,
    half_down,
    half_query,
    half_key,
    half_value,
    half_mixed,
    half_small,
    next_up,
    next_down,
    next_query,
    next_key,
    next_value,
    next_mixed,
    next_small,
    new_up,
    new_down,
    new_query,
    new_key,
    new_value,
    new_mixed,
    new_small,
):
    def stepped(m, param, state):
        state_new = hold_rate * state + (1.0 - hold_rate) * m * m
        return param - learn_rate * m * lax.rsqrt(state_new + 1e-06), state_new

    def by_rows(row, width, param, state, following, new):
        for c in range(width):
            lanes = pl.ds(128 * c, 128)
            m = scaled[pl.ds(row + 64 * c, 64), :]
            following[:, lanes], new[:, lanes] = stepped(m, param[:, lanes], state[:, lanes])

    def by_columns(row, length, param, state, following, new):
        for part in range(2):
            rows = pl.ds(part * length, length)
            m = scaled[pl.ds(row, length), :]
            if part:
                m = turn(m)
            following[rows, :], new[rows, :] = stepped(m[:, 0:64], param[rows, :], state[rows, :])

    by_rows(UP, 4, param_up, state_up, next_up, new_up)
    by_rows(QUERY, 1, param_query, state_query, next_query, new_query)
    by_rows(KEY, 1, param_key, state_key, next_key, new_key)
    by_rows(VALUE, 1, param_value, state_value, next_value, new_value)
    by_columns(DOWN, 256, param_down, state_down, next_down, new_down)
    by_columns(MIXED, 64, param_mixed, state_mixed, next_mixed, new_mixed)
    next_small[...], new_small[...] = stepped(
        scaled[pl.ds(SMALL, 1), :], param_small[...], state_small[...]
    )

    def rows_of(i, _):
        at = pl.multiple_of(i * 64, 64)
        rows = pl.ds(at, 64)
        for c in range(4):
            half_up[rows, pl.ds(128 * c, 128)] = gathered[i, pl.ds(UP + 64 * c, 64), :]
        half_query[rows, :] = gathered[i, pl.ds(QUERY, 64), :]
        half_key[rows, :] = gathered[i, pl.ds(KEY, 64), :]
        half_value[rows, :] = gathered[i, pl.ds(VALUE, 64), :]
        return 0

    lax.fori_loop(0, SIDE * SIDE, rows_of, 0)

    low = low_lanes((64, 128))
    for out, row, length in ((half_down, DOWN, 256), (half_mixed, MIXED, 64)):
        for pair in range(8):
            lanes = pl.ds(128 * pair, 128)

            def body(i, _):
                at = pl.multiple_of(i * 64, 64)
                a = gathered[2 * pair, pl.ds(row + at, 64), :].astype(jnp.float32)
                b = gathered[2 * pair + 1, pl.ds(row + at, 64), :].astype(jnp.float32)
                out[pl.ds(at, 64), lanes] = jnp.where(low, a, turn(b)).astype(jnp.bfloat16)
                out[pl.ds(length + at, 64), lanes] = jnp.where(low, turn(a), b).astype(
                    jnp.bfloat16
                )
                return 0

            lax.fori_loop(0, length // 64, body, 0)
    low = low_lanes((1, 128))
    for pair in range(8):
        lanes = pl.ds(128 * pair, 128)
        a = gathered[2 * pair, pl.ds(SMALL, 16), :].astype(jnp.float32)[0:1]
        b = gathered[2 * pair + 1, pl.ds(SMALL, 16), :].astype(jnp.float32)[0:1]
        half_small[0:1, lanes] = jnp.where(low, a, turn(b)).astype(jnp.bfloat16)
        half_small[1:2, lanes] = jnp.where(low, turn(a), b).astype(jnp.bfloat16)


def local(*arrays):
    slopes, params, states = arrays[:8], arrays[8:16], arrays[16:]
    up, down, query, key, value, mixed, norm, bias = slopes
    small = [jnp.concatenate([a[6], a[7]])[None] for a in (params, states)]
    params, states = (*params[:6], small[0]), (*states[:6], small[1])
    vmem = pl.BlockSpec(memory_space=pltpu.VMEM)
    anywhere = pl.BlockSpec(memory_space=pl.ANY)
    f32, bf16 = jnp.float32, jnp.bfloat16
    wire = pltpu.VMEM((SIDE, ROWS, 128), bf16)
    wire2 = pltpu.VMEM((ROWS, 128), bf16)
    dma = pltpu.SemaphoreType.DMA
    gathered, scaled = pl.pallas_call(
        exchange_kernel,
        out_shape=(
            jax.ShapeDtypeStruct((SIDE, SIDE, ROWS, 128), bf16),
            jax.ShapeDtypeStruct((ROWS, 128), f32),
        ),
        in_specs=[anywhere] * 8 + [vmem] * 14,
        out_specs=(vmem, vmem),
        scratch_shapes=[
            pltpu.VMEM((SIDE, SIDE, ROWS, 128), f32),
            pltpu.VMEM((512, 1024), f32),
            pltpu.VMEM((128, 1024), f32),
            pltpu.VMEM((1, 1024), f32),
            pltpu.VMEM((1, 1024), f32),
            wire,
            wire,
            wire,
            wire,
            wire,
            wire,
            pltpu.VMEM((SIDE, ROWS, 128), f32),
            wire2,
            wire2,
            wire2,
            wire2,
            wire2,
            wire2,
            pltpu.VMEM((ROWS, 128), f32),
            pltpu.VMEM((2, PEERS, 8, 128), f32),
            dma((11,)),
            dma((len(CHUNKS) * PER,)),
            dma((len(CHUNKS) * PER,)),
            dma((len(GATHERS) * PER_GATHER,)),
            dma((len(GATHERS) * PER_GATHER,)),
            dma((2 * (PEERS - 1),)),
            dma((2 * (PEERS - 1),)),
        ],
        compiler_params=pltpu.CompilerParams(
            collective_id=0, has_side_effects=True, vmem_limit_bytes=60 * 2**20
        ),
        name="exchange",
    )(
        up.reshape(SIDE, SIDE, 64, 512),
        down[0],
        query.reshape(SIDE, SIDE, 64, 128),
        key.reshape(SIDE, SIDE, 64, 128),
        value.reshape(SIDE, SIDE, 64, 128),
        mixed[0],
        norm,
        bias,
        *params,
        *states,
    )
    shapes = [jax.ShapeDtypeStruct(a.shape, f32) for a in params]
    full = [
        jax.ShapeDtypeStruct(s, bf16)
        for s in (
            (1024, 512),
            (512, 1024),
            (1024, 128),
            (1024, 128),
            (1024, 128),
            (128, 1024),
            (2, 1024),
        )
    ]
    out = pl.pallas_call(
        output_kernel,
        out_shape=(*full, *shapes, *shapes),
        in_specs=[vmem] * 16,
        out_specs=(vmem,) * 21,
        compiler_params=pltpu.CompilerParams(vmem_limit_bytes=40 * 2**20),
        name="outputs",
    )(gathered.reshape(SIDE * SIDE, ROWS, 128), scaled, *params, *states)
    half, following, new = out[:7], out[7:14], out[14:]
    return (
        *half[:6],
        half[6][0],
        half[6][1],
        *following[:6],
        following[6][0, :64],
        following[6][0, 64:],
        *new[:6],
        new[6][0, :64],
        new[6][0, 64:],
    )


def solution(mesh):
    def along(split):
        return [
            P(*(("replica", "model") if dim == 0 else ("model", "replica"))[:2])
            if dim < 2
            else P("replica")
            for dim in split
        ]

    shards = along((0, 1, 0, 0, 0, 1, 2, 2))
    slopes = [P("replica", None, "model"), P("replica", "model", None)]
    slopes = [slopes[k] for k in (0, 1, 0, 0, 0, 1)] + [P("replica", None)] * 2
    halves = [P(None, "model"), P("model", None)]
    halves = [halves[k] for k in (0, 1, 0, 0, 0, 1)] + [P()] * 2
    return jax.shard_map(
        local,
        mesh=mesh,
        in_specs=(*slopes, *shards, *shards),
        out_specs=(*halves, *shards, *shards),
        check_vma=False,
    )
```

time: 256 us -> 86.9 us (0.34)
  waiting for transfers between devices: 173 us -> 0 us
  Pallas kernels: 0 us -> 70.2 us
  local copies, waits for them, and re-layouts: 53.3 us -> 14.1 us
  between operations: 15.1 us -> 0.88 us
  other arithmetic: 8.86 us -> 1.29 us
  starting transfers between devices: 4.33 us -> 0 us
    unnamed x3 -> x0, waiting for transfers between devices: 123 us -> none
    pallas_call x0 -> x2, Pallas kernels: none -> 70.2 us  [the longest x1 65.3 us: local(): pl.pallas_call(exchange_kernel, out_shape=(jax.ShapeDtypeStruct((SIDE, SI...]
    all_gather x1 -> x0, waiting for transfers between devices: 46.9 us -> none  [rows_first(): lax.all_gather(both, axis, axis=0, tiled=True)]
    reshape x11 -> x0, local copies, waits for them, and re-layouts: 10.8 us -> none  [the longest x1 5.02 us: one_scatter(): jnp.pad(lines, ((0, 0), (0, rows * 128 - lines.shape[1]))).reshape(-1, 128)]
    transpose x4 -> x0, local copies, waits for them, and re-layouts: 8.83 us -> none  [the longest x2 4.76 us: rows_first(): finished.append(jnp.moveaxis(section, 0, dim))]
    pad x1 -> x0, local copies, waits for them, and re-layouts: 5.86 us -> none  [one_scatter(): jnp.pad(lines, ((0, 0), (0, rows * 128 - lines.shape[1]))).reshape(-1, 128)]
    another operation x6 -> x0, local copies, waits for them, and re-layouts: 5.6 us -> none  [the longest x4 5.46 us: one_scatter(): lines = jnp.concatenate([b.reshape(length, -1) for b in parts], axis=1)]
    unnamed x59 -> x40, local copies, waits for them, and re-layouts: 17.4 us -> 12.4 us
  transfers between devices with their start and end apart: 3 -> 0, of which waited for: 3 -> 0; matrix products, arithmetic and copies ran while one was open for 1% -> 0% of each run, Pallas kernels for 0% -> 0%
where the time goes in v1:
time: 86.9 us; the launch traced here: 86.5 us
  Pallas kernels  70.2 us (81%)
  local copies, waits for them, and re-layouts  14.1 us (16%)
  other arithmetic  1.29 us (1%)
  between operations  0.88 us (1%)
    pallas_call x1, Pallas kernels, local(): pl.pallas_call(exchange_kernel, out_shape=(jax.ShapeDtypeStruct((SIDE, SI...  65.3 us
    unnamed x40, local copies, waits for them, and re-layouts  12.4 us
    pallas_call x1, Pallas kernels, local(): pl.pallas_call(output_kernel, out_shape=(*full, *shapes, *shapes), in_spe...  4.97 us

profile of v1, /device:TPU:0, one launch (start us, length us, event | category | flops | bytes accessed | tf_op | source)
XLA Modules:
  0.0 86.5 jit_solution(2624351388138962600)
XLA Ops:
  0.7 1.3 %maximum_bitcast_fusion = (f32[1,128]{1,0:T(1,128)}, f32[1,128]{1,0:T(1,128)}) fusion(f32[64]{0:T(128)} %param.39, f32[64]{0:T(128)} %param.38, f32[64]{0:T(128)} %param.47, f32[64]{0:T(128)} %param.46), kind=kLoop, calls=%fused_computation.2 | loop fusion | flops 256 | bytes 2048 | tf_op jit(solution)/shard_map/broadcast_in_dim | solution.py:647
  2.0 1.5 %copy.49.param_mixed = f32[128,64]{1,0:T(8,128)} copy(f32[128,64]{0,1:T(8,128)} %param.37) | data formatting | bytes 65536 | tf_op args[13]
  3.4 1.5 %copy.51.state_mixed = f32[128,64]{1,0:T(8,128)} copy(f32[128,64]{0,1:T(8,128)} %param.45) | data formatting | bytes 65536 | tf_op args[21]
  4.9 1.7 %copy.48.param_down = f32[512,64]{1,0:T(8,128)} copy(f32[512,64]{0,1:T(8,128)} %param.33) | data formatting | bytes 262144 | tf_op args[9]
  6.7 1.7 %copy.50.state_down = f32[512,64]{1,0:T(8,128)} copy(f32[512,64]{0,1:T(8,128)} %param.41) | data formatting | bytes 262144 | tf_op args[17]
  8.4 0.0 copy-start.5
  8.4 0.0 copy-start.6
  8.4 0.0 copy-start.8
  8.5 0.0 copy-start.9
  8.5 0.0 copy-start.10
  8.5 0.0 copy-start.11
  8.5 0.0 copy-start.12
  8.5 0.0 copy-start.13
  8.5 0.0 copy-start.14
  8.5 0.0 copy-start.15
  8.5 65.3 %exchange.1 = (bf16[4,4,784,128]{3,2,1,0:T(8,128)(2,1)}, f32[784,128]{1,0:T(8,128)}) custom-call(f32[4,4,64,512]{3,2,1,0:T(8,128)} %bitcast.20, f32[512,1024]{1,0:T(8,128)} %bitcast.21, f32[4,4,64,128]{3,2,1,0:T(8,128)} %bitcast.22, f32[4,4,64,128]{3,2,1,0:T(8,128)} %bitcast.23, f32[4,4,64,128]{3,2,1,0:T(8,128)} %bitcast.24, f32[128,1024]{1,0:T(8,128)} %bitcast.25, ...), custom_call_target="tpu_custom_call" | custom-call | tf_op jit(solution)/shard_map/exchange/pallas_call | solution.py:655
  73.8 0.0 copy-done.1
  73.8 0.0 copy-done.2
  73.8 0.0 copy-done.3
  73.8 0.0 copy-done.4
  73.8 0.0 copy-done.5
  73.8 0.0 copy-done.6
  74.0 1.9 %copy-done = bf16[4,4,784,128]{3,2,1,0:T(8,128)(2,1)S(1)} copy-done((bf16[4,4,784,128]{3,2,1,0:T(8,128)(2,1)S(1)}, bf16[4,4,784,128]{3,2,1,0:T(8,128)(2,1)}, u32[]{:S(2)}) %copy-start) | copy-done | bytes 3211288
  75.9 1.0 %copy-done.7 = f32[784,128]{1,0:T(8,128)S(1)} copy-done((f32[784,128]{1,0:T(8,128)S(1)}, f32[784,128]{1,0:T(8,128)}, u32[]{:S(2)}) %copy-start.7) | copy-done | bytes 401432
  76.8 5.0 %outputs.1 = (bf16[1024,512]{1,0:T(8,128)(2,1)}, bf16[512,1024]{1,0:T(8,128)(2,1)}, bf16[1024,128]{1,0:T(8,128)(2,1)}, bf16[1024,128]{1,0:T(8,128)(2,1)}, bf16[1...) custom-call(bf16[16,784,128]{2,1,0:T(8,128)(2,1)S(1)} %bitcast.19, ...), custom_call_target="tpu_custom_call" | custom-call | tf_op jit(solution)/shard_map/outputs/pallas_call | solution.py:721
  81.8 0.6 slice_bitcast_fusion.2
  82.4 0.6 slice_bitcast_fusion
  83.0 0.6 slice_reduce_fusion
  83.6 0.7 copy.57
  84.3 0.7 copy.59
  85.0 0.8 copy.56
  85.8 0.8 copy.58
  (14 shorter events, 0.0 us)
Async XLA Ops:
  8.4 65.4 %copy-start.1 = (f32[512,64]{1,0:T(8,128)S(1)}, f32[512,64]{1,0:T(8,128)}, u32[]{:S(2)}) copy-start(f32[512,64]{1,0:T(8,128)} %copy.48.param_down) | copy-start | bytes 393220
  8.4 65.4 %copy-start.2 = (f32[512,64]{1,0:T(8,128)S(1)}, f32[512,64]{1,0:T(8,128)}, u32[]{:S(2)}) copy-start(f32[512,64]{1,0:T(8,128)} %copy.50.state_down) | copy-start | bytes 393220
  8.4 65.4 %copy-start.3 = (f32[128,64]{1,0:T(8,128)S(1)}, f32[128,64]{1,0:T(8,128)}, u32[]{:S(2)}) copy-start(f32[128,64]{1,0:T(8,128)} %copy.49.param_mixed) | copy-start | bytes 98308
  8.4 65.4 %copy-start.4 = (f32[128,64]{1,0:T(8,128)S(1)}, f32[128,64]{1,0:T(8,128)}, u32[]{:S(2)}) copy-start(f32[128,64]{1,0:T(8,128)} %copy.51.state_mixed) | copy-start | bytes 98308
  8.4 65.4 %copy-start.5 = (f32[64,512]{1,0:T(8,128)S(1)}, f32[64,512]{1,0:T(8,128)}, u32[]{:S(2)}) copy-start(f32[64,512]{1,0:T(8,128)} %param_up.3) | copy-start | bytes 393220
  8.4 65.4 %copy-start.6 = (f32[64,512]{1,0:T(8,128)S(1)}, f32[64,512]{1,0:T(8,128)}, u32[]{:S(2)}) copy-start(f32[64,512]{1,0:T(8,128)} %state_up.3) | copy-start | bytes 393220
  8.4 65.4 %copy-start.8 = (f32[64,128]{1,0:T(8,128)S(1)}, f32[64,128]{1,0:T(8,128)}, u32[]{:S(2)}) copy-start(f32[64,128]{1,0:T(8,128)} %param_query.3) | copy-start | bytes 98308
  8.5 65.4 %copy-start.9 = (f32[64,128]{1,0:T(8,128)S(1)}, f32[64,128]{1,0:T(8,128)}, u32[]{:S(2)}) copy-start(f32[64,128]{1,0:T(8,128)} %param_key.3) | copy-start | bytes 98308
  8.5 65.4 %copy-start.10 = (f32[64,128]{1,0:T(8,128)S(1)}, f32[64,128]{1,0:T(8,128)}, u32[]{:S(2)}) copy-start(f32[64,128]{1,0:T(8,128)} %param_value.3) | copy-start | bytes 98308
  8.5 65.4 %copy-start.11 = (f32[64,128]{1,0:T(8,128)S(1)}, f32[64,128]{1,0:T(8,128)}, u32[]{:S(2)}) copy-start(f32[64,128]{1,0:T(8,128)} %state_query.3) | copy-start | bytes 98308
  8.5 65.4 %copy-start.12 = (f32[64,128]{1,0:T(8,128)S(1)}, f32[64,128]{1,0:T(8,128)}, u32[]{:S(2)}) copy-start(f32[64,128]{1,0:T(8,128)} %state_key.3) | copy-start | bytes 98308
  8.5 65.4 %copy-start.13 = (f32[64,128]{1,0:T(8,128)S(1)}, f32[64,128]{1,0:T(8,128)}, u32[]{:S(2)}) copy-start(f32[64,128]{1,0:T(8,128)} %state_value.3) | copy-start | bytes 98308
  8.5 65.4 %copy-start.14 = (f32[1,128]{1,0:T(1,128)S(1)}, f32[1,128]{1,0:T(1,128)}, u32[]{:S(2)}) copy-start(f32[1,128]{1,0:T(1,128)} %get-tuple-element.100.param_small) | copy-start | bytes 1540
  8.5 65.4 %copy-start.15 = (f32[1,128]{1,0:T(1,128)S(1)}, f32[1,128]{1,0:T(1,128)}, u32[]{:S(2)}) copy-start(f32[1,128]{1,0:T(1,128)} %get-tuple-element.101.state_small) | copy-start | bytes 1540
  73.9 1.9 %copy-start = (bf16[4,4,784,128]{3,2,1,0:T(8,128)(2,1)S(1)}, bf16[4,4,784,128]{3,2,1,0:T(8,128)(2,1)}, u32[]{:S(2)}) copy-start(bf16[4,4,784,128]{3,2,1,0:T(8,128)(2,1)} %get-tuple-element.47) | copy-start | bytes 9633796
  75.8 1.0 %copy-start.7 = (f32[784,128]{1,0:T(8,128)S(1)}, f32[784,128]{1,0:T(8,128)}, u32[]{:S(2)}) copy-start(f32[784,128]{1,0:T(8,128)} %get-tuple-element.48.scaled) | copy-start | bytes 1204228

commit v2 on v1

--- a/solution.py
+++ b/solution.py
@@ -1,4 +1,5 @@
-import functools
+import contextlib
+import math
 
 import jax
 import jax.numpy as jnp
@@ -32,21 +33,22 @@
 )
 PER_GATHER = 8
 
-GRAIN = 2.0**15
-GRAIN2 = 2.0**13
-
-
-def to_wire(x, grain):
-    v = x * grain
-    v2 = v * v
-    v4 = v2 * v2
-    return (v4 * v2 * v).astype(jnp.bfloat16)
-
-
-def from_wire(c, grain):
+SPAN, BASE = 251 * math.log(2.0), 125 * math.log(2.0)
+ONE, TWO, FOUR, EIGHT = 4.0, 8.0, 16.0, 32.0
+
+
+def to_wire(x, bound):
+    level = jnp.exp(jnp.log(jnp.abs(x)) * (1.0 / 6.0) + math.log(SPAN * bound ** (-1.0 / 6.0)))
+    size = jnp.exp(level - BASE)
+    return jnp.where(x < 0.0, -size, size).astype(jnp.bfloat16)
+
+
+def from_wire(c, bound):
     c = c.astype(jnp.float32)
-    root = jnp.exp(jnp.log(jnp.abs(c)) * (1.0 / 7.0)) * (1.0 / grain)
-    return jnp.where(c < 0.0, -root, root)
+    level = (jnp.log(jnp.abs(c)) + BASE) * (bound ** (1.0 / 6.0) / SPAN)
+    square = level * level
+    size = square * square * square
+    return jnp.where(c < 0.0, -size, size)
 
 
 def low_lanes(shape):
@@ -58,8 +60,8 @@
 
 
 def beside(x):
-    half = x.shape[0] // 2
-    return jnp.concatenate([x[:half], x[half:]], axis=1)
+    half = x.shape[1] // 2
+    return jnp.concatenate([x[:, :half], x[:, half:]], axis=0).T
 
 
 def exchange_kernel(
@@ -71,20 +73,20 @@
     mixed,
     norm,
     bias,
-    param_up,
-    param_down,
-    param_query,
-    param_key,
-    param_value,
-    param_mixed,
-    param_small,
-    state_up,
-    state_down,
-    state_query,
-    state_key,
-    state_value,
-    state_mixed,
-    state_small,
+    *rest,
+):
+    given, rest = rest[:16], rest[16:]
+    held, rest = rest[2 : 2 + 16], (*rest[:2], *rest[2 + 16 :])
+    exchange(
+        (up, down, query, key, value, mixed, norm, bias), given, held[:8], held[8:], *rest
+    )
+
+
+def exchange(
+    slopes,
+    given,
+    params,
+    states,
     gathered,
     scaled,
     mine,
@@ -115,6 +117,27 @@
     nsend_sem,
     nrecv_sem,
 ):
+    up, down, query, key, value, mixed, norm, bias = slopes
+    (
+        param_up,
+        param_down,
+        param_query,
+        param_key,
+        param_value,
+        param_mixed,
+        param_norm,
+        param_bias,
+    ) = params
+    (
+        state_up,
+        state_down,
+        state_query,
+        state_key,
+        state_value,
+        state_mixed,
+        state_norm,
+        state_bias,
+    ) = states
     replica = lax.axis_index("replica")
     model = lax.axis_index("model")
     z, y = replica // SIDE, replica % SIDE
@@ -162,6 +185,7 @@
             (bias, raw_bias),
         ],
     )
+    load("given", zip(given, (*params, *states)))
 
     barrier = pltpu.get_barrier_semaphore()
     for axis in ("y", "z"):
@@ -245,8 +269,8 @@
         far, right, left = (p + 2) % SIDE, (p + 1) % SIDE, (p + SIDE - 1) % SIDE
 
         def op(i, _):
-            send_op[i, a, :] = to_wire(share(axis, far, i)[a, :], GRAIN)
-            send_op[i, b, :] = to_wire(share(axis, far, i)[b, :], GRAIN)
+            send_op[i, a, :] = to_wire(share(axis, far, i)[a, :], ONE)
+            send_op[i, b, :] = to_wire(share(axis, far, i)[b, :], ONE)
             return 0
 
         lax.fori_loop(0, SIDE, op, 0)
@@ -256,8 +280,8 @@
         copies(chunk, 1).start()
 
         def direct(i, _):
-            send_dir[i, a, :] = to_wire(share(axis, right, i)[a, :], GRAIN)
-            send_dir[i, b, :] = to_wire(share(axis, left, i)[b, :], GRAIN)
+            send_dir[i, a, :] = to_wire(share(axis, right, i)[a, :], ONE)
+            send_dir[i, b, :] = to_wire(share(axis, left, i)[b, :], ONE)
             return 0
 
         lax.fori_loop(0, SIDE, direct, 0)
@@ -273,8 +297,8 @@
             copies(chunk, number).wait_recv()
 
             def body(i, _):
-                part = from_wire(recv_op[i, rows, :], GRAIN) + share(axis, at, i)[rows, :]
-                send_fwd[i, rows, :] = to_wire(part, GRAIN)
+                part = from_wire(recv_op[i, rows, :], ONE) + share(axis, at, i)[rows, :]
+                send_fwd[i, rows, :] = to_wire(part, TWO)
                 return 0
 
             lax.fori_loop(0, SIDE, body, 0)
@@ -290,8 +314,8 @@
             for rows in halves(chunk):
                 first_sum[i, rows, :] = (
                     share(axis, p, i)[rows, :]
-                    + from_wire(recv_dir[i, rows, :], GRAIN)
-                    + from_wire(recv_fwd[i, rows, :], GRAIN)
+                    + from_wire(recv_dir[i, rows, :], ONE)
+                    + from_wire(recv_fwd[i, rows, :], TWO)
                 )
             return 0
 
@@ -301,13 +325,13 @@
         p = position[other[CHUNKS[chunk][0]]]
         a, b = halves(chunk)
         far, right, left = (p + 2) % SIDE, (p + 1) % SIDE, (p + SIDE - 1) % SIDE
-        send_op2[a, :] = to_wire(first_sum[far, a, :], GRAIN2)
+        send_op2[a, :] = to_wire(first_sum[far, a, :], FOUR)
         copies(chunk, 6).start()
-        send_op2[b, :] = to_wire(first_sum[far, b, :], GRAIN2)
+        send_op2[b, :] = to_wire(first_sum[far, b, :], FOUR)
         copies(chunk, 7).start()
-        send_dir2[a, :] = to_wire(first_sum[right, a, :], GRAIN2)
+        send_dir2[a, :] = to_wire(first_sum[right, a, :], FOUR)
         copies(chunk, 8).start()
-        send_dir2[b, :] = to_wire(first_sum[left, b, :], GRAIN2)
+        send_dir2[b, :] = to_wire(first_sum[left, b, :], FOUR)
         copies(chunk, 9).start()
 
     def second_forward(chunk):
@@ -316,8 +340,8 @@
         right, left = (p + 1) % SIDE, (p + SIDE - 1) % SIDE
         for number, rows, at in ((6, a, left), (7, b, right)):
             copies(chunk, number).wait_recv()
-            part = from_wire(recv_op2[rows, :], GRAIN2) + first_sum[at, rows, :]
-            send_fwd2[rows, :] = to_wire(part, GRAIN2)
+            part = from_wire(recv_op2[rows, :], FOUR) + first_sum[at, rows, :]
+            send_fwd2[rows, :] = to_wire(part, EIGHT)
             copies(chunk, 4 + number).start()
 
     def second_finish(chunk):
@@ -327,8 +351,8 @@
         for rows in halves(chunk):
             mean[rows, :] = (
                 first_sum[p, rows, :]
-                + from_wire(recv_dir2[rows, :], GRAIN2)
-                + from_wire(recv_fwd2[rows, :], GRAIN2)
+                + from_wire(recv_dir2[rows, :], FOUR)
+                + from_wire(recv_fwd2[rows, :], EIGHT)
             ) * (SIDE * SIDE) ** (-0.5)
 
     def row_squares(row, width, param):
@@ -476,6 +500,7 @@
         second_send(chunk)
     second_finish(2)
     second_finish(3)
+    loaded("given")
     norm_send(
         0, (row_squares(UP, 4, param_up),), (column_squares(DOWN, 256, param_down),)
     )
@@ -509,8 +534,8 @@
     updated(
         small,
         mean[small, :] * 2.0,
-        jnp.broadcast_to(param_small[...], (16, 128)),
-        jnp.broadcast_to(state_small[...], (16, 128)),
+        jnp.concatenate([param_norm[...], param_bias[...]], axis=1),
+        jnp.concatenate([state_norm[...], state_bias[...]], axis=1),
     )
     gather_send(3, 0)
     gather_send(0, 1)
@@ -537,87 +562,28 @@
             norm_copy(turn_number, step).wait_send()
 
 
-def output_kernel(
-    gathered,
-    scaled,
-    param_up,
-    param_down,
-    param_query,
-    param_key,
-    param_value,
-    param_mixed,
-    param_small,
-    state_up,
-    state_down,
-    state_query,
-    state_key,
-    state_value,
-    state_mixed,
-    state_small,
-    half_up,
-    half_down,
-    half_query,
-    half_key,
-    half_value,
-    half_mixed,
-    half_small,
-    next_up,
-    next_down,
-    next_query,
-    next_key,
-    next_value,
-    next_mixed,
-    next_small,
-    new_up,
-    new_down,
-    new_query,
-    new_key,
-    new_value,
-    new_mixed,
-    new_small,
-):
-    def stepped(m, param, state):
-        state_new = hold_rate * state + (1.0 - hold_rate) * m * m
-        return param - learn_rate * m * lax.rsqrt(state_new + 1e-06), state_new
-
-    def by_rows(row, width, param, state, following, new):
-        for c in range(width):
-            lanes = pl.ds(128 * c, 128)
-            m = scaled[pl.ds(row + 64 * c, 64), :]
-            following[:, lanes], new[:, lanes] = stepped(m, param[:, lanes], state[:, lanes])
-
-    def by_columns(row, length, param, state, following, new):
-        for part in range(2):
-            rows = pl.ds(part * length, length)
-            m = scaled[pl.ds(row, length), :]
-            if part:
-                m = turn(m)
-            following[rows, :], new[rows, :] = stepped(m[:, 0:64], param[rows, :], state[rows, :])
-
-    by_rows(UP, 4, param_up, state_up, next_up, new_up)
-    by_rows(QUERY, 1, param_query, state_query, next_query, new_query)
-    by_rows(KEY, 1, param_key, state_key, next_key, new_key)
-    by_rows(VALUE, 1, param_value, state_value, next_value, new_value)
-    by_columns(DOWN, 256, param_down, state_down, next_down, new_down)
-    by_columns(MIXED, 64, param_mixed, state_mixed, next_mixed, new_mixed)
-    next_small[...], new_small[...] = stepped(
-        scaled[pl.ds(SMALL, 1), :], param_small[...], state_small[...]
-    )
-
-    def rows_of(i, _):
-        at = pl.multiple_of(i * 64, 64)
-        rows = pl.ds(at, 64)
-        for c in range(4):
-            half_up[rows, pl.ds(128 * c, 128)] = gathered[i, pl.ds(UP + 64 * c, 64), :]
-        half_query[rows, :] = gathered[i, pl.ds(QUERY, 64), :]
-        half_key[rows, :] = gathered[i, pl.ds(KEY, 64), :]
-        half_value[rows, :] = gathered[i, pl.ds(VALUE, 64), :]
-        return 0
-
-    lax.fori_loop(0, SIDE * SIDE, rows_of, 0)
+def output_kernel(gathered, scaled, *refs):
+    params, states, refs = refs[:8], refs[8:16], refs[16:]
+    half, following, new, refs = refs[:8], refs[8:16], refs[16:24], refs[24:]
+    wide_down, wide_mixed, small_halves, sem = *refs[:2], refs[2:4], refs[-1]
+    next_held, new_held = refs[4:12], refs[12:20]
+    started = []
+
+    def store(src, dst):
+        copy = pltpu.make_async_copy(src, dst, sem.at[len(started)])
+        copy.start()
+        started.append(copy)
+
+    for c in range(4):
+        store(gathered.at[:, pl.ds(UP + 64 * c, 64), :], half[0].at[:, :, pl.ds(128 * c, 128)])
+    for number, row in ((2, QUERY), (3, KEY), (4, VALUE)):
+        store(gathered.at[:, pl.ds(row, 64), :], half[number])
 
     low = low_lanes((64, 128))
-    for out, row, length in ((half_down, DOWN, 256), (half_mixed, MIXED, 64)):
+    for out, wide, row, length in (
+        (half[1], wide_down, DOWN, 256),
+        (half[5], wide_mixed, MIXED, 64),
+    ):
         for pair in range(8):
             lanes = pl.ds(128 * pair, 128)
 
@@ -625,63 +591,97 @@
                 at = pl.multiple_of(i * 64, 64)
                 a = gathered[2 * pair, pl.ds(row + at, 64), :].astype(jnp.float32)
                 b = gathered[2 * pair + 1, pl.ds(row + at, 64), :].astype(jnp.float32)
-                out[pl.ds(at, 64), lanes] = jnp.where(low, a, turn(b)).astype(jnp.bfloat16)
-                out[pl.ds(length + at, 64), lanes] = jnp.where(low, turn(a), b).astype(
+                wide[pl.ds(at, 64), lanes] = jnp.where(low, a, turn(b)).astype(jnp.bfloat16)
+                wide[pl.ds(length + at, 64), lanes] = jnp.where(low, turn(a), b).astype(
                     jnp.bfloat16
                 )
                 return 0
 
             lax.fori_loop(0, length // 64, body, 0)
+            store(wide.at[:, lanes], out.at[:, lanes])
+
+    def step(number, at, m):
+        param, state = params[number][at], states[number][at]
+        state_new = hold_rate * state + (1.0 - hold_rate) * m * m
+        next_held[number][at] = param - learn_rate * m * lax.rsqrt(state_new + 1e-06)
+        new_held[number][at] = state_new
+
+    def done(number):
+        store(next_held[number], following[number])
+        store(new_held[number], new[number])
+
+    for number, row, width in ((0, UP, 4), (2, QUERY, 1), (3, KEY, 1), (4, VALUE, 1)):
+        for c in range(width):
+            at = (slice(None), pl.ds(128 * c, 128))
+            step(number, at, scaled[pl.ds(row + 64 * c, 64), :])
+        done(number)
+    for number, row, length in ((1, DOWN, 256), (5, MIXED, 64)):
+        columns = scaled[pl.ds(row, length), :].T
+        columns = jnp.concatenate([columns[:64], columns[64:]], axis=1)
+        step(number, (slice(None), slice(None)), columns)
+        done(number)
+    line = scaled[pl.ds(SMALL, 1), :]
+    for number, m in ((6, line[:, :64]), (7, turn(line)[:, :64])):
+        step(number, (slice(None), slice(None)), m)
+        done(number)
+
+    sub = lax.broadcasted_iota(jnp.int32, (8, 128), 0)
     low = low_lanes((1, 128))
+    lines = [jnp.zeros((8, 128), jnp.float32)] * 2
     for pair in range(8):
-        lanes = pl.ds(128 * pair, 128)
         a = gathered[2 * pair, pl.ds(SMALL, 16), :].astype(jnp.float32)[0:1]
         b = gathered[2 * pair + 1, pl.ds(SMALL, 16), :].astype(jnp.float32)[0:1]
-        half_small[0:1, lanes] = jnp.where(low, a, turn(b)).astype(jnp.bfloat16)
-        half_small[1:2, lanes] = jnp.where(low, turn(a), b).astype(jnp.bfloat16)
+        lines[0] = jnp.where(sub == pair, jnp.where(low, a, turn(b)), lines[0])
+        lines[1] = jnp.where(sub == pair, jnp.where(low, turn(a), b), lines[1])
+    for k in range(2):
+        small_halves[k][...] = lines[k].astype(jnp.bfloat16)
+        store(small_halves[k], half[6 + k])
+    for copy in started:
+        copy.wait()
+
+
+def stay(*arrays):
+    return [pltpu.with_memory_space_constraint(a, pltpu.HBM) for a in arrays]
 
 
 def local(*arrays):
     slopes, params, states = arrays[:8], arrays[8:16], arrays[16:]
     up, down, query, key, value, mixed, norm, bias = slopes
-    small = [jnp.concatenate([a[6], a[7]])[None] for a in (params, states)]
-    params, states = (*params[:6], small[0]), (*states[:6], small[1])
+
+    def shown(group):
+        up, down, query, key, value, mixed, norm, bias = group
+        return up, down.T, query, key, value, mixed.T, norm[None], bias[None]
+
+    params, states = shown(params), shown(states)
     vmem = pl.BlockSpec(memory_space=pltpu.VMEM)
     anywhere = pl.BlockSpec(memory_space=pl.ANY)
     f32, bf16 = jnp.float32, jnp.bfloat16
     wire = pltpu.VMEM((SIDE, ROWS, 128), bf16)
     wire2 = pltpu.VMEM((ROWS, 128), bf16)
     dma = pltpu.SemaphoreType.DMA
+    held = [pltpu.VMEM(a.shape, f32) for a in params]
     gathered, scaled = pl.pallas_call(
         exchange_kernel,
         out_shape=(
-            jax.ShapeDtypeStruct((SIDE, SIDE, ROWS, 128), bf16),
-            jax.ShapeDtypeStruct((ROWS, 128), f32),
+            pltpu.VMEM((SIDE, SIDE, ROWS, 128), bf16),
+            pltpu.VMEM((ROWS, 128), f32),
         ),
-        in_specs=[anywhere] * 8 + [vmem] * 14,
+        in_specs=[pl.BlockSpec(memory_space=pltpu.HBM)] * 24,
         out_specs=(vmem, vmem),
         scratch_shapes=[
+            *held,
+            *held,
             pltpu.VMEM((SIDE, SIDE, ROWS, 128), f32),
             pltpu.VMEM((512, 1024), f32),
             pltpu.VMEM((128, 1024), f32),
             pltpu.VMEM((1, 1024), f32),
             pltpu.VMEM((1, 1024), f32),
-            wire,
-            wire,
-            wire,
-            wire,
-            wire,
-            wire,
+            *[wire] * 6,
             pltpu.VMEM((SIDE, ROWS, 128), f32),
-            wire2,
-            wire2,
-            wire2,
-            wire2,
-            wire2,
-            wire2,
+            *[wire2] * 6,
             pltpu.VMEM((ROWS, 128), f32),
             pltpu.VMEM((2, PEERS, 8, 128), f32),
-            dma((11,)),
+            dma((11 + 16,)),
             dma((len(CHUNKS) * PER,)),
             dma((len(CHUNKS) * PER,)),
             dma((len(GATHERS) * PER_GATHER,)),
@@ -690,53 +690,72 @@
             dma((2 * (PEERS - 1),)),
         ],
         compiler_params=pltpu.CompilerParams(
-            collective_id=0, has_side_effects=True, vmem_limit_bytes=60 * 2**20
+            collective_id=0, has_side_effects=True, vmem_limit_bytes=48 * 2**20
         ),
         name="exchange",
     )(
-        up.reshape(SIDE, SIDE, 64, 512),
-        down[0],
-        query.reshape(SIDE, SIDE, 64, 128),
-        key.reshape(SIDE, SIDE, 64, 128),
-        value.reshape(SIDE, SIDE, 64, 128),
-        mixed[0],
-        norm,
-        bias,
-        *params,
-        *states,
-    )
-    shapes = [jax.ShapeDtypeStruct(a.shape, f32) for a in params]
+        *stay(
+            up.reshape(SIDE, SIDE, 64, 512),
+            down[0],
+            query.reshape(SIDE, SIDE, 64, 128),
+            key.reshape(SIDE, SIDE, 64, 128),
+            value.reshape(SIDE, SIDE, 64, 128),
+            mixed[0],
+            norm,
+            bias,
+            *params,
+            *states,
+        )
+    )
+    own = [jax.ShapeDtypeStruct(a.shape, f32) for a in params]
     full = [
         jax.ShapeDtypeStruct(s, bf16)
         for s in (
-            (1024, 512),
+            (16, 64, 512),
             (512, 1024),
-            (1024, 128),
-            (1024, 128),
-            (1024, 128),
+            (16, 64, 128),
+            (16, 64, 128),
+            (16, 64, 128),
             (128, 1024),
-            (2, 1024),
+            (8, 128),
+            (8, 128),
         )
     ]
     out = pl.pallas_call(
         output_kernel,
-        out_shape=(*full, *shapes, *shapes),
-        in_specs=[vmem] * 16,
-        out_specs=(vmem,) * 21,
-        compiler_params=pltpu.CompilerParams(vmem_limit_bytes=40 * 2**20),
+        out_shape=(*full, *own, *own),
+        in_specs=[vmem] * 18,
+        out_specs=(anywhere,) * 24,
+        scratch_shapes=[
+            pltpu.VMEM((512, 1024), bf16),
+            pltpu.VMEM((128, 1024), bf16),
+            pltpu.VMEM((8, 128), bf16),
+            pltpu.VMEM((8, 128), bf16),
+            *held,
+            *held,
+            dma((7 + 16 + 16 + 2,)),
+        ],
+        compiler_params=pltpu.CompilerParams(vmem_limit_bytes=16 * 2**20),
         name="outputs",
     )(gathered.reshape(SIDE * SIDE, ROWS, 128), scaled, *params, *states)
-    half, following, new = out[:7], out[7:14], out[14:]
+    half, following, new = out[:8], out[8:16], out[16:]
+    half_up, half_down, half_query, half_key, half_value, half_mixed, half_norm, half_bias = half
+
+    def back(group):
+        up, down, query, key, value, mixed, norm, bias = group
+        return up, down.T, query, key, value, mixed.T, norm[0], bias[0]
+
     return (
-        *half[:6],
-        half[6][0],
-        half[6][1],
-        *following[:6],
-        following[6][0, :64],
-        following[6][0, 64:],
-        *new[:6],
-        new[6][0, :64],
-        new[6][0, 64:],
+        half_up.reshape(1024, 512),
+        half_down,
+        half_query.reshape(1024, 128),
+        half_key.reshape(1024, 128),
+        half_value.reshape(1024, 128),
+        half_mixed,
+        half_norm.reshape(1024),
+        half_bias.reshape(1024),
+        *back(following),
+        *back(new),
     )
 
 

time: 86.9 us -> 68.5 us (0.79)
  local copies, waits for them, and re-layouts: 14.1 us -> 0.07 us
  Pallas kernels: 70.2 us -> 67.4 us
  other arithmetic: 1.29 us -> 0 us
    unnamed x40 -> x32, local copies, waits for them, and re-layouts: 12.4 us -> 0.07 us
    pallas_call x2, Pallas kernels: 70.2 us -> 67.4 us  [the longest x1 63.2 us: local(): pl.pallas_call(exchange_kernel, out_shape=(pltpu.VMEM((SIDE, SIDE, ROWS,...]
    broadcast_in_dim x1 -> x0, other arithmetic: 1.29 us -> none  [local(): small = [jnp.concatenate([a[6], a[7]])[None] for a in (params, states)]]
    squeeze x2 -> x0, local copies, waits for them, and re-layouts: 1.17 us -> none  [the longest x1 0.58 us: local(): following[6][0, 64:]]
where the time goes in v2:
time: 68.5 us; the launch traced here: 68.4 us
  Pallas kernels  67.4 us (98%)
  between operations  0.93 us (1%)
    pallas_call x1, Pallas kernels, local(): pl.pallas_call(exchange_kernel, out_shape=(pltpu.VMEM((SIDE, SIDE, ROWS,...  63.2 us
    pallas_call x1, Pallas kernels, local(): pl.pallas_call(output_kernel, out_shape=(*full, *own, *own), in_specs=[vm...  4.22 us

profile of v2, /device:TPU:0, one launch (start us, length us, event | category | flops | bytes accessed | tf_op | source)
XLA Modules:
  0.0 68.4 jit_solution(17934363213460194239)
XLA Ops:
  0.7 0.0 copy-start
  0.7 0.0 copy-start.1
  0.7 0.0 copy-start.2
  0.7 0.0 copy-start.3
  0.7 0.0 copy-start.4
  0.7 0.0 copy-start.5
  0.7 0.0 copy-start.6
  0.7 0.0 copy-start.7
  0.7 0.0 copy-start.8
  0.8 0.0 copy-start.9
  0.8 0.0 copy-start.10
  0.8 0.0 copy-start.11
  0.8 0.0 copy-start.12
  0.8 0.0 copy-start.13
  0.8 63.2 %exchange.1 = (bf16[4,4,784,128]{3,2,1,0:T(8,128)(2,1)S(1)}, f32[784,128]{1,0:T(8,128)S(1)}) custom-call(f32[4,4,64,512]{3,2,1,0:T(8,128)} %bitcast.46, f32[512,1024]{1,0:T(8,128)} %bitcast.47, f32[4,4,64,128]{3,2,1,0:T(8,128)} %bitcast.48, f32[4,4,64,128]{3,2,1,0:T(8,128)} %bitcast.49, f32[4,4,64,128]{3,2,1,0:T(8,128)} %bitcast.50, f32[128,1024]{1,0:T(8,128)} %bitcast.51, ...), custom_call_target="tpu_custom_call" | custom-call | tf_op jit(solution)/shard_map/exchange/pallas_call | solution.py:663
  64.0 0.0 copy-done
  64.0 0.0 copy-done.1
  64.0 0.0 copy-done.2
  64.0 0.0 copy-done.3
  64.1 0.0 copy-done.4
  64.1 0.0 copy-done.5
  64.1 0.0 copy-done.6
  64.1 0.0 copy-done.7
  64.1 0.0 copy-done.8
  64.1 0.0 copy-done.9
  64.1 0.0 copy-done.10
  64.1 0.0 copy-done.11
  64.1 0.0 copy-done.12
  64.1 0.0 copy-done.13
  64.2 0.0 copy-done.14
  64.2 0.0 copy-done.15
  64.2 4.2 %outputs.1 = (bf16[16,64,512]{2,1,0:T(8,128)(2,1)}, bf16[512,1024]{1,0:T(8,128)(2,1)}, bf16[16,64,128]{2,1,0:T(8,128)(2,1)}, bf16[16,64,128]{2,1,0:T(8,128)(2,1)...) custom-call(bf16[16,784,128]{2,1,0:T(8,128)(2,1)S(1)} %bitcast.29, ...), custom_call_target="tpu_custom_call" | custom-call | tf_op jit(solution)/shard_map/outputs/pallas_call | solution.py:724
  (2 shorter events, 0.0 us)
Async XLA Ops:
  0.7 63.4 %copy-start = (f32[64,512]{1,0:T(8,128)S(1)}, f32[64,512]{1,0:T(8,128)}, u32[]{:S(2)}) copy-start(f32[64,512]{1,0:T(8,128)} %refs_0_.1) | copy-start | bytes 393220
  0.7 63.4 %copy-start.1 = (f32[512,64]{0,1:T(8,128)S(1)}, f32[512,64]{0,1:T(8,128)}, u32[]{:S(2)}) copy-start(f32[512,64]{0,1:T(8,128)} %param.33) | copy-start | bytes 393220
  0.7 63.4 %copy-start.2 = (f32[64,512]{1,0:T(8,128)S(1)}, f32[64,512]{1,0:T(8,128)}, u32[]{:S(2)}) copy-start(f32[64,512]{1,0:T(8,128)} %refs_8_.1) | copy-start | bytes 393220
  0.7 63.4 %copy-start.3 = (f32[512,64]{0,1:T(8,128)S(1)}, f32[512,64]{0,1:T(8,128)}, u32[]{:S(2)}) copy-start(f32[512,64]{0,1:T(8,128)} %param.41) | copy-start | bytes 393220
  0.7 63.4 %copy-start.4 = (f32[64,128]{1,0:T(8,128)S(1)}, f32[64,128]{1,0:T(8,128)}, u32[]{:S(2)}) copy-start(f32[64,128]{1,0:T(8,128)} %refs_2_.1) | copy-start | bytes 98308
  0.7 63.4 %copy-start.5 = (f32[64,128]{1,0:T(8,128)S(1)}, f32[64,128]{1,0:T(8,128)}, u32[]{:S(2)}) copy-start(f32[64,128]{1,0:T(8,128)} %refs_3_.1) | copy-start | bytes 98308
  0.7 63.4 %copy-start.6 = (f32[64,128]{1,0:T(8,128)S(1)}, f32[64,128]{1,0:T(8,128)}, u32[]{:S(2)}) copy-start(f32[64,128]{1,0:T(8,128)} %refs_4_.1) | copy-start | bytes 98308
  0.7 63.4 %copy-start.7 = (f32[128,64]{0,1:T(8,128)S(1)}, f32[128,64]{0,1:T(8,128)}, u32[]{:S(2)}) copy-start(f32[128,64]{0,1:T(8,128)} %param.37) | copy-start | bytes 98308
  0.7 63.4 %copy-start.8 = (f32[64,128]{1,0:T(8,128)S(1)}, f32[64,128]{1,0:T(8,128)}, u32[]{:S(2)}) copy-start(f32[64,128]{1,0:T(8,128)} %refs_10_.1) | copy-start | bytes 98308
  0.8 63.4 %copy-start.9 = (f32[64,128]{1,0:T(8,128)S(1)}, f32[64,128]{1,0:T(8,128)}, u32[]{:S(2)}) copy-start(f32[64,128]{1,0:T(8,128)} %refs_11_.1) | copy-start | bytes 98308
  0.8 63.4 %copy-start.10 = (f32[64,128]{1,0:T(8,128)S(1)}, f32[64,128]{1,0:T(8,128)}, u32[]{:S(2)}) copy-start(f32[64,128]{1,0:T(8,128)} %refs_12_.1) | copy-start | bytes 98308
  0.8 63.4 %copy-start.11 = (f32[128,64]{0,1:T(8,128)S(1)}, f32[128,64]{0,1:T(8,128)}, u32[]{:S(2)}) copy-start(f32[128,64]{0,1:T(8,128)} %param.45) | copy-start | bytes 98308
  0.8 63.4 %copy-start.12 = (f32[64]{0:T(128)S(1)}, f32[64]{0:T(128)}, u32[]{:S(2)}) copy-start(f32[64]{0:T(128)} %param.38) | copy-start | bytes 772
  0.8 63.4 %copy-start.13 = (f32[64]{0:T(128)S(1)}, f32[64]{0:T(128)}, u32[]{:S(2)}) copy-start(f32[64]{0:T(128)} %param.39) | copy-start | bytes 772
  0.8 63.4 %copy-start.14 = (f32[64]{0:T(128)S(1)}, f32[64]{0:T(128)}, u32[]{:S(2)}) copy-start(f32[64]{0:T(128)} %param.46) | copy-start | bytes 772
  0.8 63.4 %copy-start.15 = (f32[64]{0:T(128)S(1)}, f32[64]{0:T(128)}, u32[]{:S(2)}) copy-start(f32[64]{0:T(128)} %param.47) | copy-start | bytes 772

commit v3 on v2

v3 whole, which is shorter than its diff:
```python
import contextlib
import math

import jax
import jax.numpy as jnp
from jax import lax
from jax.experimental import pallas as pl
from jax.experimental.pallas import tpu as pltpu
from jax.sharding import PartitionSpec as P

learn_rate = 0.025
hold_rate = 0.7
MESH = pl.DeviceIdType.MESH
SIDE = 4
PEERS = 8

UP, QUERY, KEY, MIXED, VALUE, SMALL, DOWN, ROWS = 0, 256, 320, 384, 448, 512, 528, 784

CHUNKS = (
    ("y", UP, 64, 64, 0),
    ("z", MIXED, 80, 64, 1),
    ("y", UP + 128, 64, 64, 2),
    ("z", DOWN, 64, 64, 4),
    ("y", QUERY, 64, 64, 3),
    ("z", DOWN + 128, 64, 64, 4),
)
COUNT = len(CHUNKS)
GROUPS = 5
PER = 12
PER_GATHER = 20
LOADS = 8 + 16 + 8 + 3 + 2 + 16

ORDER = (
    ("send", 0), ("send", 1), ("send", 3), ("send", 5), ("send", 4), ("send", 2), ("fwdB", 0),
    ("fwdA", 0), ("fwdA", 1), ("fwdB", 1), ("fwdA", 4), ("fwdB", 4), ("fwdB", 3), ("fwdA", 3),
    ("fwdB", 2), ("fwdA", 2), ("fwdB", 5), ("fwdA", 5), ("prepare", 0), ("fin", 0), ("fin", 1),
    ("fin", 4), ("fin", 3), ("fin", 2), ("Fwd", 1), ("fin", 5), ("Fwd", 0), ("Fwd", 4), ("Fwd", 3),
    ("Fwd", 2), ("Fin", 1), ("norm", 1), ("Fwd", 5), ("Fin", 0), ("norm", 0), ("Fin", 4),
    ("norm", 3), ("Fin", 3), ("Fin", 2), ("norm", 2), ("Fin", 5), ("norm", 4), ("ratio", 1),
    ("upd", 1), ("ratio", 0), ("upd", 0), ("ratio", 3), ("upd", 4), ("ratio", 2), ("upd", 2),
    ("ratio", 4), ("upd", 3), ("xf-", 1), ("upd", 5), ("keep", 0), ("ownF+", 1), ("xf+", 1),
    ("ownF-", 1), ("ownF-", 0), ("xf-", 0), ("ownF+", 0), ("xf+", 0), ("ownF+", 4), ("ownF-", 4),
    ("xf-", 4), ("xf+", 4), ("xf+", 2), ("ownF+", 2), ("xf-", 2), ("ownF-", 2), ("ownF+", 3),
    ("xf+", 3), ("ownF-", 3), ("xf-", 3), ("xf+", 5), ("rF-", 1), ("rF+", 1), ("xf-", 5),
    ("far", 1), ("ownF+", 5), ("ownF-", 5), ("rF+", 0), ("rF-", 0), ("lF-", 1), ("lF+", 1),
    ("lF+", 0), ("lF-", 0), ("far", 0), ("far", 4), ("far", 2), ("rF+", 4), ("rF-", 4), ("lF-", 3),
    ("lF-", 4), ("lF+", 4), ("lF+", 3), ("lF+", 2), ("lF-", 2), ("rF+", 3), ("rF-", 3), ("rF-", 2),
    ("lF-", 5), ("lF+", 5), ("rF+", 2), ("far", 3), ("far", 5), ("rF+", 5), ("rF-", 5), ("fF+", 1),
    ("fF-", 1), ("fF-", 0), ("fF+", 0), ("fF-", 4), ("fF+", 4), ("fF-", 2), ("fF+", 2), ("fF-", 3),
    ("fF+", 3), ("fF+", 5), ("fF-", 5), ("end", 1), ("end", 0), ("end", 4), ("end", 2), ("end", 3),
    ("end", 5),
)


SPAN, BASE = 251 * math.log(2.0), 125 * math.log(2.0)
ONE, TWO, FOUR, EIGHT = 4.0, 8.0, 16.0, 32.0


def to_wire(x, bound):
    level = jnp.exp(jnp.log(jnp.abs(x)) * (1.0 / 6.0) + math.log(SPAN * bound ** (-1.0 / 6.0)))
    size = jnp.exp(level - BASE)
    return jnp.where(x < 0.0, -size, size).astype(jnp.bfloat16)


def from_wire(c, bound):
    c = c.astype(jnp.float32)
    level = (jnp.log(jnp.abs(c)) + BASE) * (bound ** (1.0 / 6.0) / SPAN)
    square = level * level
    size = square * square * square
    return jnp.where(c < 0.0, -size, size)


def low_lanes(shape):
    return lax.broadcasted_iota(jnp.int32, shape, len(shape) - 1) < 64


def turn(x):
    return pltpu.roll(x, 64, 1)


def beside(x):
    half = x.shape[1] // 2
    return jnp.concatenate([x[:, :half], x[:, half:]], axis=0).T


def stage(name):
    return contextlib.nullcontext()


def exchange_kernel(*refs):
    slopes, given, refs = refs[:8], refs[8:24], refs[24:]
    gathered, wide_down, wide_mixed, small_norm, small_bias, refs = *refs[:5], refs[5:]
    following, new, refs = refs[:8], refs[8:16], refs[16:]
    params, states, refs = refs[:8], refs[8:16], refs[16:]
    exchange(
        slopes,
        given,
        gathered,
        (wide_down, wide_mixed),
        (small_norm, small_bias),
        following,
        new,
        params,
        states,
        *refs,
    )


def exchange(
    slopes,
    given,
    gathered,
    wides,
    small_halves,
    following,
    new,
    params,
    states,
    scaled,
    mine,
    raw_norm,
    raw_bias,
    packed_param,
    packed_state,
    send_op,
    send_dir,
    send_fwd,
    recv_op,
    recv_dir,
    recv_fwd,
    first_sum,
    send_op2,
    send_dir2,
    send_fwd2,
    recv_op2,
    recv_dir2,
    recv_fwd2,
    mean,
    squares,
    load_sem,
    send_sem,
    recv_sem,
    gsend_sem,
    grecv_sem,
    nsend_sem,
    nrecv_sem,
):
    up, down, query, key, value, mixed, norm, bias = slopes
    replica = lax.axis_index("replica")
    model = lax.axis_index("model")
    z, y = replica // SIDE, replica % SIDE

    def place(axis, step):
        if axis == "y":
            return (z * SIDE + (y + step) % SIDE, model)
        return (((z + step) % SIDE) * SIDE + y, model)

    position = {"y": y, "z": z}
    other = {"y": "z", "z": "y"}

    loads = {}
    count = [0]

    def load(name, pairs):
        loads[name] = []
        for src, dst in pairs:
            copy = pltpu.make_async_copy(src, dst, load_sem.at[count[0]])
            count[0] += 1
            copy.start()
            loads[name].append(copy)

    def loaded(name):
        for copy in loads.pop(name, ()):
            copy.wait()

    def up_part(part):
        return [
            (
                up.at[:, :, pl.ds(32 * part, 32), pl.ds(128 * c, 128)],
                mine.at[:, :, pl.ds(UP + 128 * part + 32 * c, 32), :],
            )
            for c in range(4)
        ]

    def columns(array, row, start, length):
        return [
            (
                array.at[:, pl.ds(start, length), pl.ds(128 * k, 128)],
                mine.at[k // 2, pl.ds(2 * (k % 2), 2), pl.ds(row + start, length), :],
            )
            for k in range(8)
        ]

    load(0, up_part(0))
    load(
        1,
        [
            *columns(mixed, MIXED, 0, 64),
            (value, mine.at[:, :, pl.ds(VALUE, 64), :]),
            (norm, raw_norm),
            (bias, raw_bias),
        ],
    )
    load(3, columns(down, DOWN, 0, 128))
    load(2, up_part(1))
    load(4, [(query, mine.at[:, :, pl.ds(QUERY, 64), :]), (key, mine.at[:, :, pl.ds(KEY, 64), :])])
    load(5, columns(down, DOWN, 128, 128))
    load("given", zip(given, (*params, *states)))

    barrier = pltpu.get_barrier_semaphore()
    for axis in ("y", "z"):
        for step in (1, SIDE - 1):
            pl.semaphore_signal(barrier, 1, device_id=place(axis, step), device_id_type=MESH)
    for step in range(1, PEERS):
        pl.semaphore_signal(
            barrier, 1, device_id=(replica, (model + step) % PEERS), device_id_type=MESH
        )
    waiting = [True]

    def pack_small():
        low = low_lanes((1, 128))
        for pair in range(8):
            lanes = pl.ds(128 * pair, 128)
            zz, yy = (2 * pair) // SIDE, (2 * pair) % SIDE
            a = raw_norm[:, lanes] * 0.5
            b = raw_bias[:, lanes] * 0.5
            mine[zz, yy, pl.ds(SMALL, 16), :] = jnp.broadcast_to(
                jnp.where(low, a, turn(b)), (16, 128)
            )
            mine[zz, yy + 1, pl.ds(SMALL, 16), :] = jnp.broadcast_to(
                jnp.where(low, turn(a), b), (16, 128)
            )

    def halves(chunk):
        _, row, first, second, _ = CHUNKS[chunk]
        return pl.ds(row, first), pl.ds(row + first, second)

    def share(axis, at, b):
        if axis == "y":
            return mine.at[b, at]
        return mine.at[at, b]

    def copies(chunk, number):
        axis = CHUNKS[chunk][0]
        a, b = halves(chunk)
        if number >= 6:
            axis = other[axis]
            bufs = ((send_op2, recv_op2), (send_dir2, recv_dir2), (send_fwd2, recv_fwd2))
            a, b = (a, slice(None)), (b, slice(None))
        else:
            bufs = ((send_op, recv_op), (send_dir, recv_dir), (send_fwd, recv_fwd))
            a, b = (slice(None), a, slice(None)), (slice(None), b, slice(None))
        kind, half = divmod(number % 6, 2)
        src, dst = bufs[kind]
        rows = b if half else a
        step = (SIDE - 1, 1)[half] if kind != 1 else (1, SIDE - 1)[half]
        k = chunk * PER + number
        return pltpu.make_async_remote_copy(
            src_ref=src.at[rows],
            dst_ref=dst.at[rows],
            send_sem=send_sem.at[k],
            recv_sem=recv_sem.at[k],
            device_id=place(axis, step),
            device_id_type=MESH,
        )

    def send(chunk):
        loaded(chunk)
        if chunk == 1:
            pack_small()
        axis = CHUNKS[chunk][0]
        p = position[axis]
        a, b = halves(chunk)
        far, right, left = (p + 2) % SIDE, (p + 1) % SIDE, (p + SIDE - 1) % SIDE

        def op(i, _):
            send_op[i, a, :] = to_wire(share(axis, far, i)[a, :], ONE)
            send_op[i, b, :] = to_wire(share(axis, far, i)[b, :], ONE)
            return 0

        lax.fori_loop(0, SIDE, op, 0)
        if waiting:
            waiting.pop()
            pl.semaphore_wait(barrier, 4 + PEERS - 1)
        copies(chunk, 0).start()
        copies(chunk, 1).start()

        def direct(i, _):
            send_dir[i, a, :] = to_wire(share(axis, right, i)[a, :], ONE)
            send_dir[i, b, :] = to_wire(share(axis, left, i)[b, :], ONE)
            return 0

        lax.fori_loop(0, SIDE, direct, 0)
        copies(chunk, 2).start()
        copies(chunk, 3).start()

    def forward(chunk, number):
        axis = CHUNKS[chunk][0]
        rows = halves(chunk)[number]
        at = (position[axis] + (SIDE - 1, 1)[number]) % SIDE
        copies(chunk, number).wait_recv()

        def body(i, _):
            part = from_wire(recv_op[i, rows, :], ONE) + share(axis, at, i)[rows, :]
            send_fwd[i, rows, :] = to_wire(part, TWO)
            return 0

        lax.fori_loop(0, SIDE, body, 0)
        copies(chunk, 4 + number).start()

    def finish(chunk):
        axis, row, first, second, _ = CHUNKS[chunk]
        p = position[axis]
        for number in (2, 3, 4, 5):
            copies(chunk, number).wait_recv()

        def summed(i, rows):
            return (
                share(axis, p, i)[rows, :]
                + from_wire(recv_dir[i, rows, :], ONE)
                + from_wire(recv_fwd[i, rows, :], TWO)
            )

        paired = {"y": 0, "z": first + second}[axis] if chunk != 1 else 64

        def pairs(t, _):
            for start in range(0, paired, 64):
                rows = pl.ds(row + start, 64)
                low = low_lanes((64, 128))
                upper, lower = summed(2 * t, rows), summed(2 * t + 1, rows)
                first_sum[2 * t, rows, :] = jnp.where(low, upper, turn(lower))
                first_sum[2 * t + 1, rows, :] = jnp.where(low, turn(upper), lower)
            return 0

        if paired:
            lax.fori_loop(0, SIDE // 2, pairs, 0)

        def plain(i, _):
            for start, stop in ((paired, max(first, paired)), (max(first, paired), first + second)):
                if stop > start:
                    rows = pl.ds(row + start, stop - start)
                    first_sum[i, rows, :] = summed(i, rows)
            return 0

        if paired < first + second:
            lax.fori_loop(0, SIDE, plain, 0)

        p = position[other[axis]]
        a, b = halves(chunk)
        far, right, left = (p + 2) % SIDE, (p + 1) % SIDE, (p + SIDE - 1) % SIDE
        send_op2[a, :] = to_wire(first_sum[far, a, :], FOUR)
        copies(chunk, 6).start()
        send_op2[b, :] = to_wire(first_sum[far, b, :], FOUR)
        copies(chunk, 7).start()
        send_dir2[a, :] = to_wire(first_sum[right, a, :], FOUR)
        copies(chunk, 8).start()
        send_dir2[b, :] = to_wire(first_sum[left, b, :], FOUR)
        copies(chunk, 9).start()

    def second_forward(chunk):
        p = position[other[CHUNKS[chunk][0]]]
        a, b = halves(chunk)
        right, left = (p + 1) % SIDE, (p + SIDE - 1) % SIDE
        for number, rows, at in ((6, a, left), (7, b, right)):
            copies(chunk, number).wait_recv()
            part = from_wire(recv_op2[rows, :], FOUR) + first_sum[at, rows, :]
            send_fwd2[rows, :] = to_wire(part, EIGHT)
            copies(chunk, 4 + number).start()

    def second_finish(chunk):
        p = position[other[CHUNKS[chunk][0]]]
        for number in (8, 9, 10, 11):
            copies(chunk, number).wait_recv()
        for rows in halves(chunk):
            mean[rows, :] = (
                first_sum[p, rows, :]
                + from_wire(recv_dir2[rows, :], FOUR)
                + from_wire(recv_fwd2[rows, :], EIGHT)
            ) * (SIDE * SIDE) ** (-0.5)

    def prepare():
        loaded("given")
        for number, row, length in ((5, MIXED, 64), (1, DOWN, 256)):
            packed_param[pl.ds(row, length), :] = beside(params[number][...])
            packed_state[pl.ds(row, length), :] = beside(states[number][...])

    def row_squares(row, width, param, top, height):
        got = jnp.zeros((height, 128), jnp.float32)
        own = jnp.zeros((height, 128), jnp.float32)
        for c in range(width):
            m = mean[pl.ds(row + height * c, height), :]
            w = param[pl.ds(top, height), pl.ds(128 * c, 128)]
            got, own = got + m * m, own + w * w
        rest = [jnp.zeros((64 - height, 128), jnp.float32)] if height < 64 else []
        both = jnp.concatenate([got, *rest, own, *rest], axis=0)
        return jnp.sum(both, axis=1, keepdims=True)

    def column_squares(row, length):
        m = mean[pl.ds(row, length), :]
        w = packed_param[pl.ds(row, length), :]
        got = jnp.sum(m * m, axis=0, keepdims=True)
        own = jnp.sum(w * w, axis=0, keepdims=True)
        got, own = got + turn(got), own + turn(own)
        return jnp.where(low_lanes((1, 128)), got, own)

    def norm_copy(group, step):
        k = group * (PEERS - 1) + step - 1
        return pltpu.make_async_remote_copy(
            src_ref=squares.at[group, 0],
            dst_ref=squares.at[group, step],
            send_sem=nsend_sem.at[k],
            recv_sem=nrecv_sem.at[k],
            device_id=(replica, (model + step) % PEERS),
            device_id_type=MESH,
        )

    def norm_send(group):
        by_rows, by_columns = [], []
        if group in (0, 2):
            by_rows = [row_squares(UP + 64 * group, 4, params[0], 16 * group, 32)]
        if group == 1:
            by_rows = [row_squares(VALUE, 1, params[4], 0, 64)]
            by_columns = [column_squares(MIXED, 64)]
        if group == 3:
            by_rows = [
                row_squares(QUERY, 1, params[2], 0, 64),
                row_squares(KEY, 1, params[3], 0, 64),
            ]
        if group == 4:
            by_columns = [column_squares(DOWN, 256)]
        tile = jnp.zeros((8, 128), jnp.float32)
        if by_rows:
            lane = lax.broadcasted_iota(jnp.int32, (128, 128), 1)
            block = jnp.zeros((128, 128), jnp.float32)
            for k, column in enumerate(by_rows):
                block = jnp.where(lane == k, column, block)
            tile = block.T[0:8]
        sub = lax.broadcasted_iota(jnp.int32, (8, 128), 0)
        for k, line in enumerate(by_columns):
            tile = jnp.where(sub == len(by_rows) + k, line, tile)
        squares[group, 0] = tile
        for step in range(1, PEERS):
            norm_copy(group, step).start()

    ratios = {}

    def norm_ratios(group):
        for step in range(1, PEERS):
            norm_copy(group, step).wait_recv()
        total = squares[group, 0]
        for step in range(1, PEERS):
            total = total + squares[group, step]
        low = low_lanes((8, 128))
        back = turn(total)
        got, own = jnp.where(low, total, back), jnp.where(low, back, total)
        ratio = jnp.sqrt(own) * lax.rsqrt(got + 1e-06)
        across = ratio
        down_rows = jnp.concatenate([ratio] * 16, axis=0).T if group != 4 else None
        ratios[group] = across, down_rows

    def stepped(m, param, state):
        state_new = hold_rate * state + (1.0 - hold_rate) * m * m
        return param - learn_rate * m * lax.rsqrt(state_new + 1e-06), state_new

    def updated(rows, m, param, state):
        scaled[rows, :] = m
        gathered[z, y, rows, :] = stepped(m, param, state)[0].astype(jnp.bfloat16)

    def row_update(row, width, ratio, number, top, height):
        for c in range(width):
            rows = pl.ds(row + height * c, height)
            at = (pl.ds(top, height), pl.ds(128 * c, 128))
            updated(rows, mean[rows, :] * ratio, params[number][at], states[number][at])

    def column_update(row, length, ratio):
        rows = pl.ds(row, length)
        updated(rows, mean[rows, :] * ratio, packed_param[rows, :], packed_state[rows, :])

    def update(chunk):
        across, down_rows = ratios[CHUNKS[chunk][4]]
        if chunk in (0, 2):
            row_update(UP + 64 * chunk, 4, down_rows[0:32, 0:1], 0, 16 * chunk, 32)
        if chunk == 1:
            column_update(MIXED, 64, across[1:2])
            row_update(VALUE, 1, down_rows[0:64, 0:1], 4, 0, 64)
            small = pl.ds(SMALL, 16)
            updated(
                small,
                mean[small, :] * 2.0,
                jnp.concatenate([params[6][...], params[7][...]], axis=1),
                jnp.concatenate([states[6][...], states[7][...]], axis=1),
            )
        if chunk == 4:
            row_update(QUERY, 1, down_rows[0:64, 0:1], 2, 0, 64)
            row_update(KEY, 1, down_rows[0:64, 1:2], 3, 0, 64)
        if chunk in (3, 5):
            column_update(CHUNKS[chunk][1], 128, across[0:1])

    def keep():
        def step(number, at, m):
            following[number][at], new[number][at] = stepped(
                m, params[number][at], states[number][at]
            )

        for part in range(2):
            for c in range(4):
                at = (pl.ds(32 * part, 32), pl.ds(128 * c, 128))
                step(0, at, scaled[pl.ds(UP + 128 * part + 32 * c, 32), :])
        everything = (slice(None), slice(None))
        for number, row in ((2, QUERY), (3, KEY), (4, VALUE)):
            step(number, everything, scaled[pl.ds(row, 64), :])
        for number, row, length in ((1, DOWN, 256), (5, MIXED, 64)):
            turned = scaled[pl.ds(row, length), :].T
            step(number, everything, jnp.concatenate([turned[:64], turned[64:]], axis=1))
        line = scaled[pl.ds(SMALL, 1), :]
        step(6, everything, line[:, :64])
        step(7, everything, turn(line)[:, :64])

    def gather_copies(chunk, number):
        name, row, first, second, _ = CHUNKS[chunk]
        a, b = pl.ds(row, first), pl.ds(row + first, second)
        whole = pl.ds(row, first + second)
        up_way = number % 2 == 0
        step = 1 if up_way else SIDE - 1
        behind = SIDE - 1 if up_way else 1
        p, q = position[name], position[other[name]]
        axis = name
        rows = whole
        if number < 4:
            axis = other[name]
            if number >= 2:
                rows, q = (b if up_way else a), (q + behind) % SIDE
        else:
            block = (number - 4) // 2 % 4
            q = (q + (0, SIDE - 1, 1, 2)[block]) % SIDE
            if number >= 12:
                rows, p = (b if up_way else a), (p + behind) % SIDE
        ref = gathered.at[q, p, rows] if name == "y" else gathered.at[p, q, rows]
        k = chunk * PER_GATHER + number
        return pltpu.make_async_remote_copy(
            src_ref=ref,
            dst_ref=ref,
            send_sem=gsend_sem.at[k],
            recv_sem=grecv_sem.at[k],
            device_id=place(axis, step),
            device_id_type=MESH,
        )

    def pass_on(chunk, awaited, started):
        for number in awaited:
            gather_copies(chunk, number).wait_recv()
        for number in started:
            gather_copies(chunk, number).start()

    def widen(chunk):
        number, row, start, length = {
            1: (1, MIXED, 0, 64),
            3: (0, DOWN, 0, 128),
            5: (0, DOWN, 128, 128),
        }[chunk]
        out = wides[number]
        half = out.shape[0] // 2
        low = low_lanes((length, 128))
        rows = pl.ds(row + start, length)
        for pair in range(8):
            lanes = pl.ds(128 * pair, 128)
            zz, yy = (2 * pair) // SIDE, (2 * pair) % SIDE
            a = gathered[zz, yy, rows, :].astype(jnp.float32)
            b = gathered[zz, yy + 1, rows, :].astype(jnp.float32)
            out[pl.ds(start, length), lanes] = jnp.where(low, a, turn(b)).astype(jnp.bfloat16)
            out[pl.ds(half + start, length), lanes] = jnp.where(low, turn(a), b).astype(
                jnp.bfloat16
            )

    def small_out():
        sub = lax.broadcasted_iota(jnp.int32, (8, 128), 0)
        low = low_lanes((1, 128))
        lines = [jnp.zeros((8, 128), jnp.float32)] * 2
        for pair in range(8):
            zz, yy = (2 * pair) // SIDE, (2 * pair) % SIDE
            a = gathered[zz, yy, pl.ds(SMALL, 16), :].astype(jnp.float32)[0:1]
            b = gathered[zz, yy + 1, pl.ds(SMALL, 16), :].astype(jnp.float32)[0:1]
            lines[0] = jnp.where(sub == pair, jnp.where(low, a, turn(b)), lines[0])
            lines[1] = jnp.where(sub == pair, jnp.where(low, turn(a), b), lines[1])
        for k in range(2):
            small_halves[k][...] = lines[k].astype(jnp.bfloat16)

    def end(chunk):
        pass_on(chunk, range(12, PER_GATHER), ())
        if chunk in (1, 3, 5):
            widen(chunk)
        if chunk == 1:
            small_out()

    def act(name, k):
        if name == "send":
            send(k)
        elif name in ("fwdA", "fwdB"):
            forward(k, int(name == "fwdB"))
        elif name == "fin":
            finish(k)
        elif name == "Fwd":
            second_forward(k)
        elif name == "Fin":
            second_finish(k)
        elif name == "prepare":
            prepare()
        elif name == "keep":
            keep()
        elif name == "norm":
            norm_send(k)
        elif name == "ratio":
            norm_ratios(k)
        elif name == "upd":
            update(k)
            pass_on(k, (), (0, 1, 4, 5))
        elif name == "xf+":
            pass_on(k, (0,), (2, 6, 7))
        elif name == "xf-":
            pass_on(k, (1,), (3, 8, 9))
        elif name == "far":
            pass_on(k, (2, 3), (10, 11))
        elif name == "end":
            end(k)
        else:
            number = 4 + 2 * ("own", "l", "r", "f").index(name[:-2]) + int(name[-1] == "-")
            pass_on(k, (number,), (number + 8,))

    for name, k in ORDER:
        with stage(f"{name}_{k}"):
            act(name, k)

    with stage("sent"):
        for chunk in range(COUNT):
            for number in range(PER):
                copies(chunk, number).wait_send()
            for number in range(PER_GATHER):
                gather_copies(chunk, number).wait_send()
        for group in range(GROUPS):
            for step in range(1, PEERS):
                norm_copy(group, step).wait_send()


def output_kernel(*refs):
    gathered, laid, refs = refs[0], refs[1:21], refs[21:]
    half, rest, sem = refs[:8], refs[8:24], refs[24]
    pairs = []
    for part in range(2):
        for c in range(4):
            pairs.append(
                (
                    gathered.at[:, pl.ds(UP + 128 * part + 32 * c, 32), :],
                    half[0].at[:, pl.ds(32 * part, 32), pl.ds(128 * c, 128)],
                )
            )
    pairs.append((laid[0], half[1]))
    for number, row in ((2, QUERY), (3, KEY), (4, VALUE)):
        pairs.append((gathered.at[:, pl.ds(row, 64), :], half[number]))
    pairs += zip(laid[1:4], half[5:])
    pairs += zip(laid[4:], rest)
    started = [pltpu.make_async_copy(*pair, sem.at[k]) for k, pair in enumerate(pairs)]
    for copy in started:
        copy.start()
    for copy in started:
        copy.wait()


def stay(*arrays):
    return [pltpu.with_memory_space_constraint(a, pltpu.HBM) for a in arrays]


def local(*arrays):
    slopes, params, states = arrays[:8], arrays[8:16], arrays[16:]
    up, down, query, key, value, mixed, norm, bias = slopes

    def shown(group):
        up, down, query, key, value, mixed, norm, bias = group
        return up, down.T, query, key, value, mixed.T, norm[None], bias[None]

    params, states = shown(params), shown(states)
    vmem = pl.BlockSpec(memory_space=pltpu.VMEM)
    anywhere = pl.BlockSpec(memory_space=pl.ANY)
    f32, bf16 = jnp.float32, jnp.bfloat16
    wire = pltpu.VMEM((SIDE, ROWS, 128), bf16)
    wire2 = pltpu.VMEM((ROWS, 128), bf16)
    dma = pltpu.SemaphoreType.DMA
    held = [pltpu.VMEM(a.shape, f32) for a in params]
    gathered, *laid = pl.pallas_call(
        exchange_kernel,
        out_shape=(
            pltpu.VMEM((SIDE, SIDE, ROWS, 128), bf16),
            pltpu.VMEM((512, 1024), bf16),
            pltpu.VMEM((128, 1024), bf16),
            pltpu.VMEM((8, 128), bf16),
            pltpu.VMEM((8, 128), bf16),
            *held,
            *held,
        ),
        in_specs=[pl.BlockSpec(memory_space=pltpu.HBM)] * 24,
        out_specs=(vmem,) * 21,
        scratch_shapes=[
            *held,
            *held,
            pltpu.VMEM((ROWS, 128), f32),
            pltpu.VMEM((SIDE, SIDE, ROWS, 128), f32),
            pltpu.VMEM((1, 1024), f32),
            pltpu.VMEM((1, 1024), f32),
            pltpu.VMEM((ROWS, 128), f32),
            pltpu.VMEM((ROWS, 128), f32),
            *[wire] * 6,
            pltpu.VMEM((SIDE, ROWS, 128), f32),
            *[wire2] * 6,
            pltpu.VMEM((ROWS, 128), f32),
            pltpu.VMEM((GROUPS, PEERS, 8, 128), f32),
            dma((LOADS,)),
            dma((COUNT * PER,)),
            dma((COUNT * PER,)),
            dma((COUNT * PER_GATHER,)),
            dma((COUNT * PER_GATHER,)),
            dma((GROUPS * (PEERS - 1),)),
            dma((GROUPS * (PEERS - 1),)),
        ],
        compiler_params=pltpu.CompilerParams(
            collective_id=0, has_side_effects=True, vmem_limit_bytes=40 * 2**20
        ),
        name="exchange",
    )(
        *stay(
            up.reshape(SIDE, SIDE, 64, 512),
            down.reshape(2, 256, 1024),
            query.reshape(SIDE, SIDE, 64, 128),
            key.reshape(SIDE, SIDE, 64, 128),
            value.reshape(SIDE, SIDE, 64, 128),
            mixed.reshape(2, 64, 1024),
            norm,
            bias,
            *params,
            *states,
        )
    )
    own = [jax.ShapeDtypeStruct(a.shape, f32) for a in params]
    full = [
        jax.ShapeDtypeStruct(s, bf16)
        for s in (
            (16, 64, 512),
            (512, 1024),
            (16, 64, 128),
            (16, 64, 128),
            (16, 64, 128),
            (128, 1024),
            (8, 128),
            (8, 128),
        )
    ]
    out = pl.pallas_call(
        output_kernel,
        out_shape=(*full, *own, *own),
        in_specs=[vmem] * 21,
        out_specs=(anywhere,) * 24,
        scratch_shapes=[dma((8 + 1 + 3 + 3 + 16,))],
        compiler_params=pltpu.CompilerParams(vmem_limit_bytes=8 * 2**20),
        name="outputs",
    )(gathered.reshape(SIDE * SIDE, ROWS, 128), *laid)
    half, following, new = out[:8], out[8:16], out[16:]
    half_up, half_down, half_query, half_key, half_value, half_mixed, half_norm, half_bias = half

    def back(group):
        up, down, query, key, value, mixed, norm, bias = group
        return up, down.T, query, key, value, mixed.T, norm[0], bias[0]

    return (
        half_up.reshape(1024, 512),
        half_down,
        half_query.reshape(1024, 128),
        half_key.reshape(1024, 128),
        half_value.reshape(1024, 128),
        half_mixed,
        half_norm.reshape(1024),
        half_bias.reshape(1024),
        *back(following),
        *back(new),
    )


def solution(mesh):
    def along(split):
        return [
            P(*(("replica", "model") if dim == 0 else ("model", "replica"))[:2])
            if dim < 2
            else P("replica")
            for dim in split
        ]

    shards = along((0, 1, 0, 0, 0, 1, 2, 2))
    slopes = [P("replica", None, "model"), P("replica", "model", None)]
    slopes = [slopes[k] for k in (0, 1, 0, 0, 0, 1)] + [P("replica", None)] * 2
    halves = [P(None, "model"), P("model", None)]
    halves = [halves[k] for k in (0, 1, 0, 0, 0, 1)] + [P()] * 2
    return jax.shard_map(
        local,
        mesh=mesh,
        in_specs=(*slopes, *shards, *shards),
        out_specs=(*halves, *shards, *shards),
        check_vma=False,
    )
```

time: 68.5 us -> 62 us (0.905)
  Pallas kernels: 67.4 us -> 61.2 us
    pallas_call x1, Pallas kernels: 63.2 us -> 59 us  [local(): pl.pallas_call(exchange_kernel, out_shape=(pltpu.VMEM((SIDE, SIDE, ROWS,...]
    pallas_call x1, Pallas kernels: 4.22 us -> 2.26 us  [local(): pl.pallas_call(output_kernel, out_shape=(*full, *own, *own), in_specs=[vm...]
where the time goes in v3:
time: 62 us; the launch traced here: 61.9 us
  Pallas kernels  61.2 us (99%)
  between operations  0.68 us (1%)
    pallas_call x1, Pallas kernels, local(): pl.pallas_call(exchange_kernel, out_shape=(pltpu.VMEM((SIDE, SIDE, ROWS,...  59 us
    pallas_call x1, Pallas kernels, local(): pl.pallas_call(output_kernel, out_shape=(*full, *own, *own), in_specs=[vm...  2.26 us

profile of v3, /device:TPU:0, one launch (start us, length us, event | category | flops | bytes accessed | tf_op | source)
XLA Modules:
  0.0 61.9 jit_solution(1618515531874586655)
XLA Ops:
  0.7 59.0 %exchange.1 = (bf16[4,4,784,128]{3,2,1,0:T(8,128)(2,1)S(1)}, bf16[512,1024]{1,0:T(8,128)(2,1)S(1)}, bf16[128,1024]{1,0:T(8,128)(2,1)S(1)}, bf16[8,128]{1,0:T(8,1...) custom-call(f32[4,4,64,512]{3,2,1,0:T(8,128)} %bitcast.30, ...), custom_call_target="tpu_custom_call" | custom-call | tf_op jit(solution)/shard_map/exchange/pallas_call | solution.py:688
  59.7 2.3 %outputs.1 = (bf16[16,64,512]{2,1,0:T(8,128)(2,1)}, bf16[512,1024]{1,0:T(8,128)(2,1)}, bf16[16,64,128]{2,1,0:T(8,128)(2,1)}, bf16[16,64,128]{2,1,0:T(8,128)(2,1)...) custom-call(bf16[16,784,128]{2,1,0:T(8,128)(2,1)S(1)} %bitcast.29, ...), custom_call_target="tpu_custom_call" | custom-call | tf_op jit(solution)/shard_map/outputs/pallas_call | solution.py:755

commit v4 on v3

--- a/solution.py
+++ b/solution.py
@@ -26,29 +26,31 @@
 )
 COUNT = len(CHUNKS)
 GROUPS = 5
-PER = 12
-PER_GATHER = 20
-LOADS = 8 + 16 + 8 + 3 + 2 + 16
+PER = 5
+PER_GATHER = 12
+LOADS = COUNT + 8
+SENDS = 9
 
 ORDER = (
-    ("send", 0), ("send", 1), ("send", 3), ("send", 5), ("send", 4), ("send", 2), ("fwdB", 0),
-    ("fwdA", 0), ("fwdA", 1), ("fwdB", 1), ("fwdA", 4), ("fwdB", 4), ("fwdB", 3), ("fwdA", 3),
-    ("fwdB", 2), ("fwdA", 2), ("fwdB", 5), ("fwdA", 5), ("prepare", 0), ("fin", 0), ("fin", 1),
-    ("fin", 4), ("fin", 3), ("fin", 2), ("Fwd", 1), ("fin", 5), ("Fwd", 0), ("Fwd", 4), ("Fwd", 3),
-    ("Fwd", 2), ("Fin", 1), ("norm", 1), ("Fwd", 5), ("Fin", 0), ("norm", 0), ("Fin", 4),
-    ("norm", 3), ("Fin", 3), ("Fin", 2), ("norm", 2), ("Fin", 5), ("norm", 4), ("ratio", 1),
-    ("upd", 1), ("ratio", 0), ("upd", 0), ("ratio", 3), ("upd", 4), ("ratio", 2), ("upd", 2),
-    ("ratio", 4), ("upd", 3), ("xf-", 1), ("upd", 5), ("keep", 0), ("ownF+", 1), ("xf+", 1),
-    ("ownF-", 1), ("ownF-", 0), ("xf-", 0), ("ownF+", 0), ("xf+", 0), ("ownF+", 4), ("ownF-", 4),
-    ("xf-", 4), ("xf+", 4), ("xf+", 2), ("ownF+", 2), ("xf-", 2), ("ownF-", 2), ("ownF+", 3),
-    ("xf+", 3), ("ownF-", 3), ("xf-", 3), ("xf+", 5), ("rF-", 1), ("rF+", 1), ("xf-", 5),
-    ("far", 1), ("ownF+", 5), ("ownF-", 5), ("rF+", 0), ("rF-", 0), ("lF-", 1), ("lF+", 1),
-    ("lF+", 0), ("lF-", 0), ("far", 0), ("far", 4), ("far", 2), ("rF+", 4), ("rF-", 4), ("lF-", 3),
-    ("lF-", 4), ("lF+", 4), ("lF+", 3), ("lF+", 2), ("lF-", 2), ("rF+", 3), ("rF-", 3), ("rF-", 2),
-    ("lF-", 5), ("lF+", 5), ("rF+", 2), ("far", 3), ("far", 5), ("rF+", 5), ("rF-", 5), ("fF+", 1),
-    ("fF-", 1), ("fF-", 0), ("fF+", 0), ("fF-", 4), ("fF+", 4), ("fF-", 2), ("fF+", 2), ("fF-", 3),
-    ("fF+", 3), ("fF+", 5), ("fF-", 5), ("end", 1), ("end", 0), ("end", 4), ("end", 2), ("end", 3),
-    ("end", 5),
+    ("so", 0), ("so", 1), ("so", 2), ("so", 4), ("so", 5), ("sd", 1), ("fwdA", 0), ("sd", 2),
+    ("fwdA", 1), ("fwdB", 1), ("so", 3), ("fwdA", 2), ("fwdA", 5), ("fwdB", 2), ("fwdB", 5),
+    ("sd", 5), ("fwdB", 0), ("sd", 3), ("fin", 1), ("prepare", 0), ("sd", 0), ("fwdA", 3),
+    ("Fwd", 1), ("sd", 4), ("fwdB", 3), ("fwdB", 4), ("fwdA", 4), ("fin", 0), ("fin", 2),
+    ("Fin", 1), ("norm", 1), ("fin", 5), ("fin", 3), ("Fwd", 0), ("Fwd", 2), ("fin", 4),
+    ("Fwd", 5), ("Fwd", 3), ("Fin", 0), ("norm", 0), ("ratio", 1), ("Fin", 2), ("upd", 1),
+    ("norm", 2), ("Fwd", 4), ("Fin", 5), ("Fin", 3), ("norm", 4), ("xf-", 1), ("Fin", 4),
+    ("xf+", 1), ("norm", 3), ("ratio", 0), ("upd", 0), ("ratio", 2), ("upd", 2), ("ratio", 4),
+    ("upd", 5), ("upd", 3), ("far", 1), ("xf+", 0), ("xf+", 2), ("xf-", 2), ("ratio", 3),
+    ("xf-", 0), ("xf-", 5), ("upd", 4), ("xf+", 5), ("rF-", 1), ("xf-", 3), ("ownF+", 5),
+    ("far", 0), ("xf+", 3), ("ownF+", 2), ("far", 2), ("xf-", 4), ("xf+", 4), ("lF+", 0),
+    ("rF+", 2), ("rF+", 1), ("lF-", 5), ("ownF-", 3), ("far", 5), ("lF-", 0), ("rF-", 2),
+    ("lF+", 1), ("ownF-", 1), ("far", 3), ("ownF-", 0), ("rF+", 3), ("fF-", 1), ("fF+", 1),
+    ("far", 4), ("fF+", 0), ("lF+", 2), ("rF+", 5), ("lF-", 1), ("ownF+", 0), ("keep", 0),
+    ("ownF-", 2), ("ownF+", 1), ("ownF-", 4), ("lF-", 3), ("rF-", 5), ("lF+", 3), ("ownF+", 3),
+    ("rF-", 4), ("fF-", 2), ("lF-", 2), ("rF+", 0), ("rF-", 3), ("ownF+", 4), ("fF+", 5),
+    ("ownF-", 5), ("lF+", 4), ("lF+", 5), ("rF+", 4), ("fF-", 0), ("fF+", 2), ("rF-", 0),
+    ("fF-", 5), ("fF-", 3), ("fF+", 3), ("lF-", 4), ("fF+", 4), ("fF-", 4), ("end", 1), ("end", 0),
+    ("end", 5), ("end", 3), ("end", 2), ("end", 4),
 )
 
 
@@ -126,26 +128,24 @@
     send_dir,
     send_fwd,
     recv_op,
-    recv_dir,
-    recv_fwd,
+    both,
     first_sum,
     send_op2,
     send_dir2,
     send_fwd2,
     recv_op2,
-    recv_dir2,
-    recv_fwd2,
+    both2,
     mean,
     squares,
     load_sem,
     send_sem,
     recv_sem,
-    gsend_sem,
     grecv_sem,
-    nsend_sem,
     nrecv_sem,
 ):
     up, down, query, key, value, mixed, norm, bias = slopes
+    recv_rest = recv_dir, recv_fwd = both.at[0], both.at[1]
+    recv_rest2 = recv_dir2, recv_fwd2 = both2.at[0], both2.at[1]
     replica = lax.axis_index("replica")
     model = lax.axis_index("model")
     z, y = replica // SIDE, replica % SIDE
@@ -158,20 +158,20 @@
     position = {"y": y, "z": z}
     other = {"y": "z", "z": "y"}
 
-    loads = {}
-    count = [0]
-
-    def load(name, pairs):
-        loads[name] = []
+    def all_of(ref, sem):
+        pltpu.make_async_copy(ref, ref, sem).wait()
+
+    def load(number, pairs):
         for src, dst in pairs:
-            copy = pltpu.make_async_copy(src, dst, load_sem.at[count[0]])
-            count[0] += 1
-            copy.start()
-            loads[name].append(copy)
-
-    def loaded(name):
-        for copy in loads.pop(name, ()):
-            copy.wait()
+            pltpu.make_async_copy(src, dst, load_sem.at[number]).start()
+
+    def loaded(number, *refs):
+        for k, ref in enumerate(refs):
+            all_of(ref, load_sem.at[number + k])
+
+    def whole(chunk):
+        _, row, first, second, _ = CHUNKS[chunk]
+        return pl.ds(row, first + second)
 
     def up_part(part):
         return [
@@ -197,15 +197,19 @@
         [
             *columns(mixed, MIXED, 0, 64),
             (value, mine.at[:, :, pl.ds(VALUE, 64), :]),
-            (norm, raw_norm),
-            (bias, raw_bias),
         ],
     )
+    load(COUNT, [(norm, raw_norm)])
+    load(COUNT + 1, [(bias, raw_bias)])
     load(3, columns(down, DOWN, 0, 128))
     load(2, up_part(1))
     load(4, [(query, mine.at[:, :, pl.ds(QUERY, 64), :]), (key, mine.at[:, :, pl.ds(KEY, 64), :])])
     load(5, columns(down, DOWN, 128, 128))
-    load("given", zip(given, (*params, *states)))
+    held = [*zip(given, (*params, *states))]
+    load(COUNT + 2, [held[k] for k in (0, 1, 8, 9)])
+    load(COUNT + 3, [held[k] for k in (2, 3, 4, 5, 10, 11, 12, 13)])
+    for k, pair in enumerate((held[6], held[7], held[14], held[15])):
+        load(COUNT + 4 + k, [pair])
 
     barrier = pltpu.get_barrier_semaphore()
     for axis in ("y", "z"):
@@ -243,35 +247,38 @@
     def copies(chunk, number):
         axis = CHUNKS[chunk][0]
         a, b = halves(chunk)
-        if number >= 6:
+        second = number >= 6
+        if second:
             axis = other[axis]
-            bufs = ((send_op2, recv_op2), (send_dir2, recv_dir2), (send_fwd2, recv_fwd2))
+            sources, targets = (send_op2, send_dir2, send_fwd2), (recv_op2, *recv_rest2)
             a, b = (a, slice(None)), (b, slice(None))
         else:
-            bufs = ((send_op, recv_op), (send_dir, recv_dir), (send_fwd, recv_fwd))
+            sources, targets = (send_op, send_dir, send_fwd), (recv_op, *recv_rest)
             a, b = (slice(None), a, slice(None)), (slice(None), b, slice(None))
         kind, half = divmod(number % 6, 2)
-        src, dst = bufs[kind]
         rows = b if half else a
         step = (SIDE - 1, 1)[half] if kind != 1 else (1, SIDE - 1)[half]
-        k = chunk * PER + number
+        arrival = (3 if second else half) if kind == 0 else (4 if second else 2)
         return pltpu.make_async_remote_copy(
-            src_ref=src.at[rows],
-            dst_ref=dst.at[rows],
-            send_sem=send_sem.at[k],
-            recv_sem=recv_sem.at[k],
+            src_ref=sources[kind].at[rows],
+            dst_ref=targets[kind].at[rows],
+            send_sem=send_sem.at[3 * second + kind],
+            recv_sem=recv_sem.at[chunk * PER + arrival],
             device_id=place(axis, step),
             device_id_type=MESH,
         )
 
     def send(chunk):
-        loaded(chunk)
         if chunk == 1:
+            loaded(chunk, mine.at[:, :, pl.ds(MIXED, 128)])
+            loaded(COUNT, raw_norm, raw_bias)
             pack_small()
+        else:
+            loaded(chunk, mine.at[:, :, whole(chunk)])
         axis = CHUNKS[chunk][0]
         p = position[axis]
         a, b = halves(chunk)
-        far, right, left = (p + 2) % SIDE, (p + 1) % SIDE, (p + SIDE - 1) % SIDE
+        far = (p + 2) % SIDE
 
         def op(i, _):
             send_op[i, a, :] = to_wire(share(axis, far, i)[a, :], ONE)
@@ -285,6 +292,12 @@
         copies(chunk, 0).start()
         copies(chunk, 1).start()
 
+    def send_direct(chunk):
+        axis = CHUNKS[chunk][0]
+        p = position[axis]
+        a, b = halves(chunk)
+        right, left = (p + 1) % SIDE, (p + SIDE - 1) % SIDE
+
         def direct(i, _):
             send_dir[i, a, :] = to_wire(share(axis, right, i)[a, :], ONE)
             send_dir[i, b, :] = to_wire(share(axis, left, i)[b, :], ONE)
@@ -311,8 +324,7 @@
     def finish(chunk):
         axis, row, first, second, _ = CHUNKS[chunk]
         p = position[axis]
-        for number in (2, 3, 4, 5):
-            copies(chunk, number).wait_recv()
+        all_of(both.at[:, :, whole(chunk)], recv_sem.at[chunk * PER + 2])
 
         def summed(i, rows):
             return (
@@ -361,16 +373,15 @@
         p = position[other[CHUNKS[chunk][0]]]
         a, b = halves(chunk)
         right, left = (p + 1) % SIDE, (p + SIDE - 1) % SIDE
+        all_of(recv_op2.at[whole(chunk)], recv_sem.at[chunk * PER + 3])
         for number, rows, at in ((6, a, left), (7, b, right)):
-            copies(chunk, number).wait_recv()
             part = from_wire(recv_op2[rows, :], FOUR) + first_sum[at, rows, :]
             send_fwd2[rows, :] = to_wire(part, EIGHT)
             copies(chunk, 4 + number).start()
 
     def second_finish(chunk):
         p = position[other[CHUNKS[chunk][0]]]
-        for number in (8, 9, 10, 11):
-            copies(chunk, number).wait_recv()
+        all_of(both2.at[:, whole(chunk)], recv_sem.at[chunk * PER + 4])
         for rows in halves(chunk):
             mean[rows, :] = (
                 first_sum[p, rows, :]
@@ -379,7 +390,8 @@
             ) * (SIDE * SIDE) ** (-0.5)
 
     def prepare():
-        loaded("given")
+        loaded(COUNT + 2, first_sum.at[0:2, 0:512], mean.at[0:512])
+        loaded(COUNT + 4, params[6], params[7], states[6], states[7])
         for number, row, length in ((5, MIXED, 64), (1, DOWN, 256)):
             packed_param[pl.ds(row, length), :] = beside(params[number][...])
             packed_state[pl.ds(row, length), :] = beside(states[number][...])
@@ -404,12 +416,11 @@
         return jnp.where(low_lanes((1, 128)), got, own)
 
     def norm_copy(group, step):
-        k = group * (PEERS - 1) + step - 1
         return pltpu.make_async_remote_copy(
             src_ref=squares.at[group, 0],
             dst_ref=squares.at[group, step],
-            send_sem=nsend_sem.at[k],
-            recv_sem=nrecv_sem.at[k],
+            send_sem=send_sem.at[8],
+            recv_sem=nrecv_sem.at[group],
             device_id=(replica, (model + step) % PEERS),
             device_id_type=MESH,
         )
@@ -445,8 +456,7 @@
     ratios = {}
 
     def norm_ratios(group):
-        for step in range(1, PEERS):
-            norm_copy(group, step).wait_recv()
+        all_of(squares.at[group, 1:PEERS], nrecv_sem.at[group])
         total = squares[group, 0]
         for step in range(1, PEERS):
             total = total + squares[group, step]
@@ -519,13 +529,12 @@
     def gather_copies(chunk, number):
         name, row, first, second, _ = CHUNKS[chunk]
         a, b = pl.ds(row, first), pl.ds(row + first, second)
-        whole = pl.ds(row, first + second)
         up_way = number % 2 == 0
         step = 1 if up_way else SIDE - 1
         behind = SIDE - 1 if up_way else 1
         p, q = position[name], position[other[name]]
         axis = name
-        rows = whole
+        rows = whole(chunk)
         if number < 4:
             axis = other[name]
             if number >= 2:
@@ -536,12 +545,12 @@
             if number >= 12:
                 rows, p = (b if up_way else a), (p + behind) % SIDE
         ref = gathered.at[q, p, rows] if name == "y" else gathered.at[p, q, rows]
-        k = chunk * PER_GATHER + number
+        arrival = min(number, 2) if number < 4 else min(number - 1, 11)
         return pltpu.make_async_remote_copy(
             src_ref=ref,
             dst_ref=ref,
-            send_sem=gsend_sem.at[k],
-            recv_sem=grecv_sem.at[k],
+            send_sem=send_sem.at[6 if number < 4 else 7],
+            recv_sem=grecv_sem.at[chunk * PER_GATHER + arrival],
             device_id=place(axis, step),
             device_id_type=MESH,
         )
@@ -586,15 +595,17 @@
             small_halves[k][...] = lines[k].astype(jnp.bfloat16)
 
     def end(chunk):
-        pass_on(chunk, range(12, PER_GATHER), ())
+        all_of(gathered.at[0, :, whole(chunk)], grecv_sem.at[chunk * PER_GATHER + 11])
         if chunk in (1, 3, 5):
             widen(chunk)
         if chunk == 1:
             small_out()
 
     def act(name, k):
-        if name == "send":
+        if name == "so":
             send(k)
+        elif name == "sd":
+            send_direct(k)
         elif name in ("fwdA", "fwdB"):
             forward(k, int(name == "fwdB"))
         elif name == "fin":
@@ -619,7 +630,8 @@
         elif name == "xf-":
             pass_on(k, (1,), (3, 8, 9))
         elif name == "far":
-            pass_on(k, (2, 3), (10, 11))
+            all_of(gathered.at[0, 0, whole(k)], grecv_sem.at[k * PER_GATHER + 2])
+            pass_on(k, (), (10, 11))
         elif name == "end":
             end(k)
         else:
@@ -631,14 +643,11 @@
             act(name, k)
 
     with stage("sent"):
-        for chunk in range(COUNT):
-            for number in range(PER):
-                copies(chunk, number).wait_send()
-            for number in range(PER_GATHER):
-                gather_copies(chunk, number).wait_send()
-        for group in range(GROUPS):
-            for step in range(1, PEERS):
-                norm_copy(group, step).wait_send()
+        for k, ref in enumerate((send_op, send_dir, send_fwd, send_op2, send_dir2, send_fwd2)):
+            all_of(ref, send_sem.at[k])
+        all_of(gathered.at[0, 0:3], send_sem.at[6])
+        all_of(gathered.at[0:3], send_sem.at[7])
+        all_of(squares.at[:, 1:PEERS], send_sem.at[8])
 
 
 def output_kernel(*refs):
@@ -707,18 +716,18 @@
             pltpu.VMEM((1, 1024), f32),
             pltpu.VMEM((ROWS, 128), f32),
             pltpu.VMEM((ROWS, 128), f32),
-            *[wire] * 6,
+            *[wire] * 4,
+            pltpu.VMEM((2, SIDE, ROWS, 128), bf16),
             pltpu.VMEM((SIDE, ROWS, 128), f32),
-            *[wire2] * 6,
+            *[wire2] * 4,
+            pltpu.VMEM((2, ROWS, 128), bf16),
             pltpu.VMEM((ROWS, 128), f32),
             pltpu.VMEM((GROUPS, PEERS, 8, 128), f32),
             dma((LOADS,)),
-            dma((COUNT * PER,)),
+            dma((SENDS,)),
             dma((COUNT * PER,)),
             dma((COUNT * PER_GATHER,)),
-            dma((COUNT * PER_GATHER,)),
-            dma((GROUPS * (PEERS - 1),)),
-            dma((GROUPS * (PEERS - 1),)),
+            dma((GROUPS,)),
         ],
         compiler_params=pltpu.CompilerParams(
             collective_id=0, has_side_effects=True, vmem_limit_bytes=40 * 2**20

time: 62 us -> 58.1 us (0.937)
  Pallas kernels: 61.2 us -> 57.2 us
    pallas_call x1, Pallas kernels: 59 us -> 55 us  [local(): pl.pallas_call(exchange_kernel, out_shape=(pltpu.VMEM((SIDE, SIDE, ROWS,...]
where the time goes in v4:
time: 58.1 us; the launch traced here: 57.9 us
  Pallas kernels  57.2 us (98%)
  between operations  0.68 us (1%)
    pallas_call x1, Pallas kernels, local(): pl.pallas_call(exchange_kernel, out_shape=(pltpu.VMEM((SIDE, SIDE, ROWS,...  55 us
    pallas_call x1, Pallas kernels, local(): pl.pallas_call(output_kernel, out_shape=(*full, *own, *own), in_specs=[vm...  2.26 us

profile of v4, /device:TPU:0, one launch (start us, length us, event | category | flops | bytes accessed | tf_op | source)
XLA Modules:
  0.0 57.9 jit_solution(4014148651296107597)
XLA Ops:
  0.7 55.0 %exchange.1 = (bf16[4,4,784,128]{3,2,1,0:T(8,128)(2,1)S(1)}, bf16[512,1024]{1,0:T(8,128)(2,1)S(1)}, bf16[128,1024]{1,0:T(8,128)(2,1)S(1)}, bf16[8,128]{1,0:T(8,1...) custom-call(f32[4,4,64,512]{3,2,1,0:T(8,128)} %bitcast.30, ...), custom_call_target="tpu_custom_call" | custom-call | tf_op jit(solution)/shard_map/exchange/pallas_call | solution.py:697
  55.6 2.3 %outputs.1 = (bf16[16,64,512]{2,1,0:T(8,128)(2,1)}, bf16[512,1024]{1,0:T(8,128)(2,1)}, bf16[16,64,128]{2,1,0:T(8,128)(2,1)}, bf16[16,64,128]{2,1,0:T(8,128)(2,1)...) custom-call(bf16[16,784,128]{2,1,0:T(8,128)(2,1)S(1)} %bitcast.29, ...), custom_call_target="tpu_custom_call" | custom-call | tf_op jit(solution)/shard_map/outputs/pallas_call | solution.py:764

commit v5 on v4

--- a/solution.py
+++ b/solution.py
@@ -17,6 +17,18 @@
 UP, QUERY, KEY, MIXED, VALUE, SMALL, DOWN, ROWS = 0, 256, 320, 384, 448, 512, 528, 784
 
 CHUNKS = (
+    ("y", UP, 32, 32),
+    ("z", MIXED, 80, 64),
+    ("y", UP + 64, 32, 32),
+    ("y", UP + 128, 32, 32),
+    ("z", DOWN, 32, 32),
+    ("y", UP + 192, 32, 32),
+    ("z", DOWN + 64, 32, 32),
+    ("y", QUERY, 64, 64),
+    ("z", DOWN + 128, 32, 32),
+    ("z", DOWN + 192, 32, 32),
+)
+GATHERS = (
     ("y", UP, 64, 64, 0),
     ("z", MIXED, 80, 64, 1),
     ("y", UP + 128, 64, 64, 2),
@@ -26,31 +38,42 @@
 )
 COUNT = len(CHUNKS)
 GROUPS = 5
-PER = 5
+PER = 8
 PER_GATHER = 12
 LOADS = COUNT + 8
 SENDS = 9
 
 ORDER = (
-    ("so", 0), ("so", 1), ("so", 2), ("so", 4), ("so", 5), ("sd", 1), ("fwdA", 0), ("sd", 2),
-    ("fwdA", 1), ("fwdB", 1), ("so", 3), ("fwdA", 2), ("fwdA", 5), ("fwdB", 2), ("fwdB", 5),
-    ("sd", 5), ("fwdB", 0), ("sd", 3), ("fin", 1), ("prepare", 0), ("sd", 0), ("fwdA", 3),
-    ("Fwd", 1), ("sd", 4), ("fwdB", 3), ("fwdB", 4), ("fwdA", 4), ("fin", 0), ("fin", 2),
-    ("Fin", 1), ("norm", 1), ("fin", 5), ("fin", 3), ("Fwd", 0), ("Fwd", 2), ("fin", 4),
-    ("Fwd", 5), ("Fwd", 3), ("Fin", 0), ("norm", 0), ("ratio", 1), ("Fin", 2), ("upd", 1),
-    ("norm", 2), ("Fwd", 4), ("Fin", 5), ("Fin", 3), ("norm", 4), ("xf-", 1), ("Fin", 4),
-    ("xf+", 1), ("norm", 3), ("ratio", 0), ("upd", 0), ("ratio", 2), ("upd", 2), ("ratio", 4),
-    ("upd", 5), ("upd", 3), ("far", 1), ("xf+", 0), ("xf+", 2), ("xf-", 2), ("ratio", 3),
-    ("xf-", 0), ("xf-", 5), ("upd", 4), ("xf+", 5), ("rF-", 1), ("xf-", 3), ("ownF+", 5),
-    ("far", 0), ("xf+", 3), ("ownF+", 2), ("far", 2), ("xf-", 4), ("xf+", 4), ("lF+", 0),
-    ("rF+", 2), ("rF+", 1), ("lF-", 5), ("ownF-", 3), ("far", 5), ("lF-", 0), ("rF-", 2),
-    ("lF+", 1), ("ownF-", 1), ("far", 3), ("ownF-", 0), ("rF+", 3), ("fF-", 1), ("fF+", 1),
-    ("far", 4), ("fF+", 0), ("lF+", 2), ("rF+", 5), ("lF-", 1), ("ownF+", 0), ("keep", 0),
-    ("ownF-", 2), ("ownF+", 1), ("ownF-", 4), ("lF-", 3), ("rF-", 5), ("lF+", 3), ("ownF+", 3),
-    ("rF-", 4), ("fF-", 2), ("lF-", 2), ("rF+", 0), ("rF-", 3), ("ownF+", 4), ("fF+", 5),
-    ("ownF-", 5), ("lF+", 4), ("lF+", 5), ("rF+", 4), ("fF-", 0), ("fF+", 2), ("rF-", 0),
-    ("fF-", 5), ("fF-", 3), ("fF+", 3), ("lF-", 4), ("fF+", 4), ("fF-", 4), ("end", 1), ("end", 0),
-    ("end", 5), ("end", 3), ("end", 2), ("end", 4),
+    ("soF", 0), ("sdF", 0), ("soF", 1), ("sdF", 1), ("soO", 2), ("soF", 4), ("soF", 7), ("sdF", 7),
+    ("soF", 3), ("soO", 1), ("sdO", 1), ("soO", 7), ("soF", 2), ("sdF", 2), ("fwdBF", 1),
+    ("fwdAF", 1), ("soF", 5), ("fwdBF", 7), ("soF", 8), ("sdF", 4), ("fwdAF", 7), ("soF", 9),
+    ("sdO", 7), ("soF", 6), ("fwdBO", 2), ("soO", 8), ("soO", 0), ("fwdAO", 1), ("fwdAF", 3),
+    ("fwdBO", 1), ("soO", 9), ("fwdBF", 0), ("fwdAF", 0), ("finF", 1), ("fwdAO", 7), ("sdF", 9),
+    ("fwdBF", 4), ("fwdAF", 8), ("fwdBO", 7), ("finF", 7), ("soO", 4), ("fwdBF", 2), ("fwdAF", 2),
+    ("fwdBF", 9), ("prepare", 0), ("soO", 3), ("fwdAF", 4), ("soO", 6), ("sdF", 8), ("soO", 5),
+    ("fwdBF", 6), ("fwdAF", 9), ("sdF", 6), ("fwdAO", 2), ("fwdBF", 3), ("finO", 1), ("Fwd", 1),
+    ("sdF", 3), ("fwdBF", 8), ("sdF", 5), ("fwdAF", 6), ("fwdBF", 5), ("finO", 7), ("fwdAF", 5),
+    ("fwdAO", 0), ("sdO", 0), ("sdO", 2), ("fwdBO", 0), ("Fwd", 7), ("fwdBO", 8), ("sdO", 9),
+    ("fwdBO", 5), ("finF", 0), ("finF", 2), ("fwdAO", 3), ("fwdBO", 4), ("fwdBO", 9), ("fwdAO", 4),
+    ("fwdBO", 3), ("fwdAO", 9), ("fwdAO", 6), ("fwdBO", 6), ("sdO", 6), ("finF", 4), ("sdO", 4),
+    ("sdO", 8), ("Fin", 1), ("norm", 1), ("finF", 6), ("finF", 9), ("fwdAO", 8), ("finF", 8),
+    ("Fin", 7), ("sdO", 3), ("norm", 3), ("fwdAO", 5), ("finF", 3), ("finF", 5), ("sdO", 5),
+    ("finO", 2), ("Fwd", 2), ("finO", 0), ("Fwd", 0), ("finO", 9), ("Fwd", 9), ("finO", 6),
+    ("Fwd", 6), ("finO", 4), ("Fwd", 4), ("finO", 3), ("finO", 8), ("Fwd", 8), ("finO", 5),
+    ("Fwd", 5), ("Fwd", 3), ("ratio", 1), ("upd", 1), ("Fin", 0), ("Fin", 2), ("norm", 0),
+    ("Fin", 9), ("ratio", 3), ("upd", 4), ("Fin", 4), ("Fin", 6), ("Fin", 8), ("norm", 4),
+    ("Fin", 3), ("Fin", 5), ("norm", 2), ("ownF+", 1), ("xf-", 1), ("xf+", 1), ("ownF+", 4),
+    ("ownF-", 4), ("xf+", 4), ("ownF-", 1), ("xf-", 4), ("ratio", 0), ("upd", 0), ("far", 1),
+    ("ratio", 4), ("upd", 3), ("ratio", 2), ("upd", 2), ("lF-", 1), ("upd", 5), ("keep", 0),
+    ("xf+", 0), ("xf-", 0), ("rF+", 1), ("xf+", 3), ("xf-", 3), ("xf+", 2), ("xf-", 2), ("xf-", 5),
+    ("xf+", 5), ("lF+", 0), ("far", 4), ("lF-", 4), ("far", 0), ("far", 3), ("lF+", 1), ("rF+", 0),
+    ("rF-", 1), ("far", 2), ("lF-", 0), ("lF+", 4), ("fF-", 1), ("fF+", 1), ("far", 5), ("lF+", 3),
+    ("rF+", 4), ("ownF-", 3), ("rF-", 2), ("rF-", 3), ("rF-", 4), ("fF-", 4), ("ownF+", 2),
+    ("rF+", 2), ("rF+", 3), ("lF+", 2), ("ownF+", 3), ("lF-", 2), ("rF+", 5), ("lF+", 5),
+    ("fF+", 4), ("ownF+", 5), ("rF-", 0), ("ownF-", 5), ("rF-", 5), ("ownF-", 2), ("lF-", 3),
+    ("fF+", 3), ("ownF+", 0), ("fF+", 0), ("ownF-", 0), ("lF-", 5), ("fF-", 0), ("fF-", 3),
+    ("fF-", 2), ("end", 1), ("fF+", 2), ("fF-", 5), ("fF+", 5), ("end", 3), ("end", 0), ("end", 4),
+    ("end", 5), ("end", 2),
 )
 
 
@@ -169,17 +192,17 @@
         for k, ref in enumerate(refs):
             all_of(ref, load_sem.at[number + k])
 
-    def whole(chunk):
-        _, row, first, second, _ = CHUNKS[chunk]
+    def whole(chunk, table=CHUNKS):
+        _, row, first, second, *_ = table[chunk]
         return pl.ds(row, first + second)
 
-    def up_part(part):
+    def up_part(part, columns):
         return [
             (
                 up.at[:, :, pl.ds(32 * part, 32), pl.ds(128 * c, 128)],
                 mine.at[:, :, pl.ds(UP + 128 * part + 32 * c, 32), :],
             )
-            for c in range(4)
+            for c in columns
         ]
 
     def columns(array, row, start, length):
@@ -191,7 +214,7 @@
             for k in range(8)
         ]
 
-    load(0, up_part(0))
+    load(0, up_part(0, (0, 1)))
     load(
         1,
         [
@@ -201,10 +224,14 @@
     )
     load(COUNT, [(norm, raw_norm)])
     load(COUNT + 1, [(bias, raw_bias)])
-    load(3, columns(down, DOWN, 0, 128))
-    load(2, up_part(1))
-    load(4, [(query, mine.at[:, :, pl.ds(QUERY, 64), :]), (key, mine.at[:, :, pl.ds(KEY, 64), :])])
-    load(5, columns(down, DOWN, 128, 128))
+    load(2, up_part(0, (2, 3)))
+    load(3, up_part(1, (0, 1)))
+    load(4, columns(down, DOWN, 0, 64))
+    load(5, up_part(1, (2, 3)))
+    load(6, columns(down, DOWN, 64, 64))
+    load(7, [(query, mine.at[:, :, pl.ds(QUERY, 64), :]), (key, mine.at[:, :, pl.ds(KEY, 64), :])])
+    load(8, columns(down, DOWN, 128, 64))
+    load(9, columns(down, DOWN, 192, 64))
     held = [*zip(given, (*params, *states))]
     load(COUNT + 2, [held[k] for k in (0, 1, 8, 9)])
     load(COUNT + 3, [held[k] for k in (2, 3, 4, 5, 10, 11, 12, 13)])
@@ -236,95 +263,111 @@
             )
 
     def halves(chunk):
-        _, row, first, second, _ = CHUNKS[chunk]
+        _, row, first, second = CHUNKS[chunk]
         return pl.ds(row, first), pl.ds(row + first, second)
+
+    def pair_of(chunk, part):
+        own = position[other[CHUNKS[chunk][0]]] // 2
+        return 2 * own if part else 2 - 2 * own
 
     def share(axis, at, b):
         if axis == "y":
             return mine.at[b, at]
         return mine.at[at, b]
 
-    def copies(chunk, number):
+    def copies(chunk, number, part=0):
         axis = CHUNKS[chunk][0]
         a, b = halves(chunk)
         second = number >= 6
         if second:
             axis = other[axis]
             sources, targets = (send_op2, send_dir2, send_fwd2), (recv_op2, *recv_rest2)
-            a, b = (a, slice(None)), (b, slice(None))
         else:
             sources, targets = (send_op, send_dir, send_fwd), (recv_op, *recv_rest)
-            a, b = (slice(None), a, slice(None)), (slice(None), b, slice(None))
         kind, half = divmod(number % 6, 2)
         rows = b if half else a
+        at = (rows, slice(None))
+        if not second:
+            at = (pl.ds(pair_of(chunk, part), 2), *at)
         step = (SIDE - 1, 1)[half] if kind != 1 else (1, SIDE - 1)[half]
-        arrival = (3 if second else half) if kind == 0 else (4 if second else 2)
+        if second:
+            arrival = 6 if kind == 0 else 7
+        else:
+            arrival = 3 * part + (half if kind == 0 else 2)
         return pltpu.make_async_remote_copy(
-            src_ref=sources[kind].at[rows],
-            dst_ref=targets[kind].at[rows],
+            src_ref=sources[kind].at[at],
+            dst_ref=targets[kind].at[at],
             send_sem=send_sem.at[3 * second + kind],
             recv_sem=recv_sem.at[chunk * PER + arrival],
             device_id=place(axis, step),
             device_id_type=MESH,
         )
 
-    def send(chunk):
-        if chunk == 1:
-            loaded(chunk, mine.at[:, :, pl.ds(MIXED, 128)])
-            loaded(COUNT, raw_norm, raw_bias)
-            pack_small()
-        else:
-            loaded(chunk, mine.at[:, :, whole(chunk)])
+    ready = set()
+
+    def send(chunk, part):
+        if chunk not in ready:
+            ready.add(chunk)
+            if chunk == 1:
+                loaded(chunk, mine.at[:, :, pl.ds(MIXED, 128)])
+                loaded(COUNT, raw_norm, raw_bias)
+                pack_small()
+            else:
+                loaded(chunk, mine.at[:, :, whole(chunk)])
         axis = CHUNKS[chunk][0]
-        p = position[axis]
-        a, b = halves(chunk)
-        far = (p + 2) % SIDE
+        far = (position[axis] + 2) % SIDE
+        pair, rows = pair_of(chunk, part), whole(chunk)
 
         def op(i, _):
-            send_op[i, a, :] = to_wire(share(axis, far, i)[a, :], ONE)
-            send_op[i, b, :] = to_wire(share(axis, far, i)[b, :], ONE)
+            send_op[pair + i, rows, :] = to_wire(share(axis, far, pair + i)[rows, :], ONE)
             return 0
 
-        lax.fori_loop(0, SIDE, op, 0)
+        lax.fori_loop(0, 2, op, 0)
         if waiting:
             waiting.pop()
             pl.semaphore_wait(barrier, 4 + PEERS - 1)
-        copies(chunk, 0).start()
-        copies(chunk, 1).start()
-
-    def send_direct(chunk):
+        copies(chunk, 0, part).start()
+        copies(chunk, 1, part).start()
+
+    def send_direct(chunk, part):
         axis = CHUNKS[chunk][0]
         p = position[axis]
         a, b = halves(chunk)
         right, left = (p + 1) % SIDE, (p + SIDE - 1) % SIDE
+        pair = pair_of(chunk, part)
 
         def direct(i, _):
-            send_dir[i, a, :] = to_wire(share(axis, right, i)[a, :], ONE)
-            send_dir[i, b, :] = to_wire(share(axis, left, i)[b, :], ONE)
+            send_dir[pair + i, a, :] = to_wire(share(axis, right, pair + i)[a, :], ONE)
+            send_dir[pair + i, b, :] = to_wire(share(axis, left, pair + i)[b, :], ONE)
             return 0
 
-        lax.fori_loop(0, SIDE, direct, 0)
-        copies(chunk, 2).start()
-        copies(chunk, 3).start()
-
-    def forward(chunk, number):
+        lax.fori_loop(0, 2, direct, 0)
+        copies(chunk, 2, part).start()
+        copies(chunk, 3, part).start()
+
+    def forward(chunk, part, number):
         axis = CHUNKS[chunk][0]
         rows = halves(chunk)[number]
         at = (position[axis] + (SIDE - 1, 1)[number]) % SIDE
-        copies(chunk, number).wait_recv()
+        pair = pair_of(chunk, part)
+        copies(chunk, number, part).wait_recv()
 
         def body(i, _):
-            part = from_wire(recv_op[i, rows, :], ONE) + share(axis, at, i)[rows, :]
-            send_fwd[i, rows, :] = to_wire(part, TWO)
+            term = from_wire(recv_op[pair + i, rows, :], ONE) + share(axis, at, pair + i)[rows, :]
+            send_fwd[pair + i, rows, :] = to_wire(term, TWO)
             return 0
 
-        lax.fori_loop(0, SIDE, body, 0)
-        copies(chunk, 4 + number).start()
-
-    def finish(chunk):
-        axis, row, first, second, _ = CHUNKS[chunk]
+        lax.fori_loop(0, 2, body, 0)
+        copies(chunk, 4 + number, part).start()
+
+    def finish(chunk, part):
+        axis, row, first, second = CHUNKS[chunk]
+        length = first + second
         p = position[axis]
-        all_of(both.at[:, :, whole(chunk)], recv_sem.at[chunk * PER + 2])
+        pair = pair_of(chunk, part)
+        all_of(
+            both.at[:, pl.ds(pair, 2), whole(chunk)], recv_sem.at[chunk * PER + 3 * part + 2]
+        )
 
         def summed(i, rows):
             return (
@@ -333,47 +376,41 @@
                 + from_wire(recv_fwd[i, rows, :], TWO)
             )
 
-        paired = {"y": 0, "z": first + second}[axis] if chunk != 1 else 64
-
-        def pairs(t, _):
-            for start in range(0, paired, 64):
-                rows = pl.ds(row + start, 64)
-                low = low_lanes((64, 128))
-                upper, lower = summed(2 * t, rows), summed(2 * t + 1, rows)
-                first_sum[2 * t, rows, :] = jnp.where(low, upper, turn(lower))
-                first_sum[2 * t + 1, rows, :] = jnp.where(low, turn(upper), lower)
-            return 0
-
+        paired = 64 if axis == "z" else 0
         if paired:
-            lax.fori_loop(0, SIDE // 2, pairs, 0)
-
-        def plain(i, _):
-            for start, stop in ((paired, max(first, paired)), (max(first, paired), first + second)):
-                if stop > start:
-                    rows = pl.ds(row + start, stop - start)
-                    first_sum[i, rows, :] = summed(i, rows)
-            return 0
-
-        if paired < first + second:
-            lax.fori_loop(0, SIDE, plain, 0)
+            rows = pl.ds(row, 64)
+            low = low_lanes((64, 128))
+            upper, lower = summed(pair, rows), summed(pair + 1, rows)
+            first_sum[pair, rows, :] = jnp.where(low, upper, turn(lower))
+            first_sum[pair + 1, rows, :] = jnp.where(low, turn(upper), lower)
+        if paired < length:
+
+            def plain(i, _):
+                rows = pl.ds(row + paired, length - paired)
+                first_sum[pair + i, rows, :] = summed(pair + i, rows)
+                return 0
+
+            lax.fori_loop(0, 2, plain, 0)
 
         p = position[other[axis]]
         a, b = halves(chunk)
         far, right, left = (p + 2) % SIDE, (p + 1) % SIDE, (p + SIDE - 1) % SIDE
-        send_op2[a, :] = to_wire(first_sum[far, a, :], FOUR)
-        copies(chunk, 6).start()
-        send_op2[b, :] = to_wire(first_sum[far, b, :], FOUR)
-        copies(chunk, 7).start()
-        send_dir2[a, :] = to_wire(first_sum[right, a, :], FOUR)
-        copies(chunk, 8).start()
-        send_dir2[b, :] = to_wire(first_sum[left, b, :], FOUR)
-        copies(chunk, 9).start()
+        if part == 0:
+            rows = whole(chunk)
+            send_op2[rows, :] = to_wire(first_sum[far, rows, :], FOUR)
+            copies(chunk, 6).start()
+            copies(chunk, 7).start()
+        else:
+            send_dir2[a, :] = to_wire(first_sum[right, a, :], FOUR)
+            copies(chunk, 8).start()
+            send_dir2[b, :] = to_wire(first_sum[left, b, :], FOUR)
+            copies(chunk, 9).start()
 
     def second_forward(chunk):
         p = position[other[CHUNKS[chunk][0]]]
         a, b = halves(chunk)
         right, left = (p + 1) % SIDE, (p + SIDE - 1) % SIDE
-        all_of(recv_op2.at[whole(chunk)], recv_sem.at[chunk * PER + 3])
+        all_of(recv_op2.at[whole(chunk)], recv_sem.at[chunk * PER + 6])
         for number, rows, at in ((6, a, left), (7, b, right)):
             part = from_wire(recv_op2[rows, :], FOUR) + first_sum[at, rows, :]
             send_fwd2[rows, :] = to_wire(part, EIGHT)
@@ -381,7 +418,7 @@
 
     def second_finish(chunk):
         p = position[other[CHUNKS[chunk][0]]]
-        all_of(both2.at[:, whole(chunk)], recv_sem.at[chunk * PER + 4])
+        all_of(both2.at[:, whole(chunk)], recv_sem.at[chunk * PER + 7])
         for rows in halves(chunk):
             mean[rows, :] = (
                 first_sum[p, rows, :]
@@ -487,7 +524,7 @@
         updated(rows, mean[rows, :] * ratio, packed_param[rows, :], packed_state[rows, :])
 
     def update(chunk):
-        across, down_rows = ratios[CHUNKS[chunk][4]]
+        across, down_rows = ratios[GATHERS[chunk][4]]
         if chunk in (0, 2):
             row_update(UP + 64 * chunk, 4, down_rows[0:32, 0:1], 0, 16 * chunk, 32)
         if chunk == 1:
@@ -504,7 +541,7 @@
             row_update(QUERY, 1, down_rows[0:64, 0:1], 2, 0, 64)
             row_update(KEY, 1, down_rows[0:64, 1:2], 3, 0, 64)
         if chunk in (3, 5):
-            column_update(CHUNKS[chunk][1], 128, across[0:1])
+            column_update(GATHERS[chunk][1], 128, across[0:1])
 
     def keep():
         def step(number, at, m):
@@ -527,14 +564,14 @@
         step(7, everything, turn(line)[:, :64])
 
     def gather_copies(chunk, number):
-        name, row, first, second, _ = CHUNKS[chunk]
+        name, row, first, second, _ = GATHERS[chunk]
         a, b = pl.ds(row, first), pl.ds(row + first, second)
         up_way = number % 2 == 0
         step = 1 if up_way else SIDE - 1
         behind = SIDE - 1 if up_way else 1
         p, q = position[name], position[other[name]]
         axis = name
-        rows = whole(chunk)
+        rows = whole(chunk, GATHERS)
         if number < 4:
             axis = other[name]
             if number >= 2:
@@ -595,21 +632,22 @@
             small_halves[k][...] = lines[k].astype(jnp.bfloat16)
 
     def end(chunk):
-        all_of(gathered.at[0, :, whole(chunk)], grecv_sem.at[chunk * PER_GATHER + 11])
+        all_of(gathered.at[0, :, whole(chunk, GATHERS)], grecv_sem.at[chunk * PER_GATHER + 11])
         if chunk in (1, 3, 5):
             widen(chunk)
         if chunk == 1:
             small_out()
 
     def act(name, k):
-        if name == "so":
-            send(k)
-        elif name == "sd":
-            send_direct(k)
-        elif name in ("fwdA", "fwdB"):
-            forward(k, int(name == "fwdB"))
-        elif name == "fin":
-            finish(k)
+        part = int(name.endswith("O"))
+        if name in ("soF", "soO"):
+            send(k, part)
+        elif name in ("sdF", "sdO"):
+            send_direct(k, part)
+        elif name[:4] in ("fwdA", "fwdB"):
+            forward(k, part, int(name[3] == "B"))
+        elif name in ("finF", "finO"):
+            finish(k, part)
         elif name == "Fwd":
             second_forward(k)
         elif name == "Fin":
@@ -630,7 +668,7 @@
         elif name == "xf-":
             pass_on(k, (1,), (3, 8, 9))
         elif name == "far":
-            all_of(gathered.at[0, 0, whole(k)], grecv_sem.at[k * PER_GATHER + 2])
+            all_of(gathered.at[0, 0, whole(k, GATHERS)], grecv_sem.at[k * PER_GATHER + 2])
             pass_on(k, (), (10, 11))
         elif name == "end":
             end(k)
@@ -726,7 +764,7 @@
             dma((LOADS,)),
             dma((SENDS,)),
             dma((COUNT * PER,)),
-            dma((COUNT * PER_GATHER,)),
+            dma((len(GATHERS) * PER_GATHER,)),
             dma((GROUPS,)),
         ],
         compiler_params=pltpu.CompilerParams(

time: 58.1 us -> 56.7 us (0.976)
  Pallas kernels: 57.2 us -> 55.9 us
    pallas_call x1, Pallas kernels: 55 us -> 53.7 us  [local(): pl.pallas_call(exchange_kernel, out_shape=(pltpu.VMEM((SIDE, SIDE, ROWS,...]
where the time goes in v5:
time: 56.7 us; the launch traced here: 56.6 us
  Pallas kernels  55.9 us (99%)
  between operations  0.68 us (1%)
    pallas_call x1, Pallas kernels, local(): pl.pallas_call(exchange_kernel, out_shape=(pltpu.VMEM((SIDE, SIDE, ROWS,...  53.7 us
    pallas_call x1, Pallas kernels, local(): pl.pallas_call(output_kernel, out_shape=(*full, *own, *own), in_specs=[vm...  2.26 us

profile of v5, /device:TPU:0, one launch (start us, length us, event | category | flops | bytes accessed | tf_op | source)
XLA Modules:
  0.0 56.6 jit_solution(5412710183814183481)
XLA Ops:
  0.7 53.7 %exchange.1 = (bf16[4,4,784,128]{3,2,1,0:T(8,128)(2,1)S(1)}, bf16[512,1024]{1,0:T(8,128)(2,1)S(1)}, bf16[128,1024]{1,0:T(8,128)(2,1)S(1)}, bf16[8,128]{1,0:T(8,1...) custom-call(f32[4,4,64,512]{3,2,1,0:T(8,128)} %bitcast.30, ...), custom_call_target="tpu_custom_call" | custom-call | tf_op jit(solution)/shard_map/exchange/pallas_call | solution.py:735
  54.3 2.3 %outputs.1 = (bf16[16,64,512]{2,1,0:T(8,128)(2,1)}, bf16[512,1024]{1,0:T(8,128)(2,1)}, bf16[16,64,128]{2,1,0:T(8,128)(2,1)}, bf16[16,64,128]{2,1,0:T(8,128)(2,1)...) custom-call(bf16[16,784,128]{2,1,0:T(8,128)(2,1)S(1)} %bitcast.29, ...), custom_call_target="tpu_custom_call" | custom-call | tf_op jit(solution)/shard_map/outputs/pallas_call | solution.py:802

commit v6 on v5

--- a/solution.py
+++ b/solution.py
@@ -38,42 +38,34 @@
 )
 COUNT = len(CHUNKS)
 GROUPS = 5
-PER = 8
-PER_GATHER = 12
+PER = 6
+PER_GATHER = 7
 LOADS = COUNT + 8
 SENDS = 9
 
 ORDER = (
-    ("soF", 0), ("sdF", 0), ("soF", 1), ("sdF", 1), ("soO", 2), ("soF", 4), ("soF", 7), ("sdF", 7),
-    ("soF", 3), ("soO", 1), ("sdO", 1), ("soO", 7), ("soF", 2), ("sdF", 2), ("fwdBF", 1),
-    ("fwdAF", 1), ("soF", 5), ("fwdBF", 7), ("soF", 8), ("sdF", 4), ("fwdAF", 7), ("soF", 9),
-    ("sdO", 7), ("soF", 6), ("fwdBO", 2), ("soO", 8), ("soO", 0), ("fwdAO", 1), ("fwdAF", 3),
-    ("fwdBO", 1), ("soO", 9), ("fwdBF", 0), ("fwdAF", 0), ("finF", 1), ("fwdAO", 7), ("sdF", 9),
-    ("fwdBF", 4), ("fwdAF", 8), ("fwdBO", 7), ("finF", 7), ("soO", 4), ("fwdBF", 2), ("fwdAF", 2),
-    ("fwdBF", 9), ("prepare", 0), ("soO", 3), ("fwdAF", 4), ("soO", 6), ("sdF", 8), ("soO", 5),
-    ("fwdBF", 6), ("fwdAF", 9), ("sdF", 6), ("fwdAO", 2), ("fwdBF", 3), ("finO", 1), ("Fwd", 1),
-    ("sdF", 3), ("fwdBF", 8), ("sdF", 5), ("fwdAF", 6), ("fwdBF", 5), ("finO", 7), ("fwdAF", 5),
-    ("fwdAO", 0), ("sdO", 0), ("sdO", 2), ("fwdBO", 0), ("Fwd", 7), ("fwdBO", 8), ("sdO", 9),
-    ("fwdBO", 5), ("finF", 0), ("finF", 2), ("fwdAO", 3), ("fwdBO", 4), ("fwdBO", 9), ("fwdAO", 4),
-    ("fwdBO", 3), ("fwdAO", 9), ("fwdAO", 6), ("fwdBO", 6), ("sdO", 6), ("finF", 4), ("sdO", 4),
-    ("sdO", 8), ("Fin", 1), ("norm", 1), ("finF", 6), ("finF", 9), ("fwdAO", 8), ("finF", 8),
-    ("Fin", 7), ("sdO", 3), ("norm", 3), ("fwdAO", 5), ("finF", 3), ("finF", 5), ("sdO", 5),
-    ("finO", 2), ("Fwd", 2), ("finO", 0), ("Fwd", 0), ("finO", 9), ("Fwd", 9), ("finO", 6),
-    ("Fwd", 6), ("finO", 4), ("Fwd", 4), ("finO", 3), ("finO", 8), ("Fwd", 8), ("finO", 5),
-    ("Fwd", 5), ("Fwd", 3), ("ratio", 1), ("upd", 1), ("Fin", 0), ("Fin", 2), ("norm", 0),
-    ("Fin", 9), ("ratio", 3), ("upd", 4), ("Fin", 4), ("Fin", 6), ("Fin", 8), ("norm", 4),
-    ("Fin", 3), ("Fin", 5), ("norm", 2), ("ownF+", 1), ("xf-", 1), ("xf+", 1), ("ownF+", 4),
-    ("ownF-", 4), ("xf+", 4), ("ownF-", 1), ("xf-", 4), ("ratio", 0), ("upd", 0), ("far", 1),
-    ("ratio", 4), ("upd", 3), ("ratio", 2), ("upd", 2), ("lF-", 1), ("upd", 5), ("keep", 0),
-    ("xf+", 0), ("xf-", 0), ("rF+", 1), ("xf+", 3), ("xf-", 3), ("xf+", 2), ("xf-", 2), ("xf-", 5),
-    ("xf+", 5), ("lF+", 0), ("far", 4), ("lF-", 4), ("far", 0), ("far", 3), ("lF+", 1), ("rF+", 0),
-    ("rF-", 1), ("far", 2), ("lF-", 0), ("lF+", 4), ("fF-", 1), ("fF+", 1), ("far", 5), ("lF+", 3),
-    ("rF+", 4), ("ownF-", 3), ("rF-", 2), ("rF-", 3), ("rF-", 4), ("fF-", 4), ("ownF+", 2),
-    ("rF+", 2), ("rF+", 3), ("lF+", 2), ("ownF+", 3), ("lF-", 2), ("rF+", 5), ("lF+", 5),
-    ("fF+", 4), ("ownF+", 5), ("rF-", 0), ("ownF-", 5), ("rF-", 5), ("ownF-", 2), ("lF-", 3),
-    ("fF+", 3), ("ownF+", 0), ("fF+", 0), ("ownF-", 0), ("lF-", 5), ("fF-", 0), ("fF-", 3),
-    ("fF-", 2), ("end", 1), ("fF+", 2), ("fF-", 5), ("fF+", 5), ("end", 3), ("end", 0), ("end", 4),
-    ("end", 5), ("end", 2),
+    ("soF", 0), ("soF", 1), ("soO", 0), ("sdF", 0), ("sdF", 1), ("soF", 4), ("soF", 2), ("soF", 7),
+    ("sdF", 7), ("soO", 1), ("soO", 3), ("soO", 5), ("sdO", 1), ("soF", 3), ("fwdF", 1),
+    ("soF", 9), ("soF", 8), ("soO", 7), ("sdF", 4), ("fwdF", 0), ("soO", 6), ("fwdF", 7),
+    ("fwdO", 1), ("fwdF", 2), ("soF", 6), ("soF", 5), ("sdO", 7), ("sdF", 8), ("fwdF", 4),
+    ("finF", 1), ("fwdO", 7), ("fwdF", 8), ("soO", 2), ("sdO", 2), ("soO", 8), ("finF", 7),
+    ("soO", 4), ("sdF", 2), ("fwdF", 9), ("sdF", 9), ("prepare", 0), ("finF", 0), ("sdF", 5),
+    ("finO", 1), ("Fwd", 1), ("sdO", 8), ("fwdF", 6), ("sdO", 0), ("fwdF", 5), ("finF", 8),
+    ("soO", 9), ("sdF", 3), ("finO", 7), ("Fwd", 7), ("fwdO", 2), ("sdF", 6), ("fwdO", 0),
+    ("fwdO", 8), ("fwdO", 4), ("fwdF", 3), ("sdO", 3), ("finF", 2), ("sdO", 9), ("fwdO", 3),
+    ("sdO", 4), ("Fin", 1), ("norm", 1), ("fwdO", 9), ("finF", 9), ("sdO", 6), ("fwdO", 6),
+    ("finF", 4), ("Fin", 7), ("norm", 3), ("finF", 5), ("finF", 6), ("finO", 0), ("Fwd", 0),
+    ("sdO", 5), ("fwdO", 5), ("finF", 3), ("finO", 2), ("Fwd", 2), ("finO", 8), ("Fwd", 8),
+    ("finO", 4), ("Fwd", 4), ("finO", 9), ("Fwd", 9), ("finO", 6), ("Fwd", 6), ("finO", 3),
+    ("Fin", 0), ("finO", 5), ("Fwd", 5), ("Fwd", 3), ("Fin", 8), ("Fin", 2), ("norm", 0),
+    ("ratio", 1), ("upd", 1), ("Fin", 9), ("Fin", 4), ("Fin", 6), ("norm", 4), ("ratio", 3),
+    ("upd", 4), ("Fin", 5), ("Fin", 3), ("norm", 2), ("xf", 1), ("ownF", 1), ("ownF", 4),
+    ("xf", 4), ("ratio", 0), ("upd", 0), ("far", 1), ("ratio", 4), ("upd", 3), ("upd", 5),
+    ("ratio", 2), ("upd", 2), ("keep", 0), ("lF", 1), ("xf", 0), ("xf", 3), ("xf", 5), ("ownF", 0),
+    ("xf", 2), ("rF", 4), ("far", 0), ("lF", 3), ("far", 4), ("far", 5), ("rF", 0), ("far", 3),
+    ("lF", 4), ("rF", 1), ("rF", 5), ("ownF", 5), ("far", 2), ("rF", 3), ("lF", 2), ("lF", 0),
+    ("lF", 5), ("fF", 5), ("fF", 0), ("ownF", 2), ("ownF", 3), ("fF", 4), ("fF", 3), ("rF", 2),
+    ("fF", 1), ("fF", 2), ("end", 5), ("end", 0), ("end", 3), ("end", 4), ("end", 1), ("end", 2),
 )
 
 
@@ -224,20 +216,6 @@
     )
     load(COUNT, [(norm, raw_norm)])
     load(COUNT + 1, [(bias, raw_bias)])
-    load(2, up_part(0, (2, 3)))
-    load(3, up_part(1, (0, 1)))
-    load(4, columns(down, DOWN, 0, 64))
-    load(5, up_part(1, (2, 3)))
-    load(6, columns(down, DOWN, 64, 64))
-    load(7, [(query, mine.at[:, :, pl.ds(QUERY, 64), :]), (key, mine.at[:, :, pl.ds(KEY, 64), :])])
-    load(8, columns(down, DOWN, 128, 64))
-    load(9, columns(down, DOWN, 192, 64))
-    held = [*zip(given, (*params, *states))]
-    load(COUNT + 2, [held[k] for k in (0, 1, 8, 9)])
-    load(COUNT + 3, [held[k] for k in (2, 3, 4, 5, 10, 11, 12, 13)])
-    for k, pair in enumerate((held[6], held[7], held[14], held[15])):
-        load(COUNT + 4 + k, [pair])
-
     barrier = pltpu.get_barrier_semaphore()
     for axis in ("y", "z"):
         for step in (1, SIDE - 1):
@@ -247,6 +225,21 @@
             barrier, 1, device_id=(replica, (model + step) % PEERS), device_id_type=MESH
         )
     waiting = [True]
+
+    def load_rest():
+        load(2, up_part(0, (2, 3)))
+        load(3, up_part(1, (0, 1)))
+        load(4, columns(down, DOWN, 0, 64))
+        load(5, up_part(1, (2, 3)))
+        load(6, columns(down, DOWN, 64, 64))
+        load(7, [(query, mine.at[:, :, pl.ds(QUERY, 64), :]), (key, mine.at[:, :, pl.ds(KEY, 64), :])])
+        load(8, columns(down, DOWN, 128, 64))
+        load(9, columns(down, DOWN, 192, 64))
+        held = [*zip(given, (*params, *states))]
+        load(COUNT + 2, [held[k] for k in (0, 1, 8, 9)])
+        load(COUNT + 3, [held[k] for k in (2, 3, 4, 5, 10, 11, 12, 13)])
+        for k, pair in enumerate((held[6], held[7], held[14], held[15])):
+            load(COUNT + 4 + k, [pair])
 
     def pack_small():
         low = low_lanes((1, 128))
@@ -291,9 +284,9 @@
             at = (pl.ds(pair_of(chunk, part), 2), *at)
         step = (SIDE - 1, 1)[half] if kind != 1 else (1, SIDE - 1)[half]
         if second:
-            arrival = 6 if kind == 0 else 7
+            arrival = 4 if kind == 0 else 5
         else:
-            arrival = 3 * part + (half if kind == 0 else 2)
+            arrival = 2 * part + (kind > 0)
         return pltpu.make_async_remote_copy(
             src_ref=sources[kind].at[at],
             dst_ref=targets[kind].at[at],
@@ -325,6 +318,7 @@
         lax.fori_loop(0, 2, op, 0)
         if waiting:
             waiting.pop()
+            load_rest()
             pl.semaphore_wait(barrier, 4 + PEERS - 1)
         copies(chunk, 0, part).start()
         copies(chunk, 1, part).start()
@@ -345,20 +339,22 @@
         copies(chunk, 2, part).start()
         copies(chunk, 3, part).start()
 
-    def forward(chunk, part, number):
+    def forward(chunk, part):
         axis = CHUNKS[chunk][0]
-        rows = halves(chunk)[number]
-        at = (position[axis] + (SIDE - 1, 1)[number]) % SIDE
+        a, b = halves(chunk)
+        right, left = (position[axis] + 1) % SIDE, (position[axis] + SIDE - 1) % SIDE
         pair = pair_of(chunk, part)
-        copies(chunk, number, part).wait_recv()
-
-        def body(i, _):
-            term = from_wire(recv_op[pair + i, rows, :], ONE) + share(axis, at, pair + i)[rows, :]
-            send_fwd[pair + i, rows, :] = to_wire(term, TWO)
-            return 0
-
-        lax.fori_loop(0, 2, body, 0)
-        copies(chunk, 4 + number, part).start()
+        all_of(recv_op.at[pl.ds(pair, 2), whole(chunk)], recv_sem.at[chunk * PER + 2 * part])
+        for number, rows, at in ((4, a, left), (5, b, right)):
+
+            def body(i, _):
+                own = share(axis, at, pair + i)[rows, :]
+                term = from_wire(recv_op[pair + i, rows, :], ONE) + own
+                send_fwd[pair + i, rows, :] = to_wire(term, TWO)
+                return 0
+
+            lax.fori_loop(0, 2, body, 0)
+            copies(chunk, number, part).start()
 
     def finish(chunk, part):
         axis, row, first, second = CHUNKS[chunk]
@@ -366,7 +362,7 @@
         p = position[axis]
         pair = pair_of(chunk, part)
         all_of(
-            both.at[:, pl.ds(pair, 2), whole(chunk)], recv_sem.at[chunk * PER + 3 * part + 2]
+            both.at[:, pl.ds(pair, 2), whole(chunk)], recv_sem.at[chunk * PER + 2 * part + 1]
         )
 
         def summed(i, rows):
@@ -410,7 +406,7 @@
         p = position[other[CHUNKS[chunk][0]]]
         a, b = halves(chunk)
         right, left = (p + 1) % SIDE, (p + SIDE - 1) % SIDE
-        all_of(recv_op2.at[whole(chunk)], recv_sem.at[chunk * PER + 6])
+        all_of(recv_op2.at[whole(chunk)], recv_sem.at[chunk * PER + 4])
         for number, rows, at in ((6, a, left), (7, b, right)):
             part = from_wire(recv_op2[rows, :], FOUR) + first_sum[at, rows, :]
             send_fwd2[rows, :] = to_wire(part, EIGHT)
@@ -418,7 +414,7 @@
 
     def second_finish(chunk):
         p = position[other[CHUNKS[chunk][0]]]
-        all_of(both2.at[:, whole(chunk)], recv_sem.at[chunk * PER + 7])
+        all_of(both2.at[:, whole(chunk)], recv_sem.at[chunk * PER + 5])
         for rows in halves(chunk):
             mean[rows, :] = (
                 first_sum[p, rows, :]
@@ -582,7 +578,7 @@
             if number >= 12:
                 rows, p = (b if up_way else a), (p + behind) % SIDE
         ref = gathered.at[q, p, rows] if name == "y" else gathered.at[p, q, rows]
-        arrival = min(number, 2) if number < 4 else min(number - 1, 11)
+        arrival = min(number // 2, 6)
         return pltpu.make_async_remote_copy(
             src_ref=ref,
             dst_ref=ref,
@@ -592,9 +588,15 @@
             device_id_type=MESH,
         )
 
-    def pass_on(chunk, awaited, started):
-        for number in awaited:
-            gather_copies(chunk, number).wait_recv()
+    def pass_on(chunk, arrival, started):
+        rows = whole(chunk, GATHERS)
+        if arrival is not None:
+            ref = gathered.at[0, 0:2, rows]
+            if arrival == 1:
+                ref = gathered.at[0, 0, rows]
+            if arrival == 6:
+                ref = gathered.at[0, :, rows]
+            all_of(ref, grecv_sem.at[chunk * PER_GATHER + arrival])
         for number in started:
             gather_copies(chunk, number).start()
 
@@ -632,7 +634,7 @@
             small_halves[k][...] = lines[k].astype(jnp.bfloat16)
 
     def end(chunk):
-        all_of(gathered.at[0, :, whole(chunk, GATHERS)], grecv_sem.at[chunk * PER_GATHER + 11])
+        pass_on(chunk, 6, ())
         if chunk in (1, 3, 5):
             widen(chunk)
         if chunk == 1:
@@ -644,8 +646,8 @@
             send(k, part)
         elif name in ("sdF", "sdO"):
             send_direct(k, part)
-        elif name[:4] in ("fwdA", "fwdB"):
-            forward(k, part, int(name[3] == "B"))
+        elif name in ("fwdF", "fwdO"):
+            forward(k, part)
         elif name in ("finF", "finO"):
             finish(k, part)
         elif name == "Fwd":
@@ -662,19 +664,16 @@
             norm_ratios(k)
         elif name == "upd":
             update(k)
-            pass_on(k, (), (0, 1, 4, 5))
-        elif name == "xf+":
-            pass_on(k, (0,), (2, 6, 7))
-        elif name == "xf-":
-            pass_on(k, (1,), (3, 8, 9))
+            pass_on(k, None, (0, 1, 4, 5))
+        elif name == "xf":
+            pass_on(k, 0, (2, 3, 6, 7, 8, 9))
         elif name == "far":
-            all_of(gathered.at[0, 0, whole(k, GATHERS)], grecv_sem.at[k * PER_GATHER + 2])
-            pass_on(k, (), (10, 11))
+            pass_on(k, 1, (10, 11))
         elif name == "end":
             end(k)
         else:
-            number = 4 + 2 * ("own", "l", "r", "f").index(name[:-2]) + int(name[-1] == "-")
-            pass_on(k, (number,), (number + 8,))
+            block = ("own", "l", "r", "f").index(name[:-1])
+            pass_on(k, 2 + block, (12 + 2 * block, 13 + 2 * block))
 
     for name, k in ORDER:
         with stage(f"{name}_{k}"):

time: 56.7 us -> 57.8 us (1.019)
  Pallas kernels: 55.9 us -> 57 us
    pallas_call x1, Pallas kernels: 53.7 us -> 54.7 us  [local(): pl.pallas_call(exchange_kernel, out_shape=(pltpu.VMEM((SIDE, SIDE, ROWS,...]
where the time goes in v6:
time: 57.8 us; the launch traced here: 57.7 us
  Pallas kernels  57 us (99%)
  between operations  0.68 us (1%)
    pallas_call x1, Pallas kernels, local(): pl.pallas_call(exchange_kernel, out_shape=(pltpu.VMEM((SIDE, SIDE, ROWS,...  54.7 us
    pallas_call x1, Pallas kernels, local(): pl.pallas_call(output_kernel, out_shape=(*full, *own, *own), in_specs=[vm...  2.26 us

profile of v6, /device:TPU:0, one launch (start us, length us, event | category | flops | bytes accessed | tf_op | source)
XLA Modules:
  0.0 57.7 jit_solution(10004254880345127201)
XLA Ops:
  0.7 54.7 %exchange.1 = (bf16[4,4,784,128]{3,2,1,0:T(8,128)(2,1)S(1)}, bf16[512,1024]{1,0:T(8,128)(2,1)S(1)}, bf16[128,1024]{1,0:T(8,128)(2,1)S(1)}, bf16[8,128]{1,0:T(8,1...) custom-call(f32[4,4,64,512]{3,2,1,0:T(8,128)} %bitcast.30, ...), custom_call_target="tpu_custom_call" | custom-call | tf_op jit(solution)/shard_map/exchange/pallas_call | solution.py:734
  55.4 2.3 %outputs.1 = (bf16[16,64,512]{2,1,0:T(8,128)(2,1)}, bf16[512,1024]{1,0:T(8,128)(2,1)}, bf16[16,64,128]{2,1,0:T(8,128)(2,1)}, bf16[16,64,128]{2,1,0:T(8,128)(2,1)...) custom-call(bf16[16,784,128]{2,1,0:T(8,128)(2,1)S(1)} %bitcast.29, ...), custom_call_target="tpu_custom_call" | custom-call | tf_op jit(solution)/shard_map/outputs/pallas_call | solution.py:801

commit v7 on v6

--- a/solution.py
+++ b/solution.py
@@ -44,28 +44,28 @@
 SENDS = 9
 
 ORDER = (
-    ("soF", 0), ("soF", 1), ("soO", 0), ("sdF", 0), ("sdF", 1), ("soF", 4), ("soF", 2), ("soF", 7),
-    ("sdF", 7), ("soO", 1), ("soO", 3), ("soO", 5), ("sdO", 1), ("soF", 3), ("fwdF", 1),
-    ("soF", 9), ("soF", 8), ("soO", 7), ("sdF", 4), ("fwdF", 0), ("soO", 6), ("fwdF", 7),
-    ("fwdO", 1), ("fwdF", 2), ("soF", 6), ("soF", 5), ("sdO", 7), ("sdF", 8), ("fwdF", 4),
-    ("finF", 1), ("fwdO", 7), ("fwdF", 8), ("soO", 2), ("sdO", 2), ("soO", 8), ("finF", 7),
-    ("soO", 4), ("sdF", 2), ("fwdF", 9), ("sdF", 9), ("prepare", 0), ("finF", 0), ("sdF", 5),
-    ("finO", 1), ("Fwd", 1), ("sdO", 8), ("fwdF", 6), ("sdO", 0), ("fwdF", 5), ("finF", 8),
-    ("soO", 9), ("sdF", 3), ("finO", 7), ("Fwd", 7), ("fwdO", 2), ("sdF", 6), ("fwdO", 0),
-    ("fwdO", 8), ("fwdO", 4), ("fwdF", 3), ("sdO", 3), ("finF", 2), ("sdO", 9), ("fwdO", 3),
-    ("sdO", 4), ("Fin", 1), ("norm", 1), ("fwdO", 9), ("finF", 9), ("sdO", 6), ("fwdO", 6),
-    ("finF", 4), ("Fin", 7), ("norm", 3), ("finF", 5), ("finF", 6), ("finO", 0), ("Fwd", 0),
-    ("sdO", 5), ("fwdO", 5), ("finF", 3), ("finO", 2), ("Fwd", 2), ("finO", 8), ("Fwd", 8),
-    ("finO", 4), ("Fwd", 4), ("finO", 9), ("Fwd", 9), ("finO", 6), ("Fwd", 6), ("finO", 3),
-    ("Fin", 0), ("finO", 5), ("Fwd", 5), ("Fwd", 3), ("Fin", 8), ("Fin", 2), ("norm", 0),
-    ("ratio", 1), ("upd", 1), ("Fin", 9), ("Fin", 4), ("Fin", 6), ("norm", 4), ("ratio", 3),
-    ("upd", 4), ("Fin", 5), ("Fin", 3), ("norm", 2), ("xf", 1), ("ownF", 1), ("ownF", 4),
-    ("xf", 4), ("ratio", 0), ("upd", 0), ("far", 1), ("ratio", 4), ("upd", 3), ("upd", 5),
-    ("ratio", 2), ("upd", 2), ("keep", 0), ("lF", 1), ("xf", 0), ("xf", 3), ("xf", 5), ("ownF", 0),
-    ("xf", 2), ("rF", 4), ("far", 0), ("lF", 3), ("far", 4), ("far", 5), ("rF", 0), ("far", 3),
-    ("lF", 4), ("rF", 1), ("rF", 5), ("ownF", 5), ("far", 2), ("rF", 3), ("lF", 2), ("lF", 0),
-    ("lF", 5), ("fF", 5), ("fF", 0), ("ownF", 2), ("ownF", 3), ("fF", 4), ("fF", 3), ("rF", 2),
-    ("fF", 1), ("fF", 2), ("end", 5), ("end", 0), ("end", 3), ("end", 4), ("end", 1), ("end", 2),
+    ("soO", 0), ("soF", 0), ("soF", 1), ("soF", 2), ("soF", 6), ("soF", 3), ("sdF", 2), ("soO", 1),
+    ("sdO", 1), ("sdF", 1), ("soO", 2), ("sdO", 2), ("soF", 7), ("soO", 5), ("soO", 3), ("sdF", 0),
+    ("fwdF", 1), ("soF", 5), ("soF", 4), ("fwdF", 2), ("soO", 6), ("fwdF", 0), ("fwdO", 0),
+    ("soO", 7), ("fwdO", 2), ("sdF", 5), ("soO", 4), ("fwdO", 1), ("soO", 9), ("soF", 8),
+    ("sdF", 6), ("finF", 1), ("sdO", 0), ("fwdF", 6), ("sdF", 7), ("finF", 2), ("sdF", 3),
+    ("fwdF", 3), ("finF", 0), ("fwdF", 5), ("soF", 9), ("sdF", 9), ("soO", 8), ("fwdF", 4),
+    ("finO", 2), ("sdO", 9), ("finO", 1), ("Fwd", 1), ("sdF", 8), ("fwdF", 7), ("fwdF", 8),
+    ("Fwd", 2), ("finO", 0), ("Fwd", 0), ("prepare", 0), ("sdO", 5), ("fwdO", 3), ("sdO", 3),
+    ("sdF", 4), ("fwdF", 9), ("fwdO", 9), ("finF", 3), ("fwdO", 5), ("fwdO", 6), ("sdO", 7),
+    ("finF", 5), ("sdO", 6), ("fwdO", 7), ("fwdO", 4), ("Fin", 1), ("norm", 1), ("finF", 6),
+    ("finF", 7), ("sdO", 4), ("sdO", 8), ("Fin", 0), ("Fin", 2), ("norm", 0), ("finF", 4),
+    ("finF", 9), ("fwdO", 8), ("finF", 8), ("finO", 3), ("Fwd", 3), ("finO", 5), ("Fwd", 5),
+    ("finO", 6), ("finO", 9), ("finO", 7), ("Fwd", 7), ("Fwd", 6), ("finO", 4), ("Fwd", 4),
+    ("Fwd", 9), ("finO", 8), ("Fwd", 8), ("ratio", 1), ("upd", 1), ("Fin", 3), ("Fin", 5),
+    ("norm", 2), ("ratio", 0), ("upd", 0), ("Fin", 7), ("norm", 3), ("Fin", 6), ("Fin", 4),
+    ("Fin", 9), ("Fin", 8), ("norm", 4), ("ownF", 1), ("xf", 1), ("xf", 0), ("ratio", 2),
+    ("upd", 2), ("ownF", 0), ("far", 1), ("ratio", 3), ("upd", 4), ("lF", 1), ("ratio", 4),
+    ("upd", 5), ("rF", 1), ("upd", 3), ("xf", 2), ("xf", 4), ("xf", 5), ("lF", 0), ("xf", 3),
+    ("far", 2), ("far", 4), ("far", 0), ("rF", 0), ("ownF", 5), ("rF", 2), ("lF", 5), ("lF", 2),
+    ("rF", 4), ("far", 5), ("keep", 0), ("far", 3), ("lF", 3), ("ownF", 2), ("fF", 1), ("fF", 2),
+    ("rF", 3), ("fF", 4), ("rF", 5), ("fF", 0), ("fF", 5), ("ownF", 3), ("ownF", 4), ("lF", 4),
+    ("fF", 3), ("end", 2), ("end", 5), ("end", 0), ("end", 1), ("end", 3), ("end", 4),
 )
 
 
@@ -690,25 +690,33 @@
 def output_kernel(*refs):
     gathered, laid, refs = refs[0], refs[1:21], refs[21:]
     half, rest, sem = refs[:8], refs[8:24], refs[24]
-    pairs = []
-    for part in range(2):
-        for c in range(4):
-            pairs.append(
-                (
-                    gathered.at[:, pl.ds(UP + 128 * part + 32 * c, 32), :],
-                    half[0].at[:, pl.ds(32 * part, 32), pl.ds(128 * c, 128)],
-                )
-            )
-    pairs.append((laid[0], half[1]))
-    for number, row in ((2, QUERY), (3, KEY), (4, VALUE)):
-        pairs.append((gathered.at[:, pl.ds(row, 64), :], half[number]))
-    pairs += zip(laid[1:4], half[5:])
-    pairs += zip(laid[4:], rest)
-    started = [pltpu.make_async_copy(*pair, sem.at[k]) for k, pair in enumerate(pairs)]
-    for copy in started:
-        copy.start()
-    for copy in started:
-        copy.wait()
+    up = [
+        (
+            gathered.at[:, pl.ds(UP + 128 * part + 32 * c, 32), :],
+            half[0].at[:, pl.ds(32 * part, 32), pl.ds(128 * c, 128)],
+        )
+        for part in range(2)
+        for c in range(4)
+    ]
+    square = [
+        (gathered.at[:, pl.ds(row, 64), :], half[number])
+        for number, row in ((2, QUERY), (3, KEY), (4, VALUE))
+    ]
+    kept = [*zip(laid[4:], rest)]
+    groups = [
+        (up, gathered.at[:, pl.ds(UP, 256)]),
+        ([(laid[0], half[1])], laid[0]),
+        (square, gathered.at[:, pl.ds(0, 192)]),
+        ([kept[k] for k in (0, 1, 8, 9)], gathered.at[0:4, 0:512]),
+        ([kept[k] for k in (2, 3, 4, 5, 10, 11, 12, 13)], gathered.at[0:2, 0:512]),
+        *[([pair], pair[0]) for pair in zip(laid[1:4], half[5:])],
+        *[([kept[k]], kept[k][0]) for k in (6, 7, 14, 15)],
+    ]
+    for k, (pairs, _) in enumerate(groups):
+        for src, dst in pairs:
+            pltpu.make_async_copy(src, dst, sem.at[k]).start()
+    for k, (_, ref) in enumerate(groups):
+        pltpu.make_async_copy(ref, ref, sem.at[k]).wait()
 
 
 def stay(*arrays):
@@ -803,7 +811,7 @@
         out_shape=(*full, *own, *own),
         in_specs=[vmem] * 21,
         out_specs=(anywhere,) * 24,
-        scratch_shapes=[dma((8 + 1 + 3 + 3 + 16,))],
+        scratch_shapes=[dma((5 + 3 + 4,))],
         compiler_params=pltpu.CompilerParams(vmem_limit_bytes=8 * 2**20),
         name="outputs",
     )(gathered.reshape(SIDE * SIDE, ROWS, 128), *laid)

time: 57.8 us -> 56.5 us (0.978)
  Pallas kernels: 57 us -> 55.7 us
    pallas_call x1, Pallas kernels: 54.7 us -> 53.6 us  [local(): pl.pallas_call(exchange_kernel, out_shape=(pltpu.VMEM((SIDE, SIDE, ROWS,...]
where the time goes in v7:
time: 56.5 us; the launch traced here: 56.4 us
  Pallas kernels  55.7 us (99%)
  between operations  0.68 us (1%)
    pallas_call x1, Pallas kernels, local(): pl.pallas_call(exchange_kernel, out_shape=(pltpu.VMEM((SIDE, SIDE, ROWS,...  53.6 us
    pallas_call x1, Pallas kernels, local(): pl.pallas_call(output_kernel, out_shape=(*full, *own, *own), in_specs=[vm...  2.1 us

profile of v7, /device:TPU:0, one launch (start us, length us, event | category | flops | bytes accessed | tf_op | source)
XLA Modules:
  0.0 56.4 jit_solution(17051580326335122394)
XLA Ops:
  0.7 53.6 %exchange.1 = (bf16[4,4,784,128]{3,2,1,0:T(8,128)(2,1)S(1)}, bf16[512,1024]{1,0:T(8,128)(2,1)S(1)}, bf16[128,1024]{1,0:T(8,128)(2,1)S(1)}, bf16[8,128]{1,0:T(8,1...) custom-call(f32[4,4,64,512]{3,2,1,0:T(8,128)} %bitcast.30, ...), custom_call_target="tpu_custom_call" | custom-call | tf_op jit(solution)/shard_map/exchange/pallas_call | solution.py:742
  54.3 2.1 %outputs.1 = (bf16[16,64,512]{2,1,0:T(8,128)(2,1)}, bf16[512,1024]{1,0:T(8,128)(2,1)}, bf16[16,64,128]{2,1,0:T(8,128)(2,1)}, bf16[16,64,128]{2,1,0:T(8,128)(2,1)...) custom-call(bf16[16,784,128]{2,1,0:T(8,128)(2,1)S(1)} %bitcast.29, ...), custom_call_target="tpu_custom_call" | custom-call | tf_op jit(solution)/shard_map/outputs/pallas_call | solution.py:809
